TPU v7x, 32 devices: a whole 2x2x4 slice. The times are simulated.
32 devices in a mesh: groups: 2 (over y), tensor: 4 (over z), dp: 2 (over x), seq: 2 (over core).
Axes of the slice: x: 2, y: 2, z: 4, core: 2. Of those that a mesh axis runs over, the one named last changes fastest.
Arguments:
- attn_heads: bfloat16 [256, 8192], P(('groups', 'dp', 'seq'), 'tensor'), parts along dimension 0, may hold values from -6 to 6
- out_weight: bfloat16 [8192, 8192], P(('tensor', 'seq')), may hold values from -0.09375 to 0.09375
- residual: bfloat16 [256, 8192], P(('groups', 'dp', 'seq'), 'tensor'), parts along dimension 0, may hold values from -32 to 32
- norm_gain: bfloat16 [8192], P('tensor'), may hold values from 0.099609375 to 1.8984375
Outputs:
- stream: bfloat16 [256, 8192], P(('groups', 'dp', 'seq'), 'tensor'), parts along dimension 0
- normed: bfloat16 [256, 8192], P(('groups', 'dp', 'seq')), parts along dimension 0
There are 2 independent parts, one for each index of `groups`. A program takes and returns all parts, laid end to end along the dimension named above; an argument that names none is the same for every part. Nothing has to cross between parts.
All inputs are finite; a program needn't handle non-finite values.
Results may differ from a plain program's by a relative error of at most 0.0056.
Values may be sent and summed in bfloat16 or wider, within the bound.
No kernel may reach another device: no remote copies, remote signals or barrier semaphores. Data moves between devices by JAX's collectives and lax.ppermute only.
A program may use at most 64 MiB of HBM per device.

v0:
```python
import jax
import jax.numpy as jnp
from jax import lax
from jax.sharding import PartitionSpec as P

D = 8192


def block_term(amount, operand, weight, row_count, halves, tensor_size):
    blocks = amount // row_count
    block_width = weight.shape[1] // tensor_size
    span_blocks = min(tensor_size, (blocks + halves - 1) // halves + 1)
    product = jnp.dot(operand, weight, preferred_element_type=jnp.float32)
    product = product.reshape(halves, row_count, span_blocks, block_width)
    product = product.transpose(2, 0, 1, 3).reshape(span_blocks * halves * row_count, block_width)
    return product


def normalize(read, gain_values, square_sum):
    stream_float = read.astype(jnp.float32)
    mean_square = square_sum[:, None] / D
    scaled = (
        stream_float * lax.rsqrt(mean_square + 1e-05) * gain_values.astype(jnp.float32)[None, :]
    )
    return scaled.astype(jnp.bfloat16)


def squares(read):
    stream_float = read.astype(jnp.float32)
    return jnp.sum(stream_float * stream_float, axis=1)


def on_device(attn_heads, out_weight, residual, norm_gain):
    row_count = attn_heads.shape[0]
    half_width = out_weight.shape[0]
    tensor_size = lax.axis_size("tensor")
    halves = lax.axis_size("seq")
    seq_index = lax.axis_index("seq")
    paired_rows = lax.all_gather(attn_heads, "seq", axis=0, tiled=True)
    operand = lax.dynamic_slice_in_dim(paired_rows, seq_index * half_width, half_width, 1)
    attended = lax.psum_scatter(
        block_term(
            row_count * lax.axis_size(("tensor", "seq")),
            operand,
            out_weight,
            row_count,
            halves,
            tensor_size,
        ),
        ("tensor", "seq"),
        scatter_dimension=0,
        tiled=True,
    )
    read = (residual.astype(jnp.float32) + attended).astype(jnp.bfloat16)
    stream_full, gain_full = (
        lax.all_gather(read, "tensor", axis=1, tiled=True),
        lax.all_gather(norm_gain, "tensor", axis=0, tiled=True),
    )
    normed = normalize(stream_full, gain_full, squares(stream_full))
    return (read, normed)


def solution(mesh):
    in_specs = (
        P(("groups", "dp", "seq"), "tensor"),
        P(("tensor", "seq"), None),
        P(("groups", "dp", "seq"), "tensor"),
        P("tensor"),
    )
    out_specs = (P(("groups", "dp", "seq"), "tensor"), P(("groups", "dp", "seq"), None))
    return jax.shard_map(
        on_device, mesh=mesh, in_specs=in_specs, out_specs=out_specs, check_vma=False
    )
```

profile of v0, /device:TPU:0, one launch (start us, length us, event | category | flops | bytes accessed | tf_op | source)
XLA Modules:
  0.0 87.8 jit_solution(3788425832741213699)
XLA Ops:
  7.2 0.0 reduce-scatter.2.cloned.1.call-start
  7.2 2.3 %all_gather.9 = bf16[64,2048]{1,0:T(8,128)(2,1)S(1)} all-gather(bf16[32,2048]{1,0:T(8,128)(2,1)} %param.4), channel_id=1, replica_groups=mesh['groups'=2,'tensor'=4,'dp'=2,'seq'=2] {'seq'}, dimensions={0}, use_global_device_ids=true | all-gather | bytes 393216 | tf_op jit(solution)/shard_map/all_gather | solution.py:39
  9.5 0.0 copy-start.2
  9.5 0.0 copy-start.1
  9.6 8.8 %fusion.3 = f32[64,8192]{1,0:T(8,128)S(1)} fusion(bf16[1024,8192]{1,0:T(8,128)(2,1)} %param.5, bf16[64,2048]{1,0:T(8,128)(2,1)S(1)} %all_gather.9, s32[]{:T(128)S(6)} %select_n.3), kind=kOutput, calls=%fused_computation.6 | convolution fusion | flops 1073741824 | bytes 19005444 | tf_op jit(solution)/shard_map/dot_general | solution.py:13
  18.4 2.4 %reshape.19 = f32[2,32,4,2048]{3,2,1,0:T(4,128)} reshape(f32[64,8192]{1,0:T(8,128)S(1)} %fusion.3) | data formatting | bytes 4194304 | tf_op jit(solution)/shard_map/reshape | solution.py:14
  20.8 4.2 %copy.7 = f32[4,2,32,2048]{3,2,1,0:T(8,128)} copy(f32[4,2,32,2048]{3,0,2,1:T(4,128)} %bitcast.4) | data formatting | bytes 4194304 | tf_op jit(solution)/shard_map/transpose | solution.py:15
  25.0 0.0 reduce-scatter.2.cloned.1.call-update
  25.0 0.0 copy-done.2
  25.0 14.8 %all_gather.11 = bf16[8192]{0:T(1024)(128)(2,1)S(1)} all-gather(bf16[2048]{0:T(1024)(128)(2,1)S(1)} %copy-done.2), channel_id=1, replica_groups=mesh['groups'=2,'tensor'=4,'dp'=2,'seq'=2] {'tensor'}, dimensions={0}, use_global_device_ids=true | all-gather | bytes 20480 | tf_op jit(solution)/shard_map/all_gather | solution.py:57
  39.8 24.1 %reduce-scatter.2.cloned.1.call-done = f32[32,2048]{1,0:T(8,128)} async-done(((f32[256,2048]{1,0:T(8,128)}), f32[32,2048]{1,0:T(8,128)}) %reduce-scatter.2.cloned.1.call-update) | async-done | bytes 262160 | tf_op jit(solution)/shard_map/reduce_scatter | solution.py:41
  63.9 0.0 copy-done.1
  63.9 1.0 %add_convert_fusion = bf16[32,2048]{1,0:T(8,128)(2,1)S(1)} fusion(f32[32,2048]{1,0:T(8,128)} %reduce-scatter.2.cloned.1.call-done, bf16[32,2048]{1,0:T(8,128)(2,1)S(1)} %copy-done.1), kind=kLoop, calls=%fused_computation.5 | loop fusion | flops 196608 | bytes 524288 | tf_op jit(solution)/shard_map/convert_element_type | solution.py:54
  64.9 0.0 copy-start
  64.9 14.9 %all_gather.10 = bf16[32,8192]{1,0:T(8,128)(2,1)S(1)} all-gather(bf16[32,2048]{1,0:T(8,128)(2,1)S(1)} %add_convert_fusion), channel_id=1, replica_groups=mesh['groups'=2,'tensor'=4,'dp'=2,'seq'=2] {'tensor'}, dimensions={1}, use_global_device_ids=true | all-gather | bytes 655360 | tf_op jit(solution)/shard_map/all_gather | solution.py:56
  79.7 0.2 fusion
  80.0 1.0 %fusion.2 = bf16[32,8192]{1,0:T(8,128)(2,1)} fusion(bf16[32,8192]{1,0:T(8,128)(2,1)S(1)} %all_gather.10, f32[8192]{0:T(1024)S(1)} %convert_element_type.19, f32[32]{0:T(128)S(1)} %add_rsqrt_fusion), kind=kLoop, calls=%fused_computation.4 | loop fusion | flops 1048576 | bytes 1081472 | tf_op jit(solution)/shard_map/convert_element_type | solution.py:25
  81.0 0.0 copy-done
  (2 shorter events, 0.0 us)
Async XLA Ops:
  7.2 56.7 %reduce-scatter.2.cloned.1.call-start = ((), (), s32[]{:S(2)}) async-start(), calls=%async_computation.1 | async-start | bytes 2359296 | tf_op jit(solution)/shard_map/reduce_scatter | solution.py:41
  9.5 15.4 %copy-start.2 = (bf16[2048]{0:T(1024)(128)(2,1)S(1)}, bf16[2048]{0:T(1024)(128)(2,1)}, u32[]{:S(2)}) copy-start(bf16[2048]{0:T(1024)(128)(2,1)} %param.7) | copy-start | bytes 12292
  9.5 54.3 %copy-start.1 = (bf16[32,2048]{1,0:T(8,128)(2,1)S(1)}, bf16[32,2048]{1,0:T(8,128)(2,1)}, u32[]{:S(2)}) copy-start(bf16[32,2048]{1,0:T(8,128)(2,1)} %param.6) | copy-start | bytes 393220
  64.9 16.1 %copy-start = (bf16[32,2048]{1,0:T(8,128)(2,1)}, bf16[32,2048]{1,0:T(8,128)(2,1)S(1)}, u32[]{:S(2)}) copy-start(bf16[32,2048]{1,0:T(8,128)(2,1)S(1)} %add_convert_fusion) | copy-start | bytes 393220
Sparse Core Ops, SparseCore 0:
  25.1 38.7 reduce-scatter.1
where the time goes:
time: 88 us; the launch traced here: 87.8 us
  blocking collectives  32 us (36%)
  waiting for transfers between devices  24.1 us (27%)
  between operations  14.1 us (16%)
  matrix products  8.82 us (10%)
  local copies, waits for them, and re-layouts  6.6 us (8%)
  other arithmetic  2.21 us (3%)
    reduce_scatter x1, waiting for transfers between devices, on_device(): lax.psum_scatter(block_term(row_count * lax.axis_size(('tensor', 'seq')),...  24.1 us
    all_gather x1, blocking collectives, on_device(): lax.all_gather(read, 'tensor', axis=1, tiled=True)  14.9 us
    all_gather x1, blocking collectives, on_device(): lax.all_gather(norm_gain, 'tensor', axis=0, tiled=True)  14.8 us
    dot_general x1, matrix products, block_term(): product = jnp.dot(operand, weight, preferred_element_type=jnp.float32)  8.82 us
    transpose x1, local copies, waits for them, and re-layouts, block_term(): product.transpose(2, 0, 1, 3)  4.15 us
    reshape x1, local copies, waits for them, and re-layouts, block_term(): product = product.reshape(halves, row_count, span_blocks, block_width)  2.43 us
    all_gather x1, blocking collectives, on_device(): paired_rows = lax.all_gather(attn_heads, 'seq', axis=0, tiled=True)  2.33 us
  transfers between devices with their start and end apart: 1, of which 1 were waited for; matrix products, arithmetic and copies ran while one was open for 0% of the time, Pallas kernels for 0%

commit v1 on v0

v1 whole, which is shorter than its diff:
```python
import functools

import jax
import jax.numpy as jnp
from jax import lax
from jax.experimental import pallas as pl
from jax.experimental.pallas import tpu as pltpu
from jax.sharding import PartitionSpec as P

VMEM = pltpu.VMEM
HBM = pltpu.HBM
MIB = 1024 * 1024
F32, BF16 = jnp.float32, jnp.bfloat16


def project_kernel(tensor, chunk, own_ref, peer_ref, weight, keep_ref, give_ref, held, sems):
    depth, width = weight.shape
    block = width // tensor
    per_block = block // chunk
    rank = lax.axis_index("tensor")
    half = lax.axis_index("seq")

    def copy(index):
        step, piece = divmod(index, per_block)
        start = (rank ^ step) * block + piece * chunk
        return pltpu.make_async_copy(
            weight.at[:, pl.ds(pl.multiple_of(start, 128), chunk)], held.at[index], sems.at[index]
        )

    count = tensor * per_block
    for index in range(count):
        copy(index).start()
    features = pl.ds(pl.multiple_of(half * depth, 128), depth)
    rows = own_ref.shape[0]
    operand = jnp.concatenate([own_ref[:, features], peer_ref[:, features]], axis=0)
    for index in range(count):
        step, piece = divmod(index, per_block)
        copy(index).wait()
        product = jnp.dot(operand, held[index], preferred_element_type=F32)
        columns = pl.ds(piece * chunk, chunk)
        keep_ref[step, :, columns] = product[:rows]
        give_ref[step, :, columns] = product[rows:].astype(BF16)


def project(own, peer, weight, tensor):
    rows = own.shape[0]
    depth, width = weight.shape
    block = width // tensor
    chunk = min(block, 512)
    count = width // chunk
    return pl.pallas_call(
        functools.partial(project_kernel, tensor, chunk),
        in_specs=[
            pl.BlockSpec(memory_space=VMEM),
            pl.BlockSpec(memory_space=VMEM),
            pl.BlockSpec(memory_space=HBM),
        ],
        out_specs=[pl.BlockSpec(memory_space=VMEM)] * 2,
        out_shape=[
            jax.ShapeDtypeStruct((tensor, rows, block), F32),
            jax.ShapeDtypeStruct((tensor, rows, block), BF16),
        ],
        scratch_shapes=[
            VMEM((count, depth, chunk), BF16),
            pltpu.SemaphoreType.DMA((count,)),
        ],
        compiler_params=pltpu.CompilerParams(vmem_limit_bytes=2 * weight.size + 8 * MIB),
        name="project",
    )(own, peer, pltpu.with_memory_space_constraint(weight, HBM))


def pair_kernel(keep_ref, got_ref, residual_ref, base_ref, *send_refs):
    base_ref[...] = residual_ref[...].astype(F32) + keep_ref[0] + got_ref[0].astype(F32)
    for step, send_ref in enumerate(send_refs, 1):
        send_ref[...] = (keep_ref[step] + got_ref[step].astype(F32)).astype(BF16)


def pair_sum(keep, got, residual):
    tensor, rows, block = keep.shape
    return pl.pallas_call(
        pair_kernel,
        in_specs=[pl.BlockSpec(memory_space=VMEM)] * 3,
        out_specs=[pl.BlockSpec(memory_space=VMEM)] * tensor,
        out_shape=[jax.ShapeDtypeStruct((rows, block), F32)]
        + [jax.ShapeDtypeStruct((rows, block), BF16)] * (tensor - 1),
        compiler_params=pltpu.CompilerParams(vmem_limit_bytes=6 * MIB),
        name="pair_sum",
    )(keep, got, residual)


def stream_kernel(base_ref, *refs):
    total = base_ref[...]
    for ref in refs[:-2]:
        total = total + ref[...].astype(F32)
    stream = total.astype(BF16)
    refs[-2][...] = stream
    refs[-1][...] = stream


def finish_stream(base, parts):
    return pl.pallas_call(
        stream_kernel,
        in_specs=[pl.BlockSpec(memory_space=VMEM)] * (1 + len(parts)),
        out_specs=[pl.BlockSpec(memory_space=VMEM)] * 2,
        out_shape=[jax.ShapeDtypeStruct(base.shape, BF16)] * 2,
        compiler_params=pltpu.CompilerParams(vmem_limit_bytes=6 * MIB),
        name="finish_stream",
    )(base, *parts)


def norm_kernel(tensor, *refs):
    pieces, gains, out_ref = refs[:tensor], refs[tensor : 2 * tensor], refs[-1]
    block = pieces[0].shape[1]
    rank = lax.axis_index("tensor")
    total = 0.0
    for piece in pieces:
        value = piece[...].astype(F32)
        total = total + jnp.sum(value * value, axis=1, keepdims=True)
    scale = lax.rsqrt(total / (tensor * block) + 1e-05)
    for step in range(tensor):
        start = pl.multiple_of((rank ^ step) * block, 128)
        value = pieces[step][...].astype(F32) * scale * gains[step][...].astype(F32)
        out_ref[:, pl.ds(start, block)] = value.astype(BF16)


def normalize(pieces, gains):
    tensor = len(pieces)
    rows, block = pieces[0].shape
    return pl.pallas_call(
        functools.partial(norm_kernel, tensor),
        in_specs=[pl.BlockSpec(memory_space=VMEM)] * (2 * tensor),
        out_specs=pl.BlockSpec(memory_space=VMEM),
        out_shape=jax.ShapeDtypeStruct((rows, tensor * block), BF16),
        compiler_params=pltpu.CompilerParams(vmem_limit_bytes=6 * MIB),
        name="normalize",
    )(*pieces, *gains)


def on_device(attn_heads, out_weight, residual, norm_gain):
    tensor = lax.axis_size("tensor")
    swap = [(0, 1), (1, 0)]

    def exchange(value, step):
        return lax.ppermute(value, "tensor", [(i, i ^ step) for i in range(tensor)])

    peer = lax.ppermute(attn_heads, "seq", swap)
    keep, give = project(attn_heads, peer, out_weight, tensor)
    got = lax.ppermute(give, "seq", swap)
    base, *sends = pair_sum(keep, got, residual)
    gain = norm_gain[None, :]
    gains = [gain] + [exchange(gain, step) for step in range(1, tensor)]
    parts = [exchange(value, step) for step, value in enumerate(sends, 1)]
    stream, piece = finish_stream(base, parts)
    pieces = [piece] + [exchange(piece, step) for step in range(1, tensor)]
    return stream, normalize(pieces, gains)


def solution(mesh):
    in_specs = (
        P(("groups", "dp", "seq"), "tensor"),
        P(("tensor", "seq"), None),
        P(("groups", "dp", "seq"), "tensor"),
        P("tensor"),
    )
    out_specs = (P(("groups", "dp", "seq"), "tensor"), P(("groups", "dp", "seq"), None))
    return jax.shard_map(
        on_device, mesh=mesh, in_specs=in_specs, out_specs=out_specs, check_vma=False
    )
```

time: 88 us -> 49.1 us (0.56)
  blocking collectives: 32 us -> 0 us
  starting transfers between devices: 0.04 us -> 18.7 us
  between operations: 14.1 us -> 0.66 us
  matrix products: 8.82 us -> 0 us
  Pallas kernels: 0 us -> 8.3 us
  local copies, waits for them, and re-layouts: 6.6 us -> 0.92 us
  waiting for transfers between devices: 24.1 us -> 20.4 us
  other arithmetic: 2.21 us -> 0 us
    all_gather x3 -> x0, blocking collectives: 32 us -> none  [the longest x1 14.9 us: on_device(): lax.all_gather(read, 'tensor', axis=1, tiled=True)]
    reduce_scatter x1 -> x0, waiting for transfers between devices: 24.1 us -> none  [on_device(): lax.psum_scatter(block_term(row_count * lax.axis_size(('tensor', 'seq')),...]
    ppermute x0 -> x11, waiting for transfers between devices: none -> 20.4 us  [the longest x9 17.6 us: exchange(): return lax.ppermute(value, 'tensor', [(i, i ^ step) for i in range(tensor)])]
    ppermute x0 -> x11, starting transfers between devices: none -> 18.7 us  [the longest x9 17.7 us: exchange(): return lax.ppermute(value, 'tensor', [(i, i ^ step) for i in range(tensor)])]
    dot_general x1 -> x0, matrix products: 8.82 us -> none  [block_term(): product = jnp.dot(operand, weight, preferred_element_type=jnp.float32)]
    pallas_call x0 -> x4, Pallas kernels: none -> 8.3 us  [the longest x1 6.38 us: project(): pl.pallas_call(functools.partial(project_kernel, tensor, chunk), in_specs...]
    transpose x1 -> x0, local copies, waits for them, and re-layouts: 4.15 us -> none  [block_term(): product.transpose(2, 0, 1, 3)]
    reshape x1 -> x0, local copies, waits for them, and re-layouts: 2.43 us -> none  [block_term(): product = product.reshape(halves, row_count, span_blocks, block_width)]
  transfers between devices with their start and end apart: 1 -> 11, of which waited for: 1 -> 6; matrix products, arithmetic and copies ran while one was open for 0% -> 0% of each run, Pallas kernels for 0% -> 0%
where the time goes in v1:
time: 49.1 us; the launch traced here: 48.9 us
  waiting for transfers between devices  20.4 us (42%)
  starting transfers between devices  18.7 us (38%)
  Pallas kernels  8.3 us (17%)
  local copies, waits for them, and re-layouts  0.92 us (2%)
  between operations  0.66 us (1%)
    ppermute x9, starting transfers between devices, exchange(): return lax.ppermute(value, 'tensor', [(i, i ^ step) for i in range(tensor)])  17.7 us
    ppermute x9, waiting for transfers between devices, exchange(): return lax.ppermute(value, 'tensor', [(i, i ^ step) for i in range(tensor)])  17.6 us
    pallas_call x1, Pallas kernels, project(): pl.pallas_call(functools.partial(project_kernel, tensor, chunk), in_specs...  6.38 us
    ppermute x1, waiting for transfers between devices, on_device(): got = lax.ppermute(give, 'seq', swap)  1.55 us
    ppermute x1, waiting for transfers between devices, on_device(): peer = lax.ppermute(attn_heads, 'seq', swap)  1.2 us
    pallas_call x1, Pallas kernels, normalize(): pl.pallas_call(functools.partial(norm_kernel, tensor), in_specs=[pl.Block...  1.1 us
  transfers between devices with their start and end apart: 11, of which 6 were waited for; matrix products, arithmetic and copies ran while one was open for 0% of the time, Pallas kernels for 0%

profile of v1, /device:TPU:0, one launch (start us, length us, event | category | flops | bytes accessed | tf_op | source)
XLA Modules:
  0.0 48.9 jit_solution(2911469158506432838)
XLA Ops:
  0.6 0.6 %collective-permute-start = (bf16[32,2048]{1,0:T(8,128)(2,1)}, bf16[32,2048]{1,0:T(8,128)(2,1)S(1)}, u32[]{:S(2)}, u32[]{:S(2)}) collective-permute-start(bf16[32,2048]{1,0:T(8,128)(2,1)} %own_ref.1), channel_id=1, source_target_pairs={{0,1},{1,0},{2,3},{3,2},{4,5},{5,4},{6,7},{7,6},{8,9},{9,8},{10,11... | collective-permute-start | bytes 393224 | tf_op jit(solution)/shard_map/ppermute | solution.py:146
  1.2 1.2 %collective-permute-done.peer_ref = bf16[32,2048]{1,0:T(8,128)(2,1)S(1)} collective-permute-done((bf16[32,2048]{1,0:T(8,128)(2,1)}, bf16[32,2048]{1,0:T(8,128)(2,1)S(1)}, u32[]{:S(2)}, u32[]{:S(2)}) %collective-permute-start) | collective-permute-done | bytes 131104 | tf_op jit(solution)/shard_map/ppermute | solution.py:146
  2.4 0.9 %copy-done = bf16[32,2048]{1,0:T(8,128)(2,1)S(1)} copy-done((bf16[32,2048]{1,0:T(8,128)(2,1)S(1)}, bf16[32,2048]{1,0:T(8,128)(2,1)}, u32[]{:S(2)}) %copy-start) | copy-done | bytes 131096
  3.3 6.4 %project.1 = (f32[4,32,2048]{2,1,0:T(8,128)S(1)}, bf16[4,32,2048]{2,1,0:T(8,128)(2,1)S(1)}) custom-call(bf16[32,2048]{1,0:T(8,128)(2,1)S(1)} %copy-done, bf16[32,2048]{1,0:T(8,128)(2,1)S(1)} %collective-permute-done.peer_ref, bf16[1024,8192]{1,0:T(8,128)(2,1)} %weight.1), custom_call_target="tpu_custom_call" | custom-call | tf_op jit(solution)/shard_map/project/pallas_call | solution.py:51
  9.7 0.4 collective-permute-start.1
  10.1 1.5 %collective-permute-done.1.got_ref = bf16[4,32,2048]{2,1,0:T(8,128)(2,1)S(1)} collective-permute-done((bf16[4,32,2048]{2,1,0:T(8,128)(2,1)S(1)}, bf16[4,32,2048]{2,1,0:T(8,128)(2,1)S(1)}, u32[]{:S(2)}, u32[]{:S(2)}) %collective-permute-start.1) | collective-permute-done | bytes 524320 | tf_op jit(solution)/shard_map/ppermute | solution.py:148
  11.7 0.1 pair_sum.1
  11.8 3.0 %collective-permute-start.2 = (bf16[32,2048]{1,0:T(8,128)(2,1)S(1)}, bf16[32,2048]{1,0:T(8,128)(2,1)S(1)}, u32[]{:S(2)}, u32[]{:S(2)}) collective-permute-start(bf16[32,2048]{1,0:T(8,128)(2,1)S(1)} %get-tuple-element.13), channel_id=1, source_target_pairs={{0,4},{4,0},{8,12},{12,8},{1,5},{5,1},{9,13},{13,9},{2,6},{6,2},{1... | collective-permute-start | bytes 393224 | tf_op jit(solution)/shard_map/ppermute | solution.py:144
  14.8 2.6 %collective-permute-start.3 = (bf16[32,2048]{1,0:T(8,128)(2,1)S(1)}, bf16[32,2048]{1,0:T(8,128)(2,1)S(1)}, u32[]{:S(2)}, u32[]{:S(2)}) collective-permute-start(bf16[32,2048]{1,0:T(8,128)(2,1)S(1)} %get-tuple-element.14), channel_id=1, source_target_pairs={{0,8},{4,12},{8,0},{12,4},{1,9},{5,13},{9,1},{13,5},{2,10},{6,14},... | collective-permute-start | bytes 393224 | tf_op jit(solution)/shard_map/ppermute | solution.py:144
  17.3 0.0 collective-permute-start.4
  17.3 3.1 %collective-permute-done.2.refs_0_ = bf16[32,2048]{1,0:T(8,128)(2,1)S(1)} collective-permute-done((bf16[32,2048]{1,0:T(8,128)(2,1)S(1)}, bf16[32,2048]{1,0:T(8,128)(2,1)S(1)}, u32[]{:S(2)}, u32[]{:S(2)}) %collective-permute-start.2) | collective-permute-done | bytes 131104 | tf_op jit(solution)/shard_map/ppermute | solution.py:144
  20.5 7.2 %collective-permute-done.3.refs_1_ = bf16[32,2048]{1,0:T(8,128)(2,1)S(1)} collective-permute-done((bf16[32,2048]{1,0:T(8,128)(2,1)S(1)}, bf16[32,2048]{1,0:T(8,128)(2,1)S(1)}, u32[]{:S(2)}, u32[]{:S(2)}) %collective-permute-start.3) | collective-permute-done | bytes 131104 | tf_op jit(solution)/shard_map/ppermute | solution.py:144
  27.6 0.0 collective-permute-done.4.refs_2_
  27.6 0.7 %finish_stream.1 = (bf16[32,2048]{1,0:T(8,128)(2,1)}, bf16[32,2048]{1,0:T(8,128)(2,1)S(1)}) custom-call(f32[32,2048]{1,0:T(8,128)S(1)} %get-tuple-element.12.base_ref, bf16[32,2048]{1,0:T(8,128)(2,1)S(1)} %collective-permute-done.2.refs_0_, bf16[32,2048]{1,0:T(8,128)(2,1)S(1)} %collective-permute-done.3.refs_1_, ...), custom_call_target="tpu_custom_call" | custom-call | tf_op jit(solution)/shard_map/finish_stream/pallas_call | solution.py:101
  28.4 2.3 %collective-permute-start.5 = (bf16[32,2048]{1,0:T(8,128)(2,1)S(1)}, bf16[32,2048]{1,0:T(8,128)(2,1)S(1)}, u32[]{:S(2)}, u32[]{:S(2)}) collective-permute-start(bf16[32,2048]{1,0:T(8,128)(2,1)S(1)} %get-tuple-element.17.refs_0_), channel_id=1, source_target_pairs={{0,4},{4,0},{8,12},{12,8},{1,5},{5,1},{9,13},{13,9},{2,6},{6,2},{1... | collective-permute-start | bytes 393224 | tf_op jit(solution)/shard_map/ppermute | solution.py:144
  30.7 1.0 %collective-permute-start.6 = (bf16[32,2048]{1,0:T(8,128)(2,1)S(1)}, bf16[32,2048]{1,0:T(8,128)(2,1)S(1)}, u32[]{:S(2)}, u32[]{:S(2)}) collective-permute-start(bf16[32,2048]{1,0:T(8,128)(2,1)S(1)} %get-tuple-element.17.refs_0_), channel_id=1, source_target_pairs={{0,8},{4,12},{8,0},{12,4},{1,9},{5,13},{9,1},{13,5},{2,10},{6,14},... | collective-permute-start | bytes 393224 | tf_op jit(solution)/shard_map/ppermute | solution.py:144
  31.7 1.5 %collective-permute-start.7 = (bf16[32,2048]{1,0:T(8,128)(2,1)S(1)}, bf16[32,2048]{1,0:T(8,128)(2,1)S(1)}, u32[]{:S(2)}, u32[]{:S(2)}) collective-permute-start(bf16[32,2048]{1,0:T(8,128)(2,1)S(1)} %get-tuple-element.17.refs_0_), channel_id=1, source_target_pairs={{0,12},{4,8},{8,4},{12,0},{1,13},{5,9},{9,5},{13,1},{2,14},{6,10},... | collective-permute-start | bytes 393224 | tf_op jit(solution)/shard_map/ppermute | solution.py:144
  33.2 2.4 %collective-permute-start.10 = (bf16[1,2048]{1,0:T(2,128)(2,1)S(1)}, bf16[1,2048]{1,0:T(2,128)(2,1)S(1)}, u32[]{:S(2)}, u32[]{:S(2)}) collective-permute-start(bf16[1,2048]{1,0:T(2,128)(2,1)S(1)} %broadcast_in_dim.3.refs_4_), channel_id=1, source_target_pairs={{0,12},{4,8},{8,4},{12,0},{1,13},{5,9},{9,5},{13,1},{2,14},{6,10},... | collective-permute-start | bytes 12296 | tf_op jit(solution)/shard_map/ppermute | solution.py:144
  35.6 0.2 collective-permute-start.8
  35.8 5.7 %collective-permute-done.10.refs_7_ = bf16[1,2048]{1,0:T(2,128)(2,1)S(1)} collective-permute-done((bf16[1,2048]{1,0:T(2,128)(2,1)S(1)}, bf16[1,2048]{1,0:T(2,128)(2,1)S(1)}, u32[]{:S(2)}, u32[]{:S(2)}) %collective-permute-start.10) | collective-permute-done | bytes 4128 | tf_op jit(solution)/shard_map/ppermute | solution.py:144
  41.5 4.7 %collective-permute-start.9 = (bf16[1,2048]{1,0:T(2,128)(2,1)S(1)}, bf16[1,2048]{1,0:T(2,128)(2,1)S(1)}, u32[]{:S(2)}, u32[]{:S(2)}) collective-permute-start(bf16[1,2048]{1,0:T(2,128)(2,1)S(1)} %broadcast_in_dim.3.refs_4_), channel_id=1, source_target_pairs={{0,8},{4,12},{8,0},{12,4},{1,9},{5,13},{9,1},{13,5},{2,10},{6,14},... | collective-permute-start | bytes 12296 | tf_op jit(solution)/shard_map/ppermute | solution.py:144
  46.2 0.0 collective-permute-done.8.refs_5_
  46.2 1.6 %collective-permute-done.9.refs_6_ = bf16[1,2048]{1,0:T(2,128)(2,1)S(1)} collective-permute-done((bf16[1,2048]{1,0:T(2,128)(2,1)S(1)}, bf16[1,2048]{1,0:T(2,128)(2,1)S(1)}, u32[]{:S(2)}, u32[]{:S(2)}) %collective-permute-start.9) | collective-permute-done | bytes 4128 | tf_op jit(solution)/shard_map/ppermute | solution.py:144
  47.8 1.1 %normalize.1 = bf16[32,8192]{1,0:T(8,128)(2,1)} custom-call(bf16[32,2048]{1,0:T(8,128)(2,1)S(1)} %get-tuple-element.17.refs_0_, bf16[32,2048]{1,0:T(8,128)(2,1)S(1)} %collective-permute-done.5.refs_1_, bf16[32,2048]{1,0:T(8,128)(2,1)S(1)} %collective-permute-done.6.refs_2_, bf16[32,2048]{1,0:T(8,128)(2,1)S(1)} %collective-permute-done.7.refs_3_, ...), custom_call_target="tpu_custom_call" | custom-call | tf_op jit(solution)/shard_map/normalize/pallas_call | solution.py:129
  (9 shorter events, 0.0 us)
Async XLA Ops:
  0.6 1.8 %collective-permute-start = (bf16[32,2048]{1,0:T(8,128)(2,1)}, bf16[32,2048]{1,0:T(8,128)(2,1)S(1)}, u32[]{:S(2)}, u32[]{:S(2)}) collective-permute-start(bf16[32,2048]{1,0:T(8,128)(2,1)} %own_ref.1), channel_id=1, source_target_pairs={{0,1},{1,0},{2,3},{3,2},{4,5},{5,4},{6,7},{7,6},{8,9},{9,8},{10,11... | collective-permute-start | bytes 393224 | tf_op jit(solution)/shard_map/ppermute | solution.py:146
  2.4 0.9 %copy-start = (bf16[32,2048]{1,0:T(8,128)(2,1)S(1)}, bf16[32,2048]{1,0:T(8,128)(2,1)}, u32[]{:S(2)}) copy-start(bf16[32,2048]{1,0:T(8,128)(2,1)} %own_ref.1) | copy-start | bytes 393220
  3.3 8.4 %copy-start.1 = (bf16[32,2048]{1,0:T(8,128)(2,1)S(1)}, bf16[32,2048]{1,0:T(8,128)(2,1)}, u32[]{:S(2)}) copy-start(bf16[32,2048]{1,0:T(8,128)(2,1)} %residual_ref.1) | copy-start | bytes 393220
  3.3 29.9 %copy-start.2 = (bf16[2048]{0:T(1024)(128)(2,1)S(1)}, bf16[2048]{0:T(1024)(128)(2,1)}, u32[]{:S(2)}) copy-start(bf16[2048]{0:T(1024)(128)(2,1)} %param.7) | copy-start | bytes 12292
  9.7 2.0 %collective-permute-start.1 = (bf16[4,32,2048]{2,1,0:T(8,128)(2,1)S(1)}, bf16[4,32,2048]{2,1,0:T(8,128)(2,1)S(1)}, u32[]{:S(2)}, u32[]{:S(2)}) collective-permute-start(bf16[4,32,2048]{2,1,0:T(8,128)(2,1)S(1)} %get-tuple-element.11), channel_id=1, source_target_pairs={{0,1},{1,0},{2,3},{3,2},{4,5},{5,4},{6,7},{7,6},{8,9},{9,8},{10,11... | collective-permute-start | bytes 1572872 | tf_op jit(solution)/shard_map/ppermute | solution.py:148
  11.8 8.7 %collective-permute-start.2 = (bf16[32,2048]{1,0:T(8,128)(2,1)S(1)}, bf16[32,2048]{1,0:T(8,128)(2,1)S(1)}, u32[]{:S(2)}, u32[]{:S(2)}) collective-permute-start(bf16[32,2048]{1,0:T(8,128)(2,1)S(1)} %get-tuple-element.13), channel_id=1, source_target_pairs={{0,4},{4,0},{8,12},{12,8},{1,5},{5,1},{9,13},{13,9},{2,6},{6,2},{1... | collective-permute-start | bytes 393224 | tf_op jit(solution)/shard_map/ppermute | solution.py:144
  14.8 12.9 %collective-permute-start.3 = (bf16[32,2048]{1,0:T(8,128)(2,1)S(1)}, bf16[32,2048]{1,0:T(8,128)(2,1)S(1)}, u32[]{:S(2)}, u32[]{:S(2)}) collective-permute-start(bf16[32,2048]{1,0:T(8,128)(2,1)S(1)} %get-tuple-element.14), channel_id=1, source_target_pairs={{0,8},{4,12},{8,0},{12,4},{1,9},{5,13},{9,1},{13,5},{2,10},{6,14},... | collective-permute-start | bytes 393224 | tf_op jit(solution)/shard_map/ppermute | solution.py:144
  17.3 10.3 %collective-permute-start.4 = (bf16[32,2048]{1,0:T(8,128)(2,1)S(1)}, bf16[32,2048]{1,0:T(8,128)(2,1)S(1)}, u32[]{:S(2)}, u32[]{:S(2)}) collective-permute-start(bf16[32,2048]{1,0:T(8,128)(2,1)S(1)} %get-tuple-element.15), channel_id=1, source_target_pairs={{0,12},{4,8},{8,4},{12,0},{1,13},{5,9},{9,5},{13,1},{2,14},{6,10},... | collective-permute-start | bytes 393224 | tf_op jit(solution)/shard_map/ppermute | solution.py:144
  28.4 19.5 %collective-permute-start.5 = (bf16[32,2048]{1,0:T(8,128)(2,1)S(1)}, bf16[32,2048]{1,0:T(8,128)(2,1)S(1)}, u32[]{:S(2)}, u32[]{:S(2)}) collective-permute-start(bf16[32,2048]{1,0:T(8,128)(2,1)S(1)} %get-tuple-element.17.refs_0_), channel_id=1, source_target_pairs={{0,4},{4,0},{8,12},{12,8},{1,5},{5,1},{9,13},{13,9},{2,6},{6,2},{1... | collective-permute-start | bytes 393224 | tf_op jit(solution)/shard_map/ppermute | solution.py:144
  30.7 17.1 %collective-permute-start.6 = (bf16[32,2048]{1,0:T(8,128)(2,1)S(1)}, bf16[32,2048]{1,0:T(8,128)(2,1)S(1)}, u32[]{:S(2)}, u32[]{:S(2)}) collective-permute-start(bf16[32,2048]{1,0:T(8,128)(2,1)S(1)} %get-tuple-element.17.refs_0_), channel_id=1, source_target_pairs={{0,8},{4,12},{8,0},{12,4},{1,9},{5,13},{9,1},{13,5},{2,10},{6,14},... | collective-permute-start | bytes 393224 | tf_op jit(solution)/shard_map/ppermute | solution.py:144
  31.7 16.1 %collective-permute-start.7 = (bf16[32,2048]{1,0:T(8,128)(2,1)S(1)}, bf16[32,2048]{1,0:T(8,128)(2,1)S(1)}, u32[]{:S(2)}, u32[]{:S(2)}) collective-permute-start(bf16[32,2048]{1,0:T(8,128)(2,1)S(1)} %get-tuple-element.17.refs_0_), channel_id=1, source_target_pairs={{0,12},{4,8},{8,4},{12,0},{1,13},{5,9},{9,5},{13,1},{2,14},{6,10},... | collective-permute-start | bytes 393224 | tf_op jit(solution)/shard_map/ppermute | solution.py:144
  33.2 8.3 %collective-permute-start.10 = (bf16[1,2048]{1,0:T(2,128)(2,1)S(1)}, bf16[1,2048]{1,0:T(2,128)(2,1)S(1)}, u32[]{:S(2)}, u32[]{:S(2)}) collective-permute-start(bf16[1,2048]{1,0:T(2,128)(2,1)S(1)} %broadcast_in_dim.3.refs_4_), channel_id=1, source_target_pairs={{0,12},{4,8},{8,4},{12,0},{1,13},{5,9},{9,5},{13,1},{2,14},{6,10},... | collective-permute-start | bytes 12296 | tf_op jit(solution)/shard_map/ppermute | solution.py:144
  35.6 10.6 %collective-permute-start.8 = (bf16[1,2048]{1,0:T(2,128)(2,1)S(1)}, bf16[1,2048]{1,0:T(2,128)(2,1)S(1)}, u32[]{:S(2)}, u32[]{:S(2)}) collective-permute-start(bf16[1,2048]{1,0:T(2,128)(2,1)S(1)} %broadcast_in_dim.3.refs_4_), channel_id=1, source_target_pairs={{0,4},{4,0},{8,12},{12,8},{1,5},{5,1},{9,13},{13,9},{2,6},{6,2},{1... | collective-permute-start | bytes 12296 | tf_op jit(solution)/shard_map/ppermute | solution.py:144
  41.5 6.3 %collective-permute-start.9 = (bf16[1,2048]{1,0:T(2,128)(2,1)S(1)}, bf16[1,2048]{1,0:T(2,128)(2,1)S(1)}, u32[]{:S(2)}, u32[]{:S(2)}) collective-permute-start(bf16[1,2048]{1,0:T(2,128)(2,1)S(1)} %broadcast_in_dim.3.refs_4_), channel_id=1, source_target_pairs={{0,8},{4,12},{8,0},{12,4},{1,9},{5,13},{9,1},{13,5},{2,10},{6,14},... | collective-permute-start | bytes 12296 | tf_op jit(solution)/shard_map/ppermute | solution.py:144

commit v2 on v0

v2 whole, which is shorter than its diff:
```python
import functools

import jax
import jax.numpy as jnp
from jax import lax
from jax.experimental import pallas as pl
from jax.experimental.pallas import tpu as pltpu
from jax.sharding import PartitionSpec as P


VMEM, HBM = pltpu.VMEM, pltpu.HBM
MIB = 1024 * 1024
F32, BF16 = jnp.float32, jnp.bfloat16
LANES = 128
SPLITS = 1


def call(kernel, in_specs, out_shape, limit, scratch=()):
    return pl.pallas_call(
        kernel,
        in_specs=[pl.BlockSpec(memory_space=space) for space in in_specs],
        out_specs=[pl.BlockSpec(memory_space=VMEM)] * len(out_shape),
        out_shape=out_shape,
        scratch_shapes=list(scratch),
        compiler_params=pltpu.CompilerParams(vmem_limit_bytes=limit),
    )


def project_kernel(tensor, chunk, steps, own_hbm, peer_ref, weight, keep_ref, give_ref, own_ref, held, own_sem, sems):
    depth, width = weight.shape
    block = width // tensor
    per_block = block // chunk
    rank = lax.axis_index("tensor")
    features = pl.ds(pl.multiple_of(lax.axis_index("seq") * depth, LANES), depth)
    own_copy = pltpu.make_async_copy(own_hbm.at[:, features], own_ref, own_sem)
    own_copy.start()

    def copy(index):
        place, piece = divmod(index, per_block)
        start = (rank ^ steps[place]) * block + piece * chunk
        return pltpu.make_async_copy(
            weight.at[:, pl.ds(pl.multiple_of(start, LANES), chunk)], held.at[index], sems.at[index]
        )

    count = len(steps) * per_block
    for index in range(count):
        copy(index).start()
    own_copy.wait()
    rows = own_ref.shape[0]
    operand = jnp.concatenate([own_ref[...], peer_ref[:, features]], axis=0)
    for index in range(count):
        place, piece = divmod(index, per_block)
        copy(index).wait()
        product = jnp.dot(operand, held[index], preferred_element_type=F32)
        columns = pl.ds(piece * chunk, chunk)
        keep_ref[place, :, columns] = product[:rows]
        give_ref[place, :, columns] = product[rows:].astype(BF16)


def project(own, peer, weight, tensor, steps):
    rows = own.shape[0]
    depth, width = weight.shape
    block = width // tensor
    chunk = min(block, 512)
    count = len(steps) * block // chunk
    return call(
        functools.partial(project_kernel, tensor, chunk, steps),
        [HBM, VMEM, HBM],
        [
            jax.ShapeDtypeStruct((len(steps), rows, block), F32),
            jax.ShapeDtypeStruct((len(steps), rows, block), BF16),
        ],
        2 * depth * chunk * count + 4 * MIB,
        [
            VMEM((rows, depth), BF16),
            VMEM((count, depth, chunk), BF16),
            pltpu.SemaphoreType.DMA(()),
            pltpu.SemaphoreType.DMA((count,)),
        ],
    )(
        pltpu.with_memory_space_constraint(own, HBM),
        peer,
        pltpu.with_memory_space_constraint(weight, HBM),
    )


def pair_kernel(steps, keep_ref, got_ref, residual_ref, gain_ref, *out_refs):
    _, rows, block = keep_ref.shape
    part = rows // SPLITS
    targets = iter(out_refs)
    for place, step in enumerate(steps):
        for split in range(SPLITS):
            target = next(targets)
            span = slice(split * part, (split + 1) * part)
            for tile in range(block // LANES):
                columns = slice(tile * LANES, (tile + 1) * LANES)
                value = keep_ref[place, span, columns] + got_ref[place, span, columns].astype(F32)
                if step == 0:
                    value = value + residual_ref[span, columns].astype(F32)
                target[tile * part : (tile + 1) * part, :] = value.astype(target.dtype)
            if step and not split:
                target[block // LANES * part :, :] = gain_ref[...]


def pair_sum(steps, keep, got, residual, gain):
    _, rows, block = keep.shape
    length = rows // SPLITS * block // LANES
    shapes = []
    for step in steps:
        for split in range(SPLITS):
            extra = gain.shape[0] if step and not split else 0
            shapes.append(jax.ShapeDtypeStruct((length + extra, LANES), BF16 if step else F32))
    outs = call(functools.partial(pair_kernel, steps), [VMEM] * 4, shapes, 6 * MIB)(
        keep, got, residual, gain
    )
    return {step: outs[i * SPLITS : (i + 1) * SPLITS] for i, step in enumerate(steps)}


def stream_kernel(base_ref, *refs):
    length = base_ref.shape[0]
    total = base_ref[...]
    for ref in refs[:-1]:
        total = total + ref[:length, :].astype(F32)
    refs[-1][...] = total.astype(BF16)


def finish_stream(base, parts):
    return call(
        stream_kernel, [VMEM] * (1 + len(parts)), [jax.ShapeDtypeStruct(base.shape, BF16)], 4 * MIB
    )(base, *parts)[0]


def norm_kernel(tensor, rows, block, *refs):
    pieces, refs = refs[: tensor * SPLITS], refs[tensor * SPLITS :]
    gains, (stream_ref, out_ref) = refs[:tensor], refs[tensor:]
    part = rows // SPLITS
    tiles = block // LANES
    rank = lax.axis_index("tensor")
    starts = [(rank ^ step) * block for step in range(tensor)]
    gain_rows = []
    for step, ref in enumerate(gains):
        first = tiles * part if step else 0
        gain_rows.append(ref[first:, :].astype(F32))
    for split in range(SPLITS):
        span = slice(split * part, (split + 1) * part)
        total = jnp.zeros((part, LANES), F32)
        for step in range(tensor):
            for tile in range(tiles):
                value = pieces[step * SPLITS + split][tile * part : (tile + 1) * part, :].astype(F32)
                total = total + value * value
        mean_square = jnp.sum(total, axis=1, keepdims=True) / (tensor * block)
        scale = jnp.broadcast_to(lax.rsqrt(mean_square + 1e-05), (part, LANES))
        for step in range(tensor):
            for tile in range(tiles):
                piece = pieces[step * SPLITS + split][tile * part : (tile + 1) * part, :]
                value = piece.astype(F32) * scale * gain_rows[step][tile : tile + 1, :]
                columns = pl.ds(pl.multiple_of(starts[step] + tile * LANES, LANES), LANES)
                out_ref[span, columns] = value.astype(BF16)
                if step == 0:
                    stream_ref[span, tile * LANES : (tile + 1) * LANES] = piece


def normalize(pieces, gains, rows, block):
    tensor = len(gains)
    return call(
        functools.partial(norm_kernel, tensor, rows, block),
        [VMEM] * (tensor * SPLITS + tensor),
        [
            jax.ShapeDtypeStruct((rows, block), BF16),
            jax.ShapeDtypeStruct((rows, tensor * block), BF16),
        ],
        6 * MIB,
    )(*pieces, *gains)


def on_device(attn_heads, out_weight, residual, norm_gain):
    tensor = lax.axis_size("tensor")
    rows, block = residual.shape
    swap = [(0, 1), (1, 0)]

    def exchange(value, step):
        return lax.ppermute(value, "tensor", [(i, i ^ step) for i in range(tensor)])

    gain = norm_gain.reshape(-1, LANES)
    gain = jnp.pad(gain, ((0, -gain.shape[0] % 16), (0, 0)))
    peer = lax.ppermute(attn_heads, "seq", swap)
    order = list(range(tensor // 2, tensor)) + list(range(1, tensor // 2)) + [0]
    waves = [order[: tensor // 2], order[tensor // 2 :]]
    got = None
    sums = {}
    arrived = {}
    for steps in waves:
        if got is not None:
            peer, _ = lax.optimization_barrier((peer, got))
        keep, give = project(attn_heads, peer, out_weight, tensor, steps)
        got = lax.ppermute(give, "seq", swap)
        sums.update(pair_sum(steps, keep, got, residual, gain))
        for step in steps:
            if step:
                arrived[step] = [exchange(value, step) for value in sums[step]]
    streams = [
        finish_stream(base, [arrived[step][split] for step in range(1, tensor)])
        for split, base in enumerate(sums[0])
    ]
    pieces = list(streams)
    for step in range(1, tensor):
        pieces += [exchange(value, step) for value in streams]
    gains = [gain] + [arrived[step][0] for step in range(1, tensor)]
    stream, normed = normalize(pieces, gains, rows, block)
    return stream, normed


def solution(mesh):
    in_specs = (
        P(("groups", "dp", "seq"), "tensor"),
        P(("tensor", "seq"), None),
        P(("groups", "dp", "seq"), "tensor"),
        P("tensor"),
    )
    out_specs = (P(("groups", "dp", "seq"), "tensor"), P(("groups", "dp", "seq"), None))

    return jax.shard_map(on_device, mesh=mesh, in_specs=in_specs, out_specs=out_specs, check_vma=False)
```

time: 88 us -> 47 us (0.53)
  blocking collectives: 32 us -> 0 us
  between operations: 14.1 us -> 0.68 us
  Pallas kernels: 0 us -> 12.4 us
  starting transfers between devices: 0.04 us -> 11.5 us
  matrix products: 8.82 us -> 0 us
  local copies, waits for them, and re-layouts: 6.6 us -> 0.01 us
  other arithmetic: 2.21 us -> 0 us
  waiting for transfers between devices: 24.1 us -> 22.3 us
    all_gather x3 -> x0, blocking collectives: 32 us -> none  [the longest x1 14.9 us: on_device(): lax.all_gather(read, 'tensor', axis=1, tiled=True)]
    reduce_scatter x1 -> x0, waiting for transfers between devices: 24.1 us -> none  [on_device(): lax.psum_scatter(block_term(row_count * lax.axis_size(('tensor', 'seq')),...]
    ppermute x0 -> x9, waiting for transfers between devices: none -> 22.3 us  [the longest x6 19.9 us: exchange(): return lax.ppermute(value, 'tensor', [(i, i ^ step) for i in range(tensor)])]
    pallas_call x0 -> x6, Pallas kernels: none -> 12.4 us  [the longest x2 11.1 us: project(): call(functools.partial(project_kernel, tensor, chunk, steps), [HBM, VMEM,...]
    ppermute x0 -> x9, starting transfers between devices: none -> 11.5 us  [the longest x6 10.1 us: exchange(): return lax.ppermute(value, 'tensor', [(i, i ^ step) for i in range(tensor)])]
    dot_general x1 -> x0, matrix products: 8.82 us -> none  [block_term(): product = jnp.dot(operand, weight, preferred_element_type=jnp.float32)]
    transpose x1 -> x0, local copies, waits for them, and re-layouts: 4.15 us -> none  [block_term(): product.transpose(2, 0, 1, 3)]
    reshape x1 -> x0, local copies, waits for them, and re-layouts: 2.43 us -> none  [block_term(): product = product.reshape(halves, row_count, span_blocks, block_width)]
  transfers between devices with their start and end apart: 1 -> 9, of which waited for: 1 -> 6; matrix products, arithmetic and copies ran while one was open for 0% -> 0% of each run, Pallas kernels for 0% -> 0%
where the time goes in v2:
time: 47 us; the launch traced here: 46.9 us
  waiting for transfers between devices  22.3 us (47%)
  Pallas kernels  12.4 us (26%)
  starting transfers between devices  11.5 us (24%)
  between operations  0.68 us (1%)
    ppermute x6, waiting for transfers between devices, exchange(): return lax.ppermute(value, 'tensor', [(i, i ^ step) for i in range(tensor)])  19.9 us
    pallas_call x2, Pallas kernels, project(): call(functools.partial(project_kernel, tensor, chunk, steps), [HBM, VMEM,...  11.1 us
    ppermute x6, starting transfers between devices, exchange(): return lax.ppermute(value, 'tensor', [(i, i ^ step) for i in range(tensor)])  10.1 us
    ppermute x1, waiting for transfers between devices, on_device(): peer = lax.ppermute(attn_heads, 'seq', swap)  1.2 us
    ppermute x2, waiting for transfers between devices, on_device(): got = lax.ppermute(give, 'seq', swap)  1.18 us
    pallas_call x1, Pallas kernels, normalize(): call(functools.partial(norm_kernel, tensor, rows, block), [VMEM] * (tenso...  1.12 us
  transfers between devices with their start and end apart: 9, of which 6 were waited for; matrix products, arithmetic and copies ran while one was open for 0% of the time, Pallas kernels for 0%

profile of v2, /device:TPU:0, one launch (start us, length us, event | category | flops | bytes accessed | tf_op | source)
XLA Modules:
  0.0 46.9 jit_solution(6092578630197447146)
XLA Ops:
  0.6 0.0 copy-start
  0.6 0.6 %collective-permute-start = (bf16[32,2048]{1,0:T(8,128)(2,1)}, bf16[32,2048]{1,0:T(8,128)(2,1)S(1)}, u32[]{:S(2)}, u32[]{:S(2)}) collective-permute-start(bf16[32,2048]{1,0:T(8,128)(2,1)} %own_hbm.3), channel_id=1, source_target_pairs={{0,1},{1,0},{2,3},{3,2},{4,5},{5,4},{6,7},{7,6},{8,9},{9,8},{10,11... | collective-permute-start | bytes 393224 | tf_op jit(solution)/shard_map/ppermute | solution.py:186
  1.2 1.2 %collective-permute-done.peer_ref = bf16[32,2048]{1,0:T(8,128)(2,1)S(1)} collective-permute-done((bf16[32,2048]{1,0:T(8,128)(2,1)}, bf16[32,2048]{1,0:T(8,128)(2,1)S(1)}, u32[]{:S(2)}, u32[]{:S(2)}) %collective-permute-start) | collective-permute-done | bytes 131104 | tf_op jit(solution)/shard_map/ppermute | solution.py:186
  2.4 5.5 %shard_map.59 = (f32[2,32,2048]{2,1,0:T(8,128)S(1)}, bf16[2,32,2048]{2,1,0:T(8,128)(2,1)S(1)}) custom-call(bf16[32,2048]{1,0:T(8,128)(2,1)} %own_hbm.3, bf16[32,2048]{1,0:T(8,128)(2,1)S(1)} %collective-permute-done.peer_ref, bf16[1024,8192]{1,0:T(8,128)(2,1)} %weight.3), custom_call_target="tpu_custom_call" | custom-call | tf_op jit(solution)/shard_map/pallas_call | solution.py:66
  8.0 0.4 collective-permute-start.1
  8.4 1.2 %collective-permute-done.1.got_ref = bf16[2,32,2048]{2,1,0:T(8,128)(2,1)S(1)} collective-permute-done((bf16[2,32,2048]{2,1,0:T(8,128)(2,1)S(1)}, bf16[2,32,2048]{2,1,0:T(8,128)(2,1)S(1)}, u32[]{:S(2)}, u32[]{:S(2)}) %collective-permute-start.1) | collective-permute-done | bytes 262176 | tf_op jit(solution)/shard_map/ppermute | solution.py:196
  9.6 5.5 %shard_map.60 = (f32[2,32,2048]{2,1,0:T(8,128)S(1)}, bf16[2,32,2048]{2,1,0:T(8,128)(2,1)S(1)}) custom-call(bf16[32,2048]{1,0:T(8,128)(2,1)} %own_hbm.3, bf16[32,2048]{1,0:T(8,128)(2,1)S(1)} %collective-permute-done.peer_ref, bf16[1024,8192]{1,0:T(8,128)(2,1)} %weight.3), custom_call_target="tpu_custom_call" | custom-call | tf_op jit(solution)/shard_map/pallas_call | solution.py:66
  15.1 0.4 collective-permute-start.2
  15.6 3.8 %collective-permute-start.4 = (bf16[528,128]{1,0:T(8,128)(2,1)S(1)}, bf16[528,128]{1,0:T(8,128)(2,1)S(1)}, u32[]{:S(2)}, u32[]{:S(2)}) collective-permute-start(bf16[528,128]{1,0:T(8,128)(2,1)S(1)} %get-tuple-element.18), channel_id=1, source_target_pairs={{0,8},{4,12},{8,0},{12,4},{1,9},{5,13},{9,1},{13,5},{2,10},{6,14},... | collective-permute-start | bytes 405512 | tf_op jit(solution)/shard_map/ppermute | solution.py:182
  19.4 1.3 %collective-permute-start.5 = (bf16[528,128]{1,0:T(8,128)(2,1)S(1)}, bf16[528,128]{1,0:T(8,128)(2,1)S(1)}, u32[]{:S(2)}, u32[]{:S(2)}) collective-permute-start(bf16[528,128]{1,0:T(8,128)(2,1)S(1)} %get-tuple-element.19), channel_id=1, source_target_pairs={{0,12},{4,8},{8,4},{12,0},{1,13},{5,9},{9,5},{13,1},{2,14},{6,10},... | collective-permute-start | bytes 405512 | tf_op jit(solution)/shard_map/ppermute | solution.py:182
  20.7 0.0 collective-permute-done.2.got_ref
  20.7 0.1 shard_map.61
  20.8 0.3 collective-permute-start.3
  21.1 8.6 %collective-permute-done.4.refs_1_.refs_6_ = bf16[528,128]{1,0:T(8,128)(2,1)S(1)} collective-permute-done((bf16[528,128]{1,0:T(8,128)(2,1)S(1)}, bf16[528,128]{1,0:T(8,128)(2,1)S(1)}, u32[]{:S(2)}, u32[]{:S(2)}) %collective-permute-start.4) | collective-permute-done | bytes 135200 | tf_op jit(solution)/shard_map/ppermute | solution.py:182
  29.7 0.0 collective-permute-done.5.refs_2_.refs_7_
  29.7 1.2 %collective-permute-done.3.refs_0_.refs_5_ = bf16[528,128]{1,0:T(8,128)(2,1)S(1)} collective-permute-done((bf16[528,128]{1,0:T(8,128)(2,1)S(1)}, bf16[528,128]{1,0:T(8,128)(2,1)S(1)}, u32[]{:S(2)}, u32[]{:S(2)}) %collective-permute-start.3) | collective-permute-done | bytes 135200 | tf_op jit(solution)/shard_map/ppermute | solution.py:182
  30.8 0.1 shard_map.63.refs_0_
  30.9 3.6 %collective-permute-start.8 = (bf16[512,128]{1,0:T(8,128)(2,1)S(1)}, bf16[512,128]{1,0:T(8,128)(2,1)S(1)}, u32[]{:S(2)}, u32[]{:S(2)}) collective-permute-start(bf16[512,128]{1,0:T(8,128)(2,1)S(1)} %shard_map.63.refs_0_), channel_id=1, source_target_pairs={{0,12},{4,8},{8,4},{12,0},{1,13},{5,9},{9,5},{13,1},{2,14},{6,10},... | collective-permute-start | bytes 393224 | tf_op jit(solution)/shard_map/ppermute | solution.py:182
  34.5 0.6 %collective-permute-start.7 = (bf16[512,128]{1,0:T(8,128)(2,1)S(1)}, bf16[512,128]{1,0:T(8,128)(2,1)S(1)}, u32[]{:S(2)}, u32[]{:S(2)}) collective-permute-start(bf16[512,128]{1,0:T(8,128)(2,1)S(1)} %shard_map.63.refs_0_), channel_id=1, source_target_pairs={{0,8},{4,12},{8,0},{12,4},{1,9},{5,13},{9,1},{13,5},{2,10},{6,14},... | collective-permute-start | bytes 393224 | tf_op jit(solution)/shard_map/ppermute | solution.py:182
  35.1 0.5 %collective-permute-start.6 = (bf16[512,128]{1,0:T(8,128)(2,1)S(1)}, bf16[512,128]{1,0:T(8,128)(2,1)S(1)}, u32[]{:S(2)}, u32[]{:S(2)}) collective-permute-start(bf16[512,128]{1,0:T(8,128)(2,1)S(1)} %shard_map.63.refs_0_), channel_id=1, source_target_pairs={{0,4},{4,0},{8,12},{12,8},{1,5},{5,1},{9,13},{13,9},{2,6},{6,2},{1... | collective-permute-start | bytes 393224 | tf_op jit(solution)/shard_map/ppermute | solution.py:182
  35.6 2.8 %collective-permute-done.8.refs_3_ = bf16[512,128]{1,0:T(8,128)(2,1)S(1)} collective-permute-done((bf16[512,128]{1,0:T(8,128)(2,1)S(1)}, bf16[512,128]{1,0:T(8,128)(2,1)S(1)}, u32[]{:S(2)}, u32[]{:S(2)}) %collective-permute-start.8) | collective-permute-done | bytes 131104 | tf_op jit(solution)/shard_map/ppermute | solution.py:182
  38.4 7.4 %collective-permute-done.7.refs_2_ = bf16[512,128]{1,0:T(8,128)(2,1)S(1)} collective-permute-done((bf16[512,128]{1,0:T(8,128)(2,1)S(1)}, bf16[512,128]{1,0:T(8,128)(2,1)S(1)}, u32[]{:S(2)}, u32[]{:S(2)}) %collective-permute-start.7) | collective-permute-done | bytes 131104 | tf_op jit(solution)/shard_map/ppermute | solution.py:182
  45.8 0.0 collective-permute-done.6.refs_1_
  45.8 1.1 %shard_map.64 = (bf16[32,2048]{1,0:T(8,128)(2,1)}, bf16[32,8192]{1,0:T(8,128)(2,1)}) custom-call(bf16[512,128]{1,0:T(8,128)(2,1)S(1)} %shard_map.63.refs_0_, bf16[512,128]{1,0:T(8,128)(2,1)S(1)} %collective-permute-done.6.refs_1_, bf16[512,128]{1,0:T(8,128)(2,1)S(1)} %collective-permute-done.7.refs_2_, bf16[512,128]{1,0:T(8,128)(2,1)S(1)} %collective-permute-done.8.refs_3_, ...), custom_call_target="tpu_custom_call" | custom-call | tf_op jit(solution)/shard_map/pallas_call | solution.py:165
  (4 shorter events, 0.1 us)
Async XLA Ops:
  0.6 14.9 %copy-start = (bf16[32,2048]{1,0:T(8,128)(2,1)S(1)}, bf16[32,2048]{1,0:T(8,128)(2,1)}, u32[]{:S(2)}) copy-start(bf16[32,2048]{1,0:T(8,128)(2,1)} %residual_ref.3) | copy-start | bytes 393220
  0.6 14.9 %copy-start.1 = (bf16[2048]{0:T(1024)(128)(2,1)S(1)}, bf16[2048]{0:T(1024)(128)(2,1)}, u32[]{:S(2)}) copy-start(bf16[2048]{0:T(1024)(128)(2,1)} %param.7) | copy-start | bytes 12292
  0.6 1.8 %collective-permute-start = (bf16[32,2048]{1,0:T(8,128)(2,1)}, bf16[32,2048]{1,0:T(8,128)(2,1)S(1)}, u32[]{:S(2)}, u32[]{:S(2)}) collective-permute-start(bf16[32,2048]{1,0:T(8,128)(2,1)} %own_hbm.3), channel_id=1, source_target_pairs={{0,1},{1,0},{2,3},{3,2},{4,5},{5,4},{6,7},{7,6},{8,9},{9,8},{10,11... | collective-permute-start | bytes 393224 | tf_op jit(solution)/shard_map/ppermute | solution.py:186
  8.0 1.6 %collective-permute-start.1 = (bf16[2,32,2048]{2,1,0:T(8,128)(2,1)S(1)}, bf16[2,32,2048]{2,1,0:T(8,128)(2,1)S(1)}, u32[]{:S(2)}, u32[]{:S(2)}) collective-permute-start(bf16[2,32,2048]{2,1,0:T(8,128)(2,1)S(1)} %get-tuple-element.11), channel_id=1, source_target_pairs={{0,1},{1,0},{2,3},{3,2},{4,5},{5,4},{6,7},{7,6},{8,9},{9,8},{10,11... | collective-permute-start | bytes 786440 | tf_op jit(solution)/shard_map/ppermute | solution.py:196
  15.1 5.6 %collective-permute-start.2 = (bf16[2,32,2048]{2,1,0:T(8,128)(2,1)S(1)}, bf16[2,32,2048]{2,1,0:T(8,128)(2,1)S(1)}, u32[]{:S(2)}, u32[]{:S(2)}) collective-permute-start(bf16[2,32,2048]{2,1,0:T(8,128)(2,1)S(1)} %get-tuple-element.14), channel_id=1, source_target_pairs={{0,1},{1,0},{2,3},{3,2},{4,5},{5,4},{6,7},{7,6},{8,9},{9,8},{10,11... | collective-permute-start | bytes 786440 | tf_op jit(solution)/shard_map/ppermute | solution.py:196
  15.6 14.1 %collective-permute-start.4 = (bf16[528,128]{1,0:T(8,128)(2,1)S(1)}, bf16[528,128]{1,0:T(8,128)(2,1)S(1)}, u32[]{:S(2)}, u32[]{:S(2)}) collective-permute-start(bf16[528,128]{1,0:T(8,128)(2,1)S(1)} %get-tuple-element.18), channel_id=1, source_target_pairs={{0,8},{4,12},{8,0},{12,4},{1,9},{5,13},{9,1},{13,5},{2,10},{6,14},... | collective-permute-start | bytes 405512 | tf_op jit(solution)/shard_map/ppermute | solution.py:182
  19.4 10.3 %collective-permute-start.5 = (bf16[528,128]{1,0:T(8,128)(2,1)S(1)}, bf16[528,128]{1,0:T(8,128)(2,1)S(1)}, u32[]{:S(2)}, u32[]{:S(2)}) collective-permute-start(bf16[528,128]{1,0:T(8,128)(2,1)S(1)} %get-tuple-element.19), channel_id=1, source_target_pairs={{0,12},{4,8},{8,4},{12,0},{1,13},{5,9},{9,5},{13,1},{2,14},{6,10},... | collective-permute-start | bytes 405512 | tf_op jit(solution)/shard_map/ppermute | solution.py:182
  20.8 10.0 %collective-permute-start.3 = (bf16[528,128]{1,0:T(8,128)(2,1)S(1)}, bf16[528,128]{1,0:T(8,128)(2,1)S(1)}, u32[]{:S(2)}, u32[]{:S(2)}) collective-permute-start(bf16[528,128]{1,0:T(8,128)(2,1)S(1)} %get-tuple-element.16), channel_id=1, source_target_pairs={{0,4},{4,0},{8,12},{12,8},{1,5},{5,1},{9,13},{13,9},{2,6},{6,2},{1... | collective-permute-start | bytes 405512 | tf_op jit(solution)/shard_map/ppermute | solution.py:182
  30.9 7.5 %collective-permute-start.8 = (bf16[512,128]{1,0:T(8,128)(2,1)S(1)}, bf16[512,128]{1,0:T(8,128)(2,1)S(1)}, u32[]{:S(2)}, u32[]{:S(2)}) collective-permute-start(bf16[512,128]{1,0:T(8,128)(2,1)S(1)} %shard_map.63.refs_0_), channel_id=1, source_target_pairs={{0,12},{4,8},{8,4},{12,0},{1,13},{5,9},{9,5},{13,1},{2,14},{6,10},... | collective-permute-start | bytes 393224 | tf_op jit(solution)/shard_map/ppermute | solution.py:182
  34.5 11.3 %collective-permute-start.7 = (bf16[512,128]{1,0:T(8,128)(2,1)S(1)}, bf16[512,128]{1,0:T(8,128)(2,1)S(1)}, u32[]{:S(2)}, u32[]{:S(2)}) collective-permute-start(bf16[512,128]{1,0:T(8,128)(2,1)S(1)} %shard_map.63.refs_0_), channel_id=1, source_target_pairs={{0,8},{4,12},{8,0},{12,4},{1,9},{5,13},{9,1},{13,5},{2,10},{6,14},... | collective-permute-start | bytes 393224 | tf_op jit(solution)/shard_map/ppermute | solution.py:182
  35.1 10.7 %collective-permute-start.6 = (bf16[512,128]{1,0:T(8,128)(2,1)S(1)}, bf16[512,128]{1,0:T(8,128)(2,1)S(1)}, u32[]{:S(2)}, u32[]{:S(2)}) collective-permute-start(bf16[512,128]{1,0:T(8,128)(2,1)S(1)} %shard_map.63.refs_0_), channel_id=1, source_target_pairs={{0,4},{4,0},{8,12},{12,8},{1,5},{5,1},{9,13},{13,9},{2,6},{6,2},{1... | collective-permute-start | bytes 393224 | tf_op jit(solution)/shard_map/ppermute | solution.py:182

commit v3 on v2

--- a/solution.py
+++ b/solution.py
@@ -13,6 +13,7 @@
 F32, BF16 = jnp.float32, jnp.bfloat16
 LANES = 128
 SPLITS = 1
+READY = 2
 
 
 def call(kernel, in_specs, out_shape, limit, scratch=()):
@@ -26,62 +27,114 @@
     )
 
 
-def project_kernel(tensor, chunk, steps, own_hbm, peer_ref, weight, keep_ref, give_ref, own_ref, held, own_sem, sems):
+def chunk_copies(tensor, chunk, steps, weight):
+    block = weight.shape[1] // tensor
+    rank = lax.axis_index("tensor")
+    copies = []
+    for step in steps:
+        for piece in range(block // chunk):
+            start = pl.multiple_of((rank ^ step) * block + piece * chunk, LANES)
+            copies.append(functools.partial(pltpu.make_async_copy, weight.at[:, pl.ds(start, chunk)]))
+    return copies
+
+
+def prefetch_kernel(tensor, chunk, steps, own_hbm, weight, own_ref, ready_ref, own_sem, sems):
+    depth = weight.shape[0]
+    features = pl.ds(pl.multiple_of(lax.axis_index("seq") * depth, LANES), depth)
+    own_copy = pltpu.make_async_copy(own_hbm.at[:, features], own_ref, own_sem)
+    own_copy.start()
+    copies = chunk_copies(tensor, chunk, steps, weight)[: ready_ref.shape[0]]
+    copies = [copy(ready_ref.at[i], sems.at[i]) for i, copy in enumerate(copies)]
+    for copy in copies:
+        copy.start()
+    for copy in copies:
+        copy.wait()
+    own_copy.wait()
+
+
+def refill_kernel(tensor, chunk, steps, _, weight, ready_ref, sems):
+    copies = chunk_copies(tensor, chunk, steps, weight)[: ready_ref.shape[0]]
+    copies = [copy(ready_ref.at[i], sems.at[i]) for i, copy in enumerate(copies)]
+    for copy in copies:
+        copy.start()
+    for copy in copies:
+        copy.wait()
+
+
+def project_kernel(tensor, chunk, steps, own_ref, peer_ref, ready_ref, weight, keep_ref, give_ref, held, sems):
     depth, width = weight.shape
     block = width // tensor
     per_block = block // chunk
-    rank = lax.axis_index("tensor")
+    early = ready_ref.shape[0]
+    copies = chunk_copies(tensor, chunk, steps, weight)[early:]
+    copies = [copy(held.at[i], sems.at[i]) for i, copy in enumerate(copies)]
+    for copy in copies:
+        copy.start()
     features = pl.ds(pl.multiple_of(lax.axis_index("seq") * depth, LANES), depth)
-    own_copy = pltpu.make_async_copy(own_hbm.at[:, features], own_ref, own_sem)
-    own_copy.start()
-
-    def copy(index):
-        place, piece = divmod(index, per_block)
-        start = (rank ^ steps[place]) * block + piece * chunk
-        return pltpu.make_async_copy(
-            weight.at[:, pl.ds(pl.multiple_of(start, LANES), chunk)], held.at[index], sems.at[index]
-        )
-
-    count = len(steps) * per_block
-    for index in range(count):
-        copy(index).start()
-    own_copy.wait()
     rows = own_ref.shape[0]
     operand = jnp.concatenate([own_ref[...], peer_ref[:, features]], axis=0)
-    for index in range(count):
+    for index in range(len(steps) * per_block):
         place, piece = divmod(index, per_block)
-        copy(index).wait()
-        product = jnp.dot(operand, held[index], preferred_element_type=F32)
+        if index < early:
+            right = ready_ref[index]
+        else:
+            copies[index - early].wait()
+            right = held[index - early]
+        product = jnp.dot(operand, right, preferred_element_type=F32)
         columns = pl.ds(piece * chunk, chunk)
         keep_ref[place, :, columns] = product[:rows]
         give_ref[place, :, columns] = product[rows:].astype(BF16)
 
 
-def project(own, peer, weight, tensor, steps):
+def chunk_of(weight, tensor):
+    block = weight.shape[1] // tensor
+    chunk = min(block, 512)
+    return chunk, min(READY * MIB // (2 * weight.shape[0] * chunk), block // chunk)
+
+
+def prefetch(own, weight, tensor, steps):
+    rows, depth = own.shape[0], weight.shape[0]
+    chunk, early = chunk_of(weight, tensor)
+    return call(
+        functools.partial(prefetch_kernel, tensor, chunk, steps),
+        [HBM, HBM],
+        [
+            jax.ShapeDtypeStruct((rows, depth), BF16),
+            jax.ShapeDtypeStruct((early, depth, chunk), BF16),
+        ],
+        2 * depth * chunk * early + 2 * MIB,
+        [pltpu.SemaphoreType.DMA(()), pltpu.SemaphoreType.DMA((early,))],
+    )(pltpu.with_memory_space_constraint(own, HBM), pltpu.with_memory_space_constraint(weight, HBM))
+
+
+def refill(after, weight, tensor, steps):
+    depth = weight.shape[0]
+    chunk, early = chunk_of(weight, tensor)
+    return call(
+        functools.partial(refill_kernel, tensor, chunk, steps),
+        [VMEM, HBM],
+        [jax.ShapeDtypeStruct((early, depth, chunk), BF16)],
+        2 * depth * chunk * early + 2 * MIB,
+        [pltpu.SemaphoreType.DMA((early,))],
+    )(after, pltpu.with_memory_space_constraint(weight, HBM))[0]
+
+
+def project(own, peer, ready, weight, tensor, steps):
     rows = own.shape[0]
     depth, width = weight.shape
     block = width // tensor
-    chunk = min(block, 512)
-    count = len(steps) * block // chunk
+    chunk, early = chunk_of(weight, tensor)
+    count = len(steps) * block // chunk - early
     return call(
         functools.partial(project_kernel, tensor, chunk, steps),
-        [HBM, VMEM, HBM],
+        [VMEM, VMEM, VMEM, HBM],
         [
             jax.ShapeDtypeStruct((len(steps), rows, block), F32),
             jax.ShapeDtypeStruct((len(steps), rows, block), BF16),
         ],
-        2 * depth * chunk * count + 4 * MIB,
-        [
-            VMEM((rows, depth), BF16),
-            VMEM((count, depth, chunk), BF16),
-            pltpu.SemaphoreType.DMA(()),
-            pltpu.SemaphoreType.DMA((count,)),
-        ],
-    )(
-        pltpu.with_memory_space_constraint(own, HBM),
-        peer,
-        pltpu.with_memory_space_constraint(weight, HBM),
-    )
+        2 * depth * chunk * (count + early) + 4 * MIB,
+        [VMEM((count, depth, chunk), BF16), pltpu.SemaphoreType.DMA((count,))],
+    )(own, peer, ready, pltpu.with_memory_space_constraint(weight, HBM))
 
 
 def pair_kernel(steps, keep_ref, got_ref, residual_ref, gain_ref, *out_refs):
@@ -110,9 +163,7 @@
         for split in range(SPLITS):
             extra = gain.shape[0] if step and not split else 0
             shapes.append(jax.ShapeDtypeStruct((length + extra, LANES), BF16 if step else F32))
-    outs = call(functools.partial(pair_kernel, steps), [VMEM] * 4, shapes, 6 * MIB)(
-        keep, got, residual, gain
-    )
+    outs = call(functools.partial(pair_kernel, steps), [VMEM] * 4, shapes, 6 * MIB)(keep, got, residual, gain)
     return {step: outs[i * SPLITS : (i + 1) * SPLITS] for i, step in enumerate(steps)}
 
 
@@ -183,17 +234,19 @@
 
     gain = norm_gain.reshape(-1, LANES)
     gain = jnp.pad(gain, ((0, -gain.shape[0] % 16), (0, 0)))
-    peer = lax.ppermute(attn_heads, "seq", swap)
     order = list(range(tensor // 2, tensor)) + list(range(1, tensor // 2)) + [0]
     waves = [order[: tensor // 2], order[tensor // 2 :]]
-    got = None
+    peer = lax.ppermute(attn_heads, "seq", swap)
+    own, ready = prefetch(attn_heads, out_weight, tensor, waves[0])
     sums = {}
     arrived = {}
-    for steps in waves:
-        if got is not None:
+    for wave, steps in enumerate(waves):
+        keep, give = project(own, peer, ready, out_weight, tensor, steps)
+        got = lax.ppermute(give, "seq", swap)
+        if wave == 0:
+            own, _ = lax.optimization_barrier((own, give))
+            ready = refill(own, out_weight, tensor, waves[1])
             peer, _ = lax.optimization_barrier((peer, got))
-        keep, give = project(attn_heads, peer, out_weight, tensor, steps)
-        got = lax.ppermute(give, "seq", swap)
         sums.update(pair_sum(steps, keep, got, residual, gain))
         for step in steps:
             if step:

time: 47 us -> 43.7 us (0.930)
  waiting for transfers between devices: 22.3 us -> 20 us
  Pallas kernels: 12.4 us -> 11.6 us
    ppermute x1, waiting for transfers between devices: 1.2 us -> 0.01 us  [on_device(): peer = lax.ppermute(attn_heads, 'seq', swap)]
    ppermute x2, waiting for transfers between devices: 1.18 us -> 0.01 us  [on_device(): got = lax.ppermute(give, 'seq', swap)]
    pallas_call x2 -> x4, Pallas kernels: 11.1 us -> 10.2 us  [the longest x2 7.08 us: project(): call(functools.partial(project_kernel, tensor, chunk, steps), [VMEM, VMEM...]
  transfers between devices with their start and end apart: 9 -> 9, of which waited for: 6 -> 4; matrix products, arithmetic and copies ran while one was open for 0% -> 0% of each run, Pallas kernels for 0% -> 8%
where the time goes in v3:
time: 43.7 us; the launch traced here: 43.5 us
  waiting for transfers between devices  20 us (46%)
  Pallas kernels  11.6 us (27%)
  starting transfers between devices  11.2 us (26%)
  between operations  0.71 us (2%)
    ppermute x6, waiting for transfers between devices, exchange(): return lax.ppermute(value, 'tensor', [(i, i ^ step) for i in range(tensor)])  20 us
    ppermute x6, starting transfers between devices, exchange(): return lax.ppermute(value, 'tensor', [(i, i ^ step) for i in range(tensor)])  10 us
    pallas_call x2, Pallas kernels, project(): call(functools.partial(project_kernel, tensor, chunk, steps), [VMEM, VMEM...  7.08 us
    pallas_call x1, Pallas kernels, prefetch(): call(functools.partial(prefetch_kernel, tensor, chunk, steps), [HBM, HBM]...  1.59 us
    pallas_call x1, Pallas kernels, refill(): call(functools.partial(refill_kernel, tensor, chunk, steps), [VMEM, HBM],...  1.57 us
    pallas_call x1, Pallas kernels, normalize(): call(functools.partial(norm_kernel, tensor, rows, block), [VMEM] * (tenso...  1.12 us
  transfers between devices with their start and end apart: 9, of which 4 were waited for; matrix products, arithmetic and copies ran while one was open for 0% of the time, Pallas kernels for 8%

profile of v3, /device:TPU:0, one launch (start us, length us, event | category | flops | bytes accessed | tf_op | source)
XLA Modules:
  0.0 43.5 jit_solution(12328094564796550942)
XLA Ops:
  0.6 0.6 %collective-permute-start = (bf16[32,2048]{1,0:T(8,128)(2,1)}, bf16[32,2048]{1,0:T(8,128)(2,1)S(1)}, u32[]{:S(2)}, u32[]{:S(2)}) collective-permute-start(bf16[32,2048]{1,0:T(8,128)(2,1)} %own_hbm.1), channel_id=1, source_target_pairs={{0,1},{1,0},{2,3},{3,2},{4,5},{5,4},{6,7},{7,6},{8,9},{9,8},{10,11... | collective-permute-start | bytes 393224 | tf_op jit(solution)/shard_map/ppermute | solution.py:239
  1.2 1.6 %shard_map.59 = (bf16[32,1024]{1,0:T(8,128)(2,1)S(1)}, bf16[2,1024,512]{2,1,0:T(8,128)(2,1)S(1)}) custom-call(bf16[32,2048]{1,0:T(8,128)(2,1)} %own_hbm.1, bf16[1024,8192]{1,0:T(8,128)(2,1)} %weight.7), custom_call_target="tpu_custom_call" | custom-call | tf_op jit(solution)/shard_map/pallas_call | solution.py:98
  2.8 3.5 %shard_map.60 = (f32[2,32,2048]{2,1,0:T(8,128)S(1)}, bf16[2,32,2048]{2,1,0:T(8,128)(2,1)S(1)}) custom-call(bf16[32,1024]{1,0:T(8,128)(2,1)S(1)} %get-tuple-element.17.own_ref._, bf16[32,2048]{1,0:T(8,128)(2,1)S(1)} %collective-permute-done.peer_ref, bf16[2,1024,512]{2,1,0:T(8,128)(2,1)S(1)} %get-tuple-element.15.ready_ref, bf16[1024,8192]{1,0:T(8,128)(2,1)} %weight.7), custom_call_target="tpu_custom_call" | custom-call | tf_op jit(solution)/shard_map/pallas_call | solution.py:128
  6.3 0.1 collective-permute-start.1
  6.4 1.6 %shard_map.61.ready_ref = bf16[2,1024,512]{2,1,0:T(8,128)(2,1)S(1)} custom-call(bf16[32,1024]{1,0:T(8,128)(2,1)S(1)} %get-tuple-element.17.own_ref._, bf16[1024,8192]{1,0:T(8,128)(2,1)} %weight.7), custom_call_target="tpu_custom_call" | custom-call | tf_op jit(solution)/shard_map/pallas_call | solution.py:113
  8.0 0.0 copy-start
  8.0 0.0 copy-start.1
  8.0 0.0 collective-permute-done.1.got_ref
  8.0 3.5 %shard_map.62 = (f32[2,32,2048]{2,1,0:T(8,128)S(1)}, bf16[2,32,2048]{2,1,0:T(8,128)(2,1)S(1)}) custom-call(bf16[32,1024]{1,0:T(8,128)(2,1)S(1)} %get-tuple-element.17.own_ref._, bf16[32,2048]{1,0:T(8,128)(2,1)S(1)} %collective-permute-done.peer_ref, bf16[2,1024,512]{2,1,0:T(8,128)(2,1)S(1)} %shard_map.61.ready_ref, bf16[1024,8192]{1,0:T(8,128)(2,1)} %weight.7), custom_call_target="tpu_custom_call" | custom-call | tf_op jit(solution)/shard_map/pallas_call | solution.py:128
  11.6 0.5 %collective-permute-start.2 = (bf16[2,32,2048]{2,1,0:T(8,128)(2,1)S(1)}, bf16[2,32,2048]{2,1,0:T(8,128)(2,1)S(1)}, u32[]{:S(2)}, u32[]{:S(2)}) collective-permute-start(bf16[2,32,2048]{2,1,0:T(8,128)(2,1)S(1)} %get-tuple-element.20), channel_id=1, source_target_pairs={{0,1},{1,0},{2,3},{3,2},{4,5},{5,4},{6,7},{7,6},{8,9},{9,8},{10,11... | collective-permute-start | bytes 786440 | tf_op jit(solution)/shard_map/ppermute | solution.py:245
  12.2 3.7 %collective-permute-start.4 = (bf16[528,128]{1,0:T(8,128)(2,1)S(1)}, bf16[528,128]{1,0:T(8,128)(2,1)S(1)}, u32[]{:S(2)}, u32[]{:S(2)}) collective-permute-start(bf16[528,128]{1,0:T(8,128)(2,1)S(1)} %get-tuple-element.24), channel_id=1, source_target_pairs={{0,8},{4,12},{8,0},{12,4},{1,9},{5,13},{9,1},{13,5},{2,10},{6,14},... | collective-permute-start | bytes 405512 | tf_op jit(solution)/shard_map/ppermute | solution.py:233
  15.9 1.3 %collective-permute-start.5 = (bf16[528,128]{1,0:T(8,128)(2,1)S(1)}, bf16[528,128]{1,0:T(8,128)(2,1)S(1)}, u32[]{:S(2)}, u32[]{:S(2)}) collective-permute-start(bf16[528,128]{1,0:T(8,128)(2,1)S(1)} %get-tuple-element.25), channel_id=1, source_target_pairs={{0,12},{4,8},{8,4},{12,0},{1,13},{5,9},{9,5},{13,1},{2,14},{6,10},... | collective-permute-start | bytes 405512 | tf_op jit(solution)/shard_map/ppermute | solution.py:233
  17.2 0.1 shard_map.63
  17.3 0.3 collective-permute-start.3
  17.6 8.5 %collective-permute-done.4.refs_1_.refs_6_ = bf16[528,128]{1,0:T(8,128)(2,1)S(1)} collective-permute-done((bf16[528,128]{1,0:T(8,128)(2,1)S(1)}, bf16[528,128]{1,0:T(8,128)(2,1)S(1)}, u32[]{:S(2)}, u32[]{:S(2)}) %collective-permute-start.4) | collective-permute-done | bytes 135200 | tf_op jit(solution)/shard_map/ppermute | solution.py:233
  26.1 1.3 %collective-permute-done.3.refs_0_.refs_5_ = bf16[528,128]{1,0:T(8,128)(2,1)S(1)} collective-permute-done((bf16[528,128]{1,0:T(8,128)(2,1)S(1)}, bf16[528,128]{1,0:T(8,128)(2,1)S(1)}, u32[]{:S(2)}, u32[]{:S(2)}) %collective-permute-start.3) | collective-permute-done | bytes 135200 | tf_op jit(solution)/shard_map/ppermute | solution.py:233
  27.4 0.1 shard_map.65.refs_0_
  27.5 3.6 %collective-permute-start.8 = (bf16[512,128]{1,0:T(8,128)(2,1)S(1)}, bf16[512,128]{1,0:T(8,128)(2,1)S(1)}, u32[]{:S(2)}, u32[]{:S(2)}) collective-permute-start(bf16[512,128]{1,0:T(8,128)(2,1)S(1)} %shard_map.65.refs_0_), channel_id=1, source_target_pairs={{0,12},{4,8},{8,4},{12,0},{1,13},{5,9},{9,5},{13,1},{2,14},{6,10},... | collective-permute-start | bytes 393224 | tf_op jit(solution)/shard_map/ppermute | solution.py:233
  31.1 0.6 %collective-permute-start.7 = (bf16[512,128]{1,0:T(8,128)(2,1)S(1)}, bf16[512,128]{1,0:T(8,128)(2,1)S(1)}, u32[]{:S(2)}, u32[]{:S(2)}) collective-permute-start(bf16[512,128]{1,0:T(8,128)(2,1)S(1)} %shard_map.65.refs_0_), channel_id=1, source_target_pairs={{0,8},{4,12},{8,0},{12,4},{1,9},{5,13},{9,1},{13,5},{2,10},{6,14},... | collective-permute-start | bytes 393224 | tf_op jit(solution)/shard_map/ppermute | solution.py:233
  31.7 0.5 %collective-permute-start.6 = (bf16[512,128]{1,0:T(8,128)(2,1)S(1)}, bf16[512,128]{1,0:T(8,128)(2,1)S(1)}, u32[]{:S(2)}, u32[]{:S(2)}) collective-permute-start(bf16[512,128]{1,0:T(8,128)(2,1)S(1)} %shard_map.65.refs_0_), channel_id=1, source_target_pairs={{0,4},{4,0},{8,12},{12,8},{1,5},{5,1},{9,13},{13,9},{2,6},{6,2},{1... | collective-permute-start | bytes 393224 | tf_op jit(solution)/shard_map/ppermute | solution.py:233
  32.2 2.8 %collective-permute-done.8.refs_3_ = bf16[512,128]{1,0:T(8,128)(2,1)S(1)} collective-permute-done((bf16[512,128]{1,0:T(8,128)(2,1)S(1)}, bf16[512,128]{1,0:T(8,128)(2,1)S(1)}, u32[]{:S(2)}, u32[]{:S(2)}) %collective-permute-start.8) | collective-permute-done | bytes 131104 | tf_op jit(solution)/shard_map/ppermute | solution.py:233
  35.0 7.4 %collective-permute-done.7.refs_2_ = bf16[512,128]{1,0:T(8,128)(2,1)S(1)} collective-permute-done((bf16[512,128]{1,0:T(8,128)(2,1)S(1)}, bf16[512,128]{1,0:T(8,128)(2,1)S(1)}, u32[]{:S(2)}, u32[]{:S(2)}) %collective-permute-start.7) | collective-permute-done | bytes 131104 | tf_op jit(solution)/shard_map/ppermute | solution.py:233
  42.4 0.0 collective-permute-done.6.refs_1_
  42.4 1.1 %shard_map.66 = (bf16[32,2048]{1,0:T(8,128)(2,1)}, bf16[32,8192]{1,0:T(8,128)(2,1)}) custom-call(bf16[512,128]{1,0:T(8,128)(2,1)S(1)} %shard_map.65.refs_0_, bf16[512,128]{1,0:T(8,128)(2,1)S(1)} %collective-permute-done.6.refs_1_, bf16[512,128]{1,0:T(8,128)(2,1)S(1)} %collective-permute-done.7.refs_2_, bf16[512,128]{1,0:T(8,128)(2,1)S(1)} %collective-permute-done.8.refs_3_, ...), custom_call_target="tpu_custom_call" | custom-call | tf_op jit(solution)/shard_map/pallas_call | solution.py:216
  (6 shorter events, 0.1 us)
Async XLA Ops:
  0.6 2.2 %collective-permute-start = (bf16[32,2048]{1,0:T(8,128)(2,1)}, bf16[32,2048]{1,0:T(8,128)(2,1)S(1)}, u32[]{:S(2)}, u32[]{:S(2)}) collective-permute-start(bf16[32,2048]{1,0:T(8,128)(2,1)} %own_hbm.1), channel_id=1, source_target_pairs={{0,1},{1,0},{2,3},{3,2},{4,5},{5,4},{6,7},{7,6},{8,9},{9,8},{10,11... | collective-permute-start | bytes 393224 | tf_op jit(solution)/shard_map/ppermute | solution.py:239
  6.3 1.7 %collective-permute-start.1 = (bf16[2,32,2048]{2,1,0:T(8,128)(2,1)S(1)}, bf16[2,32,2048]{2,1,0:T(8,128)(2,1)S(1)}, u32[]{:S(2)}, u32[]{:S(2)}) collective-permute-start(bf16[2,32,2048]{2,1,0:T(8,128)(2,1)S(1)} %get-tuple-element.16), channel_id=1, source_target_pairs={{0,1},{1,0},{2,3},{3,2},{4,5},{5,4},{6,7},{7,6},{8,9},{9,8},{10,11... | collective-permute-start | bytes 786440 | tf_op jit(solution)/shard_map/ppermute | solution.py:245
  8.0 4.1 %copy-start = (bf16[32,2048]{1,0:T(8,128)(2,1)S(1)}, bf16[32,2048]{1,0:T(8,128)(2,1)}, u32[]{:S(2)}) copy-start(bf16[32,2048]{1,0:T(8,128)(2,1)} %residual_ref.3) | copy-start | bytes 393220
  8.0 4.1 %copy-start.1 = (bf16[2048]{0:T(1024)(128)(2,1)S(1)}, bf16[2048]{0:T(1024)(128)(2,1)}, u32[]{:S(2)}) copy-start(bf16[2048]{0:T(1024)(128)(2,1)} %param.7) | copy-start | bytes 12292
  11.6 5.6 %collective-permute-start.2 = (bf16[2,32,2048]{2,1,0:T(8,128)(2,1)S(1)}, bf16[2,32,2048]{2,1,0:T(8,128)(2,1)S(1)}, u32[]{:S(2)}, u32[]{:S(2)}) collective-permute-start(bf16[2,32,2048]{2,1,0:T(8,128)(2,1)S(1)} %get-tuple-element.20), channel_id=1, source_target_pairs={{0,1},{1,0},{2,3},{3,2},{4,5},{5,4},{6,7},{7,6},{8,9},{9,8},{10,11... | collective-permute-start | bytes 786440 | tf_op jit(solution)/shard_map/ppermute | solution.py:245
  12.2 13.9 %collective-permute-start.4 = (bf16[528,128]{1,0:T(8,128)(2,1)S(1)}, bf16[528,128]{1,0:T(8,128)(2,1)S(1)}, u32[]{:S(2)}, u32[]{:S(2)}) collective-permute-start(bf16[528,128]{1,0:T(8,128)(2,1)S(1)} %get-tuple-element.24), channel_id=1, source_target_pairs={{0,8},{4,12},{8,0},{12,4},{1,9},{5,13},{9,1},{13,5},{2,10},{6,14},... | collective-permute-start | bytes 405512 | tf_op jit(solution)/shard_map/ppermute | solution.py:233
  15.9 10.3 %collective-permute-start.5 = (bf16[528,128]{1,0:T(8,128)(2,1)S(1)}, bf16[528,128]{1,0:T(8,128)(2,1)S(1)}, u32[]{:S(2)}, u32[]{:S(2)}) collective-permute-start(bf16[528,128]{1,0:T(8,128)(2,1)S(1)} %get-tuple-element.25), channel_id=1, source_target_pairs={{0,12},{4,8},{8,4},{12,0},{1,13},{5,9},{9,5},{13,1},{2,14},{6,10},... | collective-permute-start | bytes 405512 | tf_op jit(solution)/shard_map/ppermute | solution.py:233
  17.3 10.1 %collective-permute-start.3 = (bf16[528,128]{1,0:T(8,128)(2,1)S(1)}, bf16[528,128]{1,0:T(8,128)(2,1)S(1)}, u32[]{:S(2)}, u32[]{:S(2)}) collective-permute-start(bf16[528,128]{1,0:T(8,128)(2,1)S(1)} %get-tuple-element.22), channel_id=1, source_target_pairs={{0,4},{4,0},{8,12},{12,8},{1,5},{5,1},{9,13},{13,9},{2,6},{6,2},{1... | collective-permute-start | bytes 405512 | tf_op jit(solution)/shard_map/ppermute | solution.py:233
  27.5 7.5 %collective-permute-start.8 = (bf16[512,128]{1,0:T(8,128)(2,1)S(1)}, bf16[512,128]{1,0:T(8,128)(2,1)S(1)}, u32[]{:S(2)}, u32[]{:S(2)}) collective-permute-start(bf16[512,128]{1,0:T(8,128)(2,1)S(1)} %shard_map.65.refs_0_), channel_id=1, source_target_pairs={{0,12},{4,8},{8,4},{12,0},{1,13},{5,9},{9,5},{13,1},{2,14},{6,10},... | collective-permute-start | bytes 393224 | tf_op jit(solution)/shard_map/ppermute | solution.py:233
  31.1 11.3 %collective-permute-start.7 = (bf16[512,128]{1,0:T(8,128)(2,1)S(1)}, bf16[512,128]{1,0:T(8,128)(2,1)S(1)}, u32[]{:S(2)}, u32[]{:S(2)}) collective-permute-start(bf16[512,128]{1,0:T(8,128)(2,1)S(1)} %shard_map.65.refs_0_), channel_id=1, source_target_pairs={{0,8},{4,12},{8,0},{12,4},{1,9},{5,13},{9,1},{13,5},{2,10},{6,14},... | collective-permute-start | bytes 393224 | tf_op jit(solution)/shard_map/ppermute | solution.py:233
  31.7 10.7 %collective-permute-start.6 = (bf16[512,128]{1,0:T(8,128)(2,1)S(1)}, bf16[512,128]{1,0:T(8,128)(2,1)S(1)}, u32[]{:S(2)}, u32[]{:S(2)}) collective-permute-start(bf16[512,128]{1,0:T(8,128)(2,1)S(1)} %shard_map.65.refs_0_), channel_id=1, source_target_pairs={{0,4},{4,0},{8,12},{12,8},{1,5},{5,1},{9,13},{13,9},{2,6},{6,2},{1... | collective-permute-start | bytes 393224 | tf_op jit(solution)/shard_map/ppermute | solution.py:233

commit v4 on v3

--- a/solution.py
+++ b/solution.py
@@ -12,8 +12,8 @@
 MIB = 1024 * 1024
 F32, BF16 = jnp.float32, jnp.bfloat16
 LANES = 128
-SPLITS = 1
 READY = 2
+CHUNK = 512
 
 
 def call(kernel, in_specs, out_shape, limit, scratch=()):
@@ -88,7 +88,7 @@
 
 def chunk_of(weight, tensor):
     block = weight.shape[1] // tensor
-    chunk = min(block, 512)
+    chunk = min(block, CHUNK)
     return chunk, min(READY * MIB // (2 * weight.shape[0] * chunk), block // chunk)
 
 
@@ -139,89 +139,95 @@
 
 def pair_kernel(steps, keep_ref, got_ref, residual_ref, gain_ref, *out_refs):
     _, rows, block = keep_ref.shape
-    part = rows // SPLITS
-    targets = iter(out_refs)
     for place, step in enumerate(steps):
-        for split in range(SPLITS):
-            target = next(targets)
-            span = slice(split * part, (split + 1) * part)
-            for tile in range(block // LANES):
-                columns = slice(tile * LANES, (tile + 1) * LANES)
-                value = keep_ref[place, span, columns] + got_ref[place, span, columns].astype(F32)
-                if step == 0:
-                    value = value + residual_ref[span, columns].astype(F32)
-                target[tile * part : (tile + 1) * part, :] = value.astype(target.dtype)
-            if step and not split:
-                target[block // LANES * part :, :] = gain_ref[...]
+        target = out_refs[place]
+        for tile in range(block // LANES):
+            columns = slice(tile * LANES, (tile + 1) * LANES)
+            value = keep_ref[place, :, columns] + got_ref[place, :, columns].astype(F32)
+            if step == 0:
+                value = value + residual_ref[:, columns].astype(F32)
+            target[tile * rows : (tile + 1) * rows, :] = value.astype(target.dtype)
+        if step:
+            target[block // LANES * rows :, :] = gain_ref[...]
 
 
 def pair_sum(steps, keep, got, residual, gain):
     _, rows, block = keep.shape
-    length = rows // SPLITS * block // LANES
-    shapes = []
-    for step in steps:
-        for split in range(SPLITS):
-            extra = gain.shape[0] if step and not split else 0
-            shapes.append(jax.ShapeDtypeStruct((length + extra, LANES), BF16 if step else F32))
-    outs = call(functools.partial(pair_kernel, steps), [VMEM] * 4, shapes, 6 * MIB)(keep, got, residual, gain)
-    return {step: outs[i * SPLITS : (i + 1) * SPLITS] for i, step in enumerate(steps)}
-
-
-def stream_kernel(base_ref, *refs):
+    length = rows * block // LANES
+    shapes = [
+        jax.ShapeDtypeStruct((length + gain.shape[0], LANES), BF16)
+        if step
+        else jax.ShapeDtypeStruct((length, LANES), F32)
+        for step in steps
+    ]
+    outs = call(functools.partial(pair_kernel, steps), [VMEM] * 4, shapes, 6 * MIB)(
+        keep, got, residual, gain
+    )
+    return dict(zip(steps, outs))
+
+
+def stream_kernel(count, base_ref, *refs):
     length = base_ref.shape[0]
     total = base_ref[...]
-    for ref in refs[:-1]:
+    for ref in refs[:count]:
         total = total + ref[:length, :].astype(F32)
-    refs[-1][...] = total.astype(BF16)
-
-
-def finish_stream(base, parts):
-    return call(
-        stream_kernel, [VMEM] * (1 + len(parts)), [jax.ShapeDtypeStruct(base.shape, BF16)], 4 * MIB
-    )(base, *parts)[0]
-
-
-def norm_kernel(tensor, rows, block, *refs):
-    pieces, refs = refs[: tensor * SPLITS], refs[tensor * SPLITS :]
+    stream = total.astype(BF16)
+    refs[count][...] = stream
+    for half, ref in enumerate(refs[count + 1 :]):
+        ref[...] = stream[half * length // 2 : (half + 1) * length // 2]
+
+
+def finish_stream(base, parts, halves):
+    length = base.shape[0]
+    shapes = [jax.ShapeDtypeStruct(base.shape, BF16)]
+    if halves:
+        shapes += [jax.ShapeDtypeStruct((length // 2, LANES), BF16)] * 2
+    return call(
+        functools.partial(stream_kernel, len(parts)), [VMEM] * (1 + len(parts)), shapes, 4 * MIB
+    )(base, *parts)
+
+
+def norm_kernel(rows, block, counts, *refs):
+    tensor = len(counts)
+    tiles = block // LANES
+    refs = list(refs)
+    pieces = []
+    for count in counts:
+        group = [refs.pop(0) for _ in range(count)]
+        size = tiles // count
+        pieces.append([(group[tile // size], tile % size) for tile in range(tiles)])
     gains, (stream_ref, out_ref) = refs[:tensor], refs[tensor:]
-    part = rows // SPLITS
-    tiles = block // LANES
     rank = lax.axis_index("tensor")
-    starts = [(rank ^ step) * block for step in range(tensor)]
-    gain_rows = []
-    for step, ref in enumerate(gains):
-        first = tiles * part if step else 0
-        gain_rows.append(ref[first:, :].astype(F32))
-    for split in range(SPLITS):
-        span = slice(split * part, (split + 1) * part)
-        total = jnp.zeros((part, LANES), F32)
-        for step in range(tensor):
-            for tile in range(tiles):
-                value = pieces[step * SPLITS + split][tile * part : (tile + 1) * part, :].astype(F32)
-                total = total + value * value
-        mean_square = jnp.sum(total, axis=1, keepdims=True) / (tensor * block)
-        scale = jnp.broadcast_to(lax.rsqrt(mean_square + 1e-05), (part, LANES))
-        for step in range(tensor):
-            for tile in range(tiles):
-                piece = pieces[step * SPLITS + split][tile * part : (tile + 1) * part, :]
-                value = piece.astype(F32) * scale * gain_rows[step][tile : tile + 1, :]
-                columns = pl.ds(pl.multiple_of(starts[step] + tile * LANES, LANES), LANES)
-                out_ref[span, columns] = value.astype(BF16)
-                if step == 0:
-                    stream_ref[span, tile * LANES : (tile + 1) * LANES] = piece
+    total = jnp.zeros((rows, LANES), F32)
+    for piece in pieces:
+        for ref, tile in piece:
+            value = ref[tile * rows : (tile + 1) * rows, :].astype(F32)
+            total = total + value * value
+    mean_square = jnp.sum(total, axis=1, keepdims=True) / (tensor * block)
+    scale = jnp.broadcast_to(lax.rsqrt(mean_square + 1e-05), (rows, LANES))
+    for step, piece in enumerate(pieces):
+        gain = gains[step][tiles * rows if step else 0 :, :].astype(F32)
+        for index, (ref, tile) in enumerate(piece):
+            value = ref[tile * rows : (tile + 1) * rows, :]
+            start = pl.multiple_of((rank ^ step) * block + index * LANES, LANES)
+            scaled = value.astype(F32) * scale * gain[index : index + 1, :]
+            out_ref[:, pl.ds(start, LANES)] = scaled.astype(BF16)
+            if step == 0:
+                stream_ref[:, index * LANES : (index + 1) * LANES] = value
 
 
 def normalize(pieces, gains, rows, block):
     tensor = len(gains)
-    return call(
-        functools.partial(norm_kernel, tensor, rows, block),
-        [VMEM] * (tensor * SPLITS + tensor),
+    flat = [part for piece in pieces for part in piece]
+    return call(
+        functools.partial(norm_kernel, rows, block, [len(piece) for piece in pieces]),
+        [VMEM] * (len(flat) + tensor),
         [
             jax.ShapeDtypeStruct((rows, block), BF16),
             jax.ShapeDtypeStruct((rows, tensor * block), BF16),
         ],
         6 * MIB,
-    )(*pieces, *gains)
+    )(*flat, *gains)
 
 
 def on_device(attn_heads, out_weight, residual, norm_gain):
@@ -250,17 +256,21 @@
         sums.update(pair_sum(steps, keep, got, residual, gain))
         for step in steps:
             if step:
-                arrived[step] = [exchange(value, step) for value in sums[step]]
-    streams = [
-        finish_stream(base, [arrived[step][split] for step in range(1, tensor)])
-        for split, base in enumerate(sums[0])
-    ]
-    pieces = list(streams)
-    for step in range(1, tensor):
-        pieces += [exchange(value, step) for value in streams]
-    gains = [gain] + [arrived[step][0] for step in range(1, tensor)]
-    stream, normed = normalize(pieces, gains, rows, block)
-    return stream, normed
+                arrived[step] = exchange(sums[step], step)
+    parts = [arrived[step] for step in range(1, tensor)]
+    stream, *halves = finish_stream(sums[0], parts, tensor == 4)
+    pieces = [[stream]] + [None] * (tensor - 1)
+    if halves:
+        first, second = halves
+        relayed = exchange(first, 2)
+        pieces[1] = [exchange(stream, 1)]
+        pieces[2] = [relayed, exchange(second, 2)]
+        direct = exchange(second, 3)
+        pieces[3] = [exchange(relayed, 1), direct]
+    else:
+        for step in range(1, tensor):
+            pieces[step] = [exchange(stream, step)]
+    return normalize(pieces, [gain] + parts, rows, block)
 
 
 def solution(mesh):

time: 43.7 us -> 43.2 us (0.989)
  waiting for transfers between devices: 20 us -> 16.1 us
  starting transfers between devices: 11.2 us -> 14.6 us
    ppermute x6 -> x8, waiting for transfers between devices: 20 us -> 16.1 us  [exchange(): return lax.ppermute(value, 'tensor', [(i, i ^ step) for i in range(tensor)])]
    ppermute x6 -> x8, starting transfers between devices: 10 us -> 13.4 us  [exchange(): return lax.ppermute(value, 'tensor', [(i, i ^ step) for i in range(tensor)])]
  transfers between devices with their start and end apart: 9 -> 11, of which waited for: 4 -> 6; matrix products, arithmetic and copies ran while one was open for 0% -> 0% of each run, Pallas kernels for 8% -> 8%
where the time goes in v4:
time: 43.2 us; the launch traced here: 43.1 us
  waiting for transfers between devices  16.1 us (37%)
  starting transfers between devices  14.6 us (34%)
  Pallas kernels  11.5 us (27%)
  between operations  0.72 us (2%)
    ppermute x8, waiting for transfers between devices, exchange(): return lax.ppermute(value, 'tensor', [(i, i ^ step) for i in range(tensor)])  16.1 us
    ppermute x8, starting transfers between devices, exchange(): return lax.ppermute(value, 'tensor', [(i, i ^ step) for i in range(tensor)])  13.4 us
    pallas_call x2, Pallas kernels, project(): call(functools.partial(project_kernel, tensor, chunk, steps), [VMEM, VMEM...  7.08 us
    pallas_call x1, Pallas kernels, prefetch(): call(functools.partial(prefetch_kernel, tensor, chunk, steps), [HBM, HBM]...  1.59 us
    pallas_call x1, Pallas kernels, refill(): call(functools.partial(refill_kernel, tensor, chunk, steps), [VMEM, HBM],...  1.57 us
    pallas_call x1, Pallas kernels, normalize(): call(functools.partial(norm_kernel, rows, block, [len(piece) for piece in...  1.12 us
  transfers between devices with their start and end apart: 11, of which 6 were waited for; matrix products, arithmetic and copies ran while one was open for 0% of the time, Pallas kernels for 8%

profile of v4, /device:TPU:0, one launch (start us, length us, event | category | flops | bytes accessed | tf_op | source)
XLA Modules:
  0.0 43.1 jit_solution(2023228794666078692)
XLA Ops:
  0.6 0.6 %collective-permute-start = (bf16[32,2048]{1,0:T(8,128)(2,1)}, bf16[32,2048]{1,0:T(8,128)(2,1)S(1)}, u32[]{:S(2)}, u32[]{:S(2)}) collective-permute-start(bf16[32,2048]{1,0:T(8,128)(2,1)} %own_hbm.1), channel_id=1, source_target_pairs={{0,1},{1,0},{2,3},{3,2},{4,5},{5,4},{6,7},{7,6},{8,9},{9,8},{10,11... | collective-permute-start | bytes 393224 | tf_op jit(solution)/shard_map/ppermute | solution.py:245
  1.2 1.6 %shard_map.59 = (bf16[32,1024]{1,0:T(8,128)(2,1)S(1)}, bf16[2,1024,512]{2,1,0:T(8,128)(2,1)S(1)}) custom-call(bf16[32,2048]{1,0:T(8,128)(2,1)} %own_hbm.1, bf16[1024,8192]{1,0:T(8,128)(2,1)} %weight.7), custom_call_target="tpu_custom_call" | custom-call | tf_op jit(solution)/shard_map/pallas_call | solution.py:98
  2.8 3.5 %shard_map.60 = (f32[2,32,2048]{2,1,0:T(8,128)S(1)}, bf16[2,32,2048]{2,1,0:T(8,128)(2,1)S(1)}) custom-call(bf16[32,1024]{1,0:T(8,128)(2,1)S(1)} %get-tuple-element.20.own_ref._, bf16[32,2048]{1,0:T(8,128)(2,1)S(1)} %collective-permute-done.peer_ref, bf16[2,1024,512]{2,1,0:T(8,128)(2,1)S(1)} %get-tuple-element.18.ready_ref, bf16[1024,8192]{1,0:T(8,128)(2,1)} %weight.7), custom_call_target="tpu_custom_call" | custom-call | tf_op jit(solution)/shard_map/pallas_call | solution.py:128
  6.3 0.1 collective-permute-start.1
  6.4 1.6 %shard_map.61.ready_ref = bf16[2,1024,512]{2,1,0:T(8,128)(2,1)S(1)} custom-call(bf16[32,1024]{1,0:T(8,128)(2,1)S(1)} %get-tuple-element.20.own_ref._, bf16[1024,8192]{1,0:T(8,128)(2,1)} %weight.7), custom_call_target="tpu_custom_call" | custom-call | tf_op jit(solution)/shard_map/pallas_call | solution.py:113
  8.0 3.5 %shard_map.62 = (f32[2,32,2048]{2,1,0:T(8,128)S(1)}, bf16[2,32,2048]{2,1,0:T(8,128)(2,1)S(1)}) custom-call(bf16[32,1024]{1,0:T(8,128)(2,1)S(1)} %get-tuple-element.20.own_ref._, bf16[32,2048]{1,0:T(8,128)(2,1)S(1)} %collective-permute-done.peer_ref, bf16[2,1024,512]{2,1,0:T(8,128)(2,1)S(1)} %shard_map.61.ready_ref, bf16[1024,8192]{1,0:T(8,128)(2,1)} %weight.7), custom_call_target="tpu_custom_call" | custom-call | tf_op jit(solution)/shard_map/pallas_call | solution.py:128
  11.6 0.5 %collective-permute-start.2 = (bf16[2,32,2048]{2,1,0:T(8,128)(2,1)S(1)}, bf16[2,32,2048]{2,1,0:T(8,128)(2,1)S(1)}, u32[]{:S(2)}, u32[]{:S(2)}) collective-permute-start(bf16[2,32,2048]{2,1,0:T(8,128)(2,1)S(1)} %get-tuple-element.23), channel_id=1, source_target_pairs={{0,1},{1,0},{2,3},{3,2},{4,5},{5,4},{6,7},{7,6},{8,9},{9,8},{10,11... | collective-permute-start | bytes 786440 | tf_op jit(solution)/shard_map/ppermute | solution.py:251
  12.2 3.7 %collective-permute-start.4 = (bf16[528,128]{1,0:T(8,128)(2,1)S(1)}, bf16[528,128]{1,0:T(8,128)(2,1)S(1)}, u32[]{:S(2)}, u32[]{:S(2)}) collective-permute-start(bf16[528,128]{1,0:T(8,128)(2,1)S(1)} %get-tuple-element.27), channel_id=1, source_target_pairs={{0,8},{4,12},{8,0},{12,4},{1,9},{5,13},{9,1},{13,5},{2,10},{6,14},... | collective-permute-start | bytes 405512 | tf_op jit(solution)/shard_map/ppermute | solution.py:239
  15.9 1.3 %collective-permute-start.5 = (bf16[528,128]{1,0:T(8,128)(2,1)S(1)}, bf16[528,128]{1,0:T(8,128)(2,1)S(1)}, u32[]{:S(2)}, u32[]{:S(2)}) collective-permute-start(bf16[528,128]{1,0:T(8,128)(2,1)S(1)} %get-tuple-element.28), channel_id=1, source_target_pairs={{0,12},{4,8},{8,4},{12,0},{1,13},{5,9},{9,5},{13,1},{2,14},{6,10},... | collective-permute-start | bytes 405512 | tf_op jit(solution)/shard_map/ppermute | solution.py:239
  17.2 0.1 shard_map.63
  17.3 0.3 collective-permute-start.3
  17.6 8.5 %collective-permute-done.4.refs_1_.refs_8_ = bf16[528,128]{1,0:T(8,128)(2,1)S(1)} collective-permute-done((bf16[528,128]{1,0:T(8,128)(2,1)S(1)}, bf16[528,128]{1,0:T(8,128)(2,1)S(1)}, u32[]{:S(2)}, u32[]{:S(2)}) %collective-permute-start.4) | collective-permute-done | bytes 135200 | tf_op jit(solution)/shard_map/ppermute | solution.py:239
  26.1 1.3 %collective-permute-done.3.refs_0_.refs_7_ = bf16[528,128]{1,0:T(8,128)(2,1)S(1)} collective-permute-done((bf16[528,128]{1,0:T(8,128)(2,1)S(1)}, bf16[528,128]{1,0:T(8,128)(2,1)S(1)}, u32[]{:S(2)}, u32[]{:S(2)}) %collective-permute-start.3) | collective-permute-done | bytes 135200 | tf_op jit(solution)/shard_map/ppermute | solution.py:239
  27.4 0.1 shard_map.65
  27.5 4.1 %collective-permute-start.7 = (bf16[256,128]{1,0:T(8,128)(2,1)S(1)}, bf16[256,128]{1,0:T(8,128)(2,1)S(1)}, u32[]{:S(2)}, u32[]{:S(2)}) collective-permute-start(bf16[256,128]{1,0:T(8,128)(2,1)S(1)} %get-tuple-element.30), channel_id=1, source_target_pairs={{0,8},{4,12},{8,0},{12,4},{1,9},{5,13},{9,1},{13,5},{2,10},{6,14},... | collective-permute-start | bytes 196616 | tf_op jit(solution)/shard_map/ppermute | solution.py:239
  31.6 0.0 collective-permute-start.6
  31.6 1.5 %collective-permute-start.10 = (bf16[256,128]{1,0:T(8,128)(2,1)S(1)}, bf16[256,128]{1,0:T(8,128)(2,1)S(1)}, u32[]{:S(2)}, u32[]{:S(2)}) collective-permute-start(bf16[256,128]{1,0:T(8,128)(2,1)S(1)} %get-tuple-element.31), channel_id=1, source_target_pairs={{0,12},{4,8},{8,4},{12,0},{1,13},{5,9},{9,5},{13,1},{2,14},{6,10},... | collective-permute-start | bytes 196616 | tf_op jit(solution)/shard_map/ppermute | solution.py:239
  33.2 1.9 %collective-permute-start.8 = (bf16[256,128]{1,0:T(8,128)(2,1)S(1)}, bf16[256,128]{1,0:T(8,128)(2,1)S(1)}, u32[]{:S(2)}, u32[]{:S(2)}) collective-permute-start(bf16[256,128]{1,0:T(8,128)(2,1)S(1)} %get-tuple-element.31), channel_id=1, source_target_pairs={{0,8},{4,12},{8,0},{12,4},{1,9},{5,13},{9,1},{13,5},{2,10},{6,14},... | collective-permute-start | bytes 196616 | tf_op jit(solution)/shard_map/ppermute | solution.py:239
  35.1 0.4 collective-permute-done.7.refs_2_
  35.5 0.5 %collective-permute-start.9 = (bf16[256,128]{1,0:T(8,128)(2,1)S(1)}, bf16[256,128]{1,0:T(8,128)(2,1)S(1)}, u32[]{:S(2)}, u32[]{:S(2)}) collective-permute-start(bf16[256,128]{1,0:T(8,128)(2,1)S(1)} %collective-permute-done.7.refs_2_), channel_id=1, source_target_pairs={{0,4},{4,0},{8,12},{12,8},{1,5},{5,1},{9,13},{13,9},{2,6},{6,2},{1... | collective-permute-start | bytes 196616 | tf_op jit(solution)/shard_map/ppermute | solution.py:239
  36.0 3.1 %collective-permute-done.10.refs_5_ = bf16[256,128]{1,0:T(8,128)(2,1)S(1)} collective-permute-done((bf16[256,128]{1,0:T(8,128)(2,1)S(1)}, bf16[256,128]{1,0:T(8,128)(2,1)S(1)}, u32[]{:S(2)}, u32[]{:S(2)}) %collective-permute-start.10) | collective-permute-done | bytes 65568 | tf_op jit(solution)/shard_map/ppermute | solution.py:239
  39.2 2.0 %collective-permute-done.8.refs_3_ = bf16[256,128]{1,0:T(8,128)(2,1)S(1)} collective-permute-done((bf16[256,128]{1,0:T(8,128)(2,1)S(1)}, bf16[256,128]{1,0:T(8,128)(2,1)S(1)}, u32[]{:S(2)}, u32[]{:S(2)}) %collective-permute-start.8) | collective-permute-done | bytes 65568 | tf_op jit(solution)/shard_map/ppermute | solution.py:239
  41.2 0.8 %collective-permute-done.9.refs_4_ = bf16[256,128]{1,0:T(8,128)(2,1)S(1)} collective-permute-done((bf16[256,128]{1,0:T(8,128)(2,1)S(1)}, bf16[256,128]{1,0:T(8,128)(2,1)S(1)}, u32[]{:S(2)}, u32[]{:S(2)}) %collective-permute-start.9) | collective-permute-done | bytes 65568 | tf_op jit(solution)/shard_map/ppermute | solution.py:239
  41.9 1.1 %shard_map.66 = (bf16[32,2048]{1,0:T(8,128)(2,1)}, bf16[32,8192]{1,0:T(8,128)(2,1)}) custom-call(bf16[512,128]{1,0:T(8,128)(2,1)S(1)} %get-tuple-element.29.refs_0_, bf16[512,128]{1,0:T(8,128)(2,1)S(1)} %collective-permute-done.6.refs_1_, bf16[256,128]{1,0:T(8,128)(2,1)S(1)} %collective-permute-done.7.refs_2_, ...), custom_call_target="tpu_custom_call" | custom-call | tf_op jit(solution)/shard_map/pallas_call | solution.py:222
  (10 shorter events, 0.1 us)
Async XLA Ops:
  0.6 2.2 %collective-permute-start = (bf16[32,2048]{1,0:T(8,128)(2,1)}, bf16[32,2048]{1,0:T(8,128)(2,1)S(1)}, u32[]{:S(2)}, u32[]{:S(2)}) collective-permute-start(bf16[32,2048]{1,0:T(8,128)(2,1)} %own_hbm.1), channel_id=1, source_target_pairs={{0,1},{1,0},{2,3},{3,2},{4,5},{5,4},{6,7},{7,6},{8,9},{9,8},{10,11... | collective-permute-start | bytes 393224 | tf_op jit(solution)/shard_map/ppermute | solution.py:245
  6.3 1.7 %collective-permute-start.1 = (bf16[2,32,2048]{2,1,0:T(8,128)(2,1)S(1)}, bf16[2,32,2048]{2,1,0:T(8,128)(2,1)S(1)}, u32[]{:S(2)}, u32[]{:S(2)}) collective-permute-start(bf16[2,32,2048]{2,1,0:T(8,128)(2,1)S(1)} %get-tuple-element.19), channel_id=1, source_target_pairs={{0,1},{1,0},{2,3},{3,2},{4,5},{5,4},{6,7},{7,6},{8,9},{9,8},{10,11... | collective-permute-start | bytes 786440 | tf_op jit(solution)/shard_map/ppermute | solution.py:251
  8.0 4.1 %copy-start = (bf16[32,2048]{1,0:T(8,128)(2,1)S(1)}, bf16[32,2048]{1,0:T(8,128)(2,1)}, u32[]{:S(2)}) copy-start(bf16[32,2048]{1,0:T(8,128)(2,1)} %residual_ref.3) | copy-start | bytes 393220
  8.0 4.1 %copy-start.1 = (bf16[2048]{0:T(1024)(128)(2,1)S(1)}, bf16[2048]{0:T(1024)(128)(2,1)}, u32[]{:S(2)}) copy-start(bf16[2048]{0:T(1024)(128)(2,1)} %param.7) | copy-start | bytes 12292
  11.6 5.6 %collective-permute-start.2 = (bf16[2,32,2048]{2,1,0:T(8,128)(2,1)S(1)}, bf16[2,32,2048]{2,1,0:T(8,128)(2,1)S(1)}, u32[]{:S(2)}, u32[]{:S(2)}) collective-permute-start(bf16[2,32,2048]{2,1,0:T(8,128)(2,1)S(1)} %get-tuple-element.23), channel_id=1, source_target_pairs={{0,1},{1,0},{2,3},{3,2},{4,5},{5,4},{6,7},{7,6},{8,9},{9,8},{10,11... | collective-permute-start | bytes 786440 | tf_op jit(solution)/shard_map/ppermute | solution.py:251
  12.2 13.9 %collective-permute-start.4 = (bf16[528,128]{1,0:T(8,128)(2,1)S(1)}, bf16[528,128]{1,0:T(8,128)(2,1)S(1)}, u32[]{:S(2)}, u32[]{:S(2)}) collective-permute-start(bf16[528,128]{1,0:T(8,128)(2,1)S(1)} %get-tuple-element.27), channel_id=1, source_target_pairs={{0,8},{4,12},{8,0},{12,4},{1,9},{5,13},{9,1},{13,5},{2,10},{6,14},... | collective-permute-start | bytes 405512 | tf_op jit(solution)/shard_map/ppermute | solution.py:239
  15.9 10.3 %collective-permute-start.5 = (bf16[528,128]{1,0:T(8,128)(2,1)S(1)}, bf16[528,128]{1,0:T(8,128)(2,1)S(1)}, u32[]{:S(2)}, u32[]{:S(2)}) collective-permute-start(bf16[528,128]{1,0:T(8,128)(2,1)S(1)} %get-tuple-element.28), channel_id=1, source_target_pairs={{0,12},{4,8},{8,4},{12,0},{1,13},{5,9},{9,5},{13,1},{2,14},{6,10},... | collective-permute-start | bytes 405512 | tf_op jit(solution)/shard_map/ppermute | solution.py:239
  17.3 10.1 %collective-permute-start.3 = (bf16[528,128]{1,0:T(8,128)(2,1)S(1)}, bf16[528,128]{1,0:T(8,128)(2,1)S(1)}, u32[]{:S(2)}, u32[]{:S(2)}) collective-permute-start(bf16[528,128]{1,0:T(8,128)(2,1)S(1)} %get-tuple-element.25), channel_id=1, source_target_pairs={{0,4},{4,0},{8,12},{12,8},{1,5},{5,1},{9,13},{13,9},{2,6},{6,2},{1... | collective-permute-start | bytes 405512 | tf_op jit(solution)/shard_map/ppermute | solution.py:239
  27.5 8.0 %collective-permute-start.7 = (bf16[256,128]{1,0:T(8,128)(2,1)S(1)}, bf16[256,128]{1,0:T(8,128)(2,1)S(1)}, u32[]{:S(2)}, u32[]{:S(2)}) collective-permute-start(bf16[256,128]{1,0:T(8,128)(2,1)S(1)} %get-tuple-element.30), channel_id=1, source_target_pairs={{0,8},{4,12},{8,0},{12,4},{1,9},{5,13},{9,1},{13,5},{2,10},{6,14},... | collective-permute-start | bytes 196616 | tf_op jit(solution)/shard_map/ppermute | solution.py:239
  31.6 9.6 %collective-permute-start.6 = (bf16[512,128]{1,0:T(8,128)(2,1)S(1)}, bf16[512,128]{1,0:T(8,128)(2,1)S(1)}, u32[]{:S(2)}, u32[]{:S(2)}) collective-permute-start(bf16[512,128]{1,0:T(8,128)(2,1)S(1)} %get-tuple-element.29.refs_0_), channel_id=1, source_target_pairs={{0,4},{4,0},{8,12},{12,8},{1,5},{5,1},{9,13},{13,9},{2,6},{6,2},{1... | collective-permute-start | bytes 393224 | tf_op jit(solution)/shard_map/ppermute | solution.py:239
  31.6 7.5 %collective-permute-start.10 = (bf16[256,128]{1,0:T(8,128)(2,1)S(1)}, bf16[256,128]{1,0:T(8,128)(2,1)S(1)}, u32[]{:S(2)}, u32[]{:S(2)}) collective-permute-start(bf16[256,128]{1,0:T(8,128)(2,1)S(1)} %get-tuple-element.31), channel_id=1, source_target_pairs={{0,12},{4,8},{8,4},{12,0},{1,13},{5,9},{9,5},{13,1},{2,14},{6,10},... | collective-permute-start | bytes 196616 | tf_op jit(solution)/shard_map/ppermute | solution.py:239
  33.2 8.0 %collective-permute-start.8 = (bf16[256,128]{1,0:T(8,128)(2,1)S(1)}, bf16[256,128]{1,0:T(8,128)(2,1)S(1)}, u32[]{:S(2)}, u32[]{:S(2)}) collective-permute-start(bf16[256,128]{1,0:T(8,128)(2,1)S(1)} %get-tuple-element.31), channel_id=1, source_target_pairs={{0,8},{4,12},{8,0},{12,4},{1,9},{5,13},{9,1},{13,5},{2,10},{6,14},... | collective-permute-start | bytes 196616 | tf_op jit(solution)/shard_map/ppermute | solution.py:239
  35.5 6.4 %collective-permute-start.9 = (bf16[256,128]{1,0:T(8,128)(2,1)S(1)}, bf16[256,128]{1,0:T(8,128)(2,1)S(1)}, u32[]{:S(2)}, u32[]{:S(2)}) collective-permute-start(bf16[256,128]{1,0:T(8,128)(2,1)S(1)} %collective-permute-done.7.refs_2_), channel_id=1, source_target_pairs={{0,4},{4,0},{8,12},{12,8},{1,5},{5,1},{9,13},{13,9},{2,6},{6,2},{1... | collective-permute-start | bytes 196616 | tf_op jit(solution)/shard_map/ppermute | solution.py:239

commit v5 on v4

--- a/solution.py
+++ b/solution.py
@@ -61,11 +61,11 @@
         copy.wait()
 
 
-def project_kernel(tensor, chunk, steps, own_ref, peer_ref, ready_ref, weight, keep_ref, give_ref, held, sems):
+def project_kernel(tensor, chunk, steps, early, own_ref, peer_ref, *refs):
+    *ready_refs, weight, keep_ref, give_ref, held, sems = refs
     depth, width = weight.shape
     block = width // tensor
     per_block = block // chunk
-    early = ready_ref.shape[0]
     copies = chunk_copies(tensor, chunk, steps, weight)[early:]
     copies = [copy(held.at[i], sems.at[i]) for i, copy in enumerate(copies)]
     for copy in copies:
@@ -76,7 +76,7 @@
     for index in range(len(steps) * per_block):
         place, piece = divmod(index, per_block)
         if index < early:
-            right = ready_ref[index]
+            right = ready_refs[0][index]
         else:
             copies[index - early].wait()
             right = held[index - early]
@@ -124,70 +124,81 @@
     depth, width = weight.shape
     block = width // tensor
     chunk, early = chunk_of(weight, tensor)
+    ready = [] if ready is None else [ready]
+    early = early if ready else 0
     count = len(steps) * block // chunk - early
     return call(
-        functools.partial(project_kernel, tensor, chunk, steps),
-        [VMEM, VMEM, VMEM, HBM],
+        functools.partial(project_kernel, tensor, chunk, steps, early),
+        [VMEM] * (2 + len(ready)) + [HBM],
         [
             jax.ShapeDtypeStruct((len(steps), rows, block), F32),
             jax.ShapeDtypeStruct((len(steps), rows, block), BF16),
         ],
         2 * depth * chunk * (count + early) + 4 * MIB,
         [VMEM((count, depth, chunk), BF16), pltpu.SemaphoreType.DMA((count,))],
-    )(own, peer, ready, pltpu.with_memory_space_constraint(weight, HBM))
-
-
-def pair_kernel(steps, keep_ref, got_ref, residual_ref, gain_ref, *out_refs):
-    _, rows, block = keep_ref.shape
-    for place, step in enumerate(steps):
-        target = out_refs[place]
-        for tile in range(block // LANES):
+    )(own, peer, *ready, pltpu.with_memory_space_constraint(weight, HBM))
+
+
+def pair_kernel(plan, keep_ref, got_ref, gain_ref, *out_refs):
+    rows = keep_ref.shape[1]
+    for (place, first, last, gained), target in zip(plan, out_refs):
+        for tile in range(first, last):
             columns = slice(tile * LANES, (tile + 1) * LANES)
             value = keep_ref[place, :, columns] + got_ref[place, :, columns].astype(F32)
-            if step == 0:
-                value = value + residual_ref[:, columns].astype(F32)
-            target[tile * rows : (tile + 1) * rows, :] = value.astype(target.dtype)
-        if step:
-            target[block // LANES * rows :, :] = gain_ref[...]
-
-
-def pair_sum(steps, keep, got, residual, gain):
+            target[(tile - first) * rows : (tile - first + 1) * rows, :] = value.astype(target.dtype)
+        if gained:
+            target[(last - first) * rows :, :] = gain_ref[...]
+
+
+def pair_sum(plan, keep, got, gain):
+    rows = keep.shape[1]
+    shapes = [
+        jax.ShapeDtypeStruct(((last - first) * rows + gained * gain.shape[0], LANES), dtype)
+        for _, first, last, gained, dtype in plan
+    ]
+    kernel = functools.partial(pair_kernel, [entry[:4] for entry in plan])
+    return call(kernel, [VMEM] * 3, shapes, 6 * MIB)(keep, got, gain)
+
+
+def relay_kernel(mine_ref, got_ref, out_ref):
+    out_ref[...] = (mine_ref[...] + got_ref[...].astype(F32)).astype(BF16)
+
+
+def relay_sum(mine, got):
+    shapes = [jax.ShapeDtypeStruct(mine.shape, BF16)]
+    return call(relay_kernel, [VMEM] * 2, shapes, 4 * MIB)(mine, got)[0]
+
+
+def stream_kernel(spans, keep_ref, got_ref, residual_ref, *refs):
+    _, rows, block = keep_ref.shape
+    parts, stream_ref, halves = refs[: len(spans)], refs[len(spans)], refs[len(spans) + 1 :]
+    tiles = block // LANES
+    for tile in range(tiles):
+        columns = slice(tile * LANES, (tile + 1) * LANES)
+        value = keep_ref[0, :, columns] + got_ref[0, :, columns].astype(F32)
+        value = value + residual_ref[:, columns].astype(F32)
+        for (first, last), part in zip(spans, parts):
+            if first <= tile < last:
+                value = value + part[(tile - first) * rows : (tile - first + 1) * rows, :].astype(F32)
+        stream = value.astype(BF16)
+        stream_ref[tile * rows : (tile + 1) * rows, :] = stream
+        if halves:
+            half, index = divmod(tile, tiles // 2)
+            halves[half][index * rows : (index + 1) * rows, :] = stream
+
+
+def finish_stream(keep, got, residual, parts, spans, halves):
     _, rows, block = keep.shape
     length = rows * block // LANES
-    shapes = [
-        jax.ShapeDtypeStruct((length + gain.shape[0], LANES), BF16)
-        if step
-        else jax.ShapeDtypeStruct((length, LANES), F32)
-        for step in steps
-    ]
-    outs = call(functools.partial(pair_kernel, steps), [VMEM] * 4, shapes, 6 * MIB)(
-        keep, got, residual, gain
-    )
-    return dict(zip(steps, outs))
-
-
-def stream_kernel(count, base_ref, *refs):
-    length = base_ref.shape[0]
-    total = base_ref[...]
-    for ref in refs[:count]:
-        total = total + ref[:length, :].astype(F32)
-    stream = total.astype(BF16)
-    refs[count][...] = stream
-    for half, ref in enumerate(refs[count + 1 :]):
-        ref[...] = stream[half * length // 2 : (half + 1) * length // 2]
-
-
-def finish_stream(base, parts, halves):
-    length = base.shape[0]
-    shapes = [jax.ShapeDtypeStruct(base.shape, BF16)]
+    shapes = [jax.ShapeDtypeStruct((length, LANES), BF16)]
     if halves:
         shapes += [jax.ShapeDtypeStruct((length // 2, LANES), BF16)] * 2
     return call(
-        functools.partial(stream_kernel, len(parts)), [VMEM] * (1 + len(parts)), shapes, 4 * MIB
-    )(base, *parts)
-
-
-def norm_kernel(rows, block, counts, *refs):
+        functools.partial(stream_kernel, spans), [VMEM] * (3 + len(parts)), shapes, 4 * MIB
+    )(keep, got, residual, *parts)
+
+
+def norm_kernel(rows, block, counts, gain_rows, *refs):
     tensor = len(counts)
     tiles = block // LANES
     refs = list(refs)
@@ -206,7 +217,7 @@
     mean_square = jnp.sum(total, axis=1, keepdims=True) / (tensor * block)
     scale = jnp.broadcast_to(lax.rsqrt(mean_square + 1e-05), (rows, LANES))
     for step, piece in enumerate(pieces):
-        gain = gains[step][tiles * rows if step else 0 :, :].astype(F32)
+        gain = gains[step][gains[step].shape[0] - gain_rows :, :].astype(F32)
         for index, (ref, tile) in enumerate(piece):
             value = ref[tile * rows : (tile + 1) * rows, :]
             start = pl.multiple_of((rank ^ step) * block + index * LANES, LANES)
@@ -220,7 +231,9 @@
     tensor = len(gains)
     flat = [part for piece in pieces for part in piece]
     return call(
-        functools.partial(norm_kernel, rows, block, [len(piece) for piece in pieces]),
+        functools.partial(
+            norm_kernel, rows, block, [len(piece) for piece in pieces], gains[0].shape[0]
+        ),
         [VMEM] * (len(flat) + tensor),
         [
             jax.ShapeDtypeStruct((rows, block), BF16),
@@ -240,25 +253,49 @@
 
     gain = norm_gain.reshape(-1, LANES)
     gain = jnp.pad(gain, ((0, -gain.shape[0] % 16), (0, 0)))
-    order = list(range(tensor // 2, tensor)) + list(range(1, tensor // 2)) + [0]
-    waves = [order[: tensor // 2], order[tensor // 2 :]]
+    relay = tensor == 4
+    waves = [list(range(tensor - 1, 0, -1)), [0]]
+    tiles = block // LANES
+    half = tiles // 2
     peer = lax.ppermute(attn_heads, "seq", swap)
     own, ready = prefetch(attn_heads, out_weight, tensor, waves[0])
-    sums = {}
-    arrived = {}
+    parts = []
+    spans = []
+    gains = [gain] + [None] * (tensor - 1)
+
+    def receive(part, first, last):
+        parts.append(part)
+        spans.append((first, last))
+        return part
+
     for wave, steps in enumerate(waves):
         keep, give = project(own, peer, ready, out_weight, tensor, steps)
         got = lax.ppermute(give, "seq", swap)
-        if wave == 0:
-            own, _ = lax.optimization_barrier((own, give))
-            ready = refill(own, out_weight, tensor, waves[1])
-            peer, _ = lax.optimization_barrier((peer, got))
-        sums.update(pair_sum(steps, keep, got, residual, gain))
-        for step in steps:
-            if step:
-                arrived[step] = exchange(sums[step], step)
-    parts = [arrived[step] for step in range(1, tensor)]
-    stream, *halves = finish_stream(sums[0], parts, tensor == 4)
+        if wave:
+            break
+        own, _ = lax.optimization_barrier((own, give))
+        ready = refill(own, out_weight, tensor, waves[1])
+        peer, _ = lax.optimization_barrier((peer, got))
+        if relay:
+            plan = [
+                (0, 0, half, False, BF16),
+                (1, half, tiles, True, BF16),
+                (0, half, tiles, True, BF16),
+                (2, 0, tiles, True, BF16),
+                (1, 0, half, False, F32),
+            ]
+            away, near, far, beside, mine = pair_sum(plan, keep, got, gain)
+            relayed = exchange(away, 1)
+            gains[2] = receive(exchange(near, 2), half, tiles)
+            gains[3] = receive(exchange(far, 3), half, tiles)
+            gains[1] = receive(exchange(beside, 1), 0, tiles)
+            through = relay_sum(mine, relayed)
+            receive(exchange(through, 2), 0, half)
+        else:
+            plan = [(place, 0, tiles, True, BF16) for place in range(len(steps))]
+            for step, value in zip(steps, pair_sum(plan, keep, got, gain)):
+                gains[step] = receive(exchange(value, step), 0, tiles)
+    stream, *halves = finish_stream(keep, got, residual, parts, spans, relay)
     pieces = [[stream]] + [None] * (tensor - 1)
     if halves:
         first, second = halves
@@ -270,7 +307,7 @@
     else:
         for step in range(1, tensor):
             pieces[step] = [exchange(stream, step)]
-    return normalize(pieces, [gain] + parts, rows, block)
+    return normalize(pieces, gains, rows, block)
 
 
 def solution(mesh):

time: 43.2 us -> 43.3 us (level)
  starting transfers between devices: 14.6 us -> 17 us
  waiting for transfers between devices: 16.1 us -> 13.9 us
    ppermute x8 -> x10, waiting for transfers between devices: 16.1 us -> 12.2 us  [exchange(): return lax.ppermute(value, 'tensor', [(i, i ^ step) for i in range(tensor)])]
    ppermute x8 -> x10, starting transfers between devices: 13.4 us -> 16.2 us  [exchange(): return lax.ppermute(value, 'tensor', [(i, i ^ step) for i in range(tensor)])]
    ppermute x2, waiting for transfers between devices: 0.01 us -> 1.7 us  [on_device(): got = lax.ppermute(give, 'seq', swap)]
  transfers between devices with their start and end apart: 11 -> 13, of which waited for: 6 -> 8; matrix products, arithmetic and copies ran while one was open for 0% -> 0% of each run, Pallas kernels for 8% -> 12%
where the time goes in v5:
time: 43.3 us; the launch traced here: 43.1 us
  starting transfers between devices  17 us (39%)
  waiting for transfers between devices  13.9 us (32%)
  Pallas kernels  11.5 us (27%)
  between operations  0.71 us (2%)
    ppermute x10, starting transfers between devices, exchange(): return lax.ppermute(value, 'tensor', [(i, i ^ step) for i in range(tensor)])  16.2 us
    ppermute x10, waiting for transfers between devices, exchange(): return lax.ppermute(value, 'tensor', [(i, i ^ step) for i in range(tensor)])  12.2 us
    pallas_call x2, Pallas kernels, project(): call(functools.partial(project_kernel, tensor, chunk, steps, early), [VME...  7.01 us
    ppermute x2, waiting for transfers between devices, on_device(): got = lax.ppermute(give, 'seq', swap)  1.7 us
    pallas_call x1, Pallas kernels, prefetch(): call(functools.partial(prefetch_kernel, tensor, chunk, steps), [HBM, HBM]...  1.59 us
    pallas_call x1, Pallas kernels, refill(): call(functools.partial(refill_kernel, tensor, chunk, steps), [VMEM, HBM],...  1.56 us
    pallas_call x1, Pallas kernels, normalize(): call(functools.partial(norm_kernel, rows, block, [len(piece) for piece in...  1.12 us
  transfers between devices with their start and end apart: 13, of which 8 were waited for; matrix products, arithmetic and copies ran while one was open for 0% of the time, Pallas kernels for 12%

profile of v5, /device:TPU:0, one launch (start us, length us, event | category | flops | bytes accessed | tf_op | source)
XLA Modules:
  0.0 43.1 jit_solution(16593193857635701641)
XLA Ops:
  0.6 0.6 %collective-permute-start = (bf16[32,2048]{1,0:T(8,128)(2,1)}, bf16[32,2048]{1,0:T(8,128)(2,1)S(1)}, u32[]{:S(2)}, u32[]{:S(2)}) collective-permute-start(bf16[32,2048]{1,0:T(8,128)(2,1)} %own_hbm.1), channel_id=1, source_target_pairs={{0,1},{1,0},{2,3},{3,2},{4,5},{5,4},{6,7},{7,6},{8,9},{9,8},{10,11... | collective-permute-start | bytes 393224 | tf_op jit(solution)/shard_map/ppermute | solution.py:260
  1.2 1.6 %shard_map.59 = (bf16[32,1024]{1,0:T(8,128)(2,1)S(1)}, bf16[2,1024,512]{2,1,0:T(8,128)(2,1)S(1)}) custom-call(bf16[32,2048]{1,0:T(8,128)(2,1)} %own_hbm.1, bf16[1024,8192]{1,0:T(8,128)(2,1)} %refs_1_.3), custom_call_target="tpu_custom_call" | custom-call | tf_op jit(solution)/shard_map/pallas_call | solution.py:98
  2.8 4.8 %shard_map.60 = (f32[3,32,2048]{2,1,0:T(8,128)S(1)}, bf16[3,32,2048]{2,1,0:T(8,128)(2,1)S(1)}) custom-call(bf16[32,1024]{1,0:T(8,128)(2,1)S(1)} %get-tuple-element.21.own_ref._, bf16[32,2048]{1,0:T(8,128)(2,1)S(1)} %collective-permute-done.peer_ref, bf16[2,1024,512]{2,1,0:T(8,128)(2,1)S(1)} %get-tuple-element.19.refs_0_, bf16[1024,8192]{1,0:T(8,128)(2,1)} %refs_1_.3), custom_call_target="tpu_custom_call" | custom-call | tf_op jit(solution)/shard_map/pallas_call | solution.py:130
  7.7 1.7 %collective-permute-done.1.got_ref = bf16[3,32,2048]{2,1,0:T(8,128)(2,1)S(1)} collective-permute-done((bf16[3,32,2048]{2,1,0:T(8,128)(2,1)S(1)}, bf16[3,32,2048]{2,1,0:T(8,128)(2,1)S(1)}, u32[]{:S(2)}, u32[]{:S(2)}) %collective-permute-start.1) | collective-permute-done | bytes 393248 | tf_op jit(solution)/shard_map/ppermute | solution.py:273
  9.5 2.8 %collective-permute-start.5 = (bf16[528,128]{1,0:T(8,128)(2,1)S(1)}, bf16[528,128]{1,0:T(8,128)(2,1)S(1)}, u32[]{:S(2)}, u32[]{:S(2)}) collective-permute-start(bf16[528,128]{1,0:T(8,128)(2,1)S(1)} %get-tuple-element.28), channel_id=1, source_target_pairs={{0,4},{4,0},{8,12},{12,8},{1,5},{5,1},{9,13},{13,9},{2,6},{6,2},{1... | collective-permute-start | bytes 405512 | tf_op jit(solution)/shard_map/ppermute | solution.py:252
  12.3 1.6 %shard_map.61.refs_0_ = bf16[2,1024,512]{2,1,0:T(8,128)(2,1)S(1)} custom-call(bf16[32,1024]{1,0:T(8,128)(2,1)S(1)} %get-tuple-element.21.own_ref._, bf16[1024,8192]{1,0:T(8,128)(2,1)} %refs_1_.3), custom_call_target="tpu_custom_call" | custom-call | tf_op jit(solution)/shard_map/pallas_call | solution.py:113
  13.9 2.2 %shard_map.62 = (f32[1,32,2048]{2,1,0:T(8,128)S(1)}, bf16[1,32,2048]{2,1,0:T(8,128)(2,1)S(1)}) custom-call(bf16[32,1024]{1,0:T(8,128)(2,1)S(1)} %get-tuple-element.21.own_ref._, bf16[32,2048]{1,0:T(8,128)(2,1)S(1)} %collective-permute-done.peer_ref, bf16[2,1024,512]{2,1,0:T(8,128)(2,1)S(1)} %shard_map.61.refs_0_, bf16[1024,8192]{1,0:T(8,128)(2,1)} %refs_1_.3), custom_call_target="tpu_custom_call" | custom-call | tf_op jit(solution)/shard_map/pallas_call | solution.py:130
  16.1 0.2 collective-permute-start.2
  16.3 3.0 %collective-permute-start.3 = (bf16[272,128]{1,0:T(8,128)(2,1)S(1)}, bf16[272,128]{1,0:T(8,128)(2,1)S(1)}, u32[]{:S(2)}, u32[]{:S(2)}) collective-permute-start(bf16[272,128]{1,0:T(8,128)(2,1)S(1)} %get-tuple-element.26), channel_id=1, source_target_pairs={{0,8},{4,12},{8,0},{12,4},{1,9},{5,13},{9,1},{13,5},{2,10},{6,14},... | collective-permute-start | bytes 208904 | tf_op jit(solution)/shard_map/ppermute | solution.py:252
  19.3 1.3 %collective-permute-start.4 = (bf16[272,128]{1,0:T(8,128)(2,1)S(1)}, bf16[272,128]{1,0:T(8,128)(2,1)S(1)}, u32[]{:S(2)}, u32[]{:S(2)}) collective-permute-start(bf16[272,128]{1,0:T(8,128)(2,1)S(1)} %get-tuple-element.27), channel_id=1, source_target_pairs={{0,12},{4,8},{8,4},{12,0},{1,13},{5,9},{9,5},{13,1},{2,14},{6,10},... | collective-permute-start | bytes 208904 | tf_op jit(solution)/shard_map/ppermute | solution.py:252
  20.7 1.8 %collective-permute-start.7 = (bf16[256,128]{1,0:T(8,128)(2,1)S(1)}, bf16[256,128]{1,0:T(8,128)(2,1)S(1)}, u32[]{:S(2)}, u32[]{:S(2)}) collective-permute-start(bf16[256,128]{1,0:T(8,128)(2,1)S(1)} %shard_map.64), channel_id=1, source_target_pairs={{0,8},{4,12},{8,0},{12,4},{1,9},{5,13},{9,1},{13,5},{2,10},{6,14},... | collective-permute-start | bytes 196616 | tf_op jit(solution)/shard_map/ppermute | solution.py:252
  22.4 1.4 %collective-permute-done.3.refs_0_.refs_8_ = bf16[272,128]{1,0:T(8,128)(2,1)S(1)} collective-permute-done((bf16[272,128]{1,0:T(8,128)(2,1)S(1)}, bf16[272,128]{1,0:T(8,128)(2,1)S(1)}, u32[]{:S(2)}, u32[]{:S(2)}) %collective-permute-start.3) | collective-permute-done | bytes 69664 | tf_op jit(solution)/shard_map/ppermute | solution.py:252
  23.8 2.3 %collective-permute-done.4.refs_1_.refs_9_ = bf16[272,128]{1,0:T(8,128)(2,1)S(1)} collective-permute-done((bf16[272,128]{1,0:T(8,128)(2,1)S(1)}, bf16[272,128]{1,0:T(8,128)(2,1)S(1)}, u32[]{:S(2)}, u32[]{:S(2)}) %collective-permute-start.4) | collective-permute-done | bytes 69664 | tf_op jit(solution)/shard_map/ppermute | solution.py:252
  26.1 3.2 %collective-permute-done.7.refs_3_ = bf16[256,128]{1,0:T(8,128)(2,1)S(1)} collective-permute-done((bf16[256,128]{1,0:T(8,128)(2,1)S(1)}, bf16[256,128]{1,0:T(8,128)(2,1)S(1)}, u32[]{:S(2)}, u32[]{:S(2)}) %collective-permute-start.7) | collective-permute-done | bytes 65568 | tf_op jit(solution)/shard_map/ppermute | solution.py:252
  29.5 1.4 %collective-permute-start.9 = (bf16[256,128]{1,0:T(8,128)(2,1)S(1)}, bf16[256,128]{1,0:T(8,128)(2,1)S(1)}, u32[]{:S(2)}, u32[]{:S(2)}) collective-permute-start(bf16[256,128]{1,0:T(8,128)(2,1)S(1)} %get-tuple-element.32), channel_id=1, source_target_pairs={{0,8},{4,12},{8,0},{12,4},{1,9},{5,13},{9,1},{13,5},{2,10},{6,14},... | collective-permute-start | bytes 196616 | tf_op jit(solution)/shard_map/ppermute | solution.py:252
  30.8 2.8 %collective-permute-start.8 = (bf16[512,128]{1,0:T(8,128)(2,1)S(1)}, bf16[512,128]{1,0:T(8,128)(2,1)S(1)}, u32[]{:S(2)}, u32[]{:S(2)}) collective-permute-start(bf16[512,128]{1,0:T(8,128)(2,1)S(1)} %get-tuple-element.31.refs_0_), channel_id=1, source_target_pairs={{0,4},{4,0},{8,12},{12,8},{1,5},{5,1},{9,13},{13,9},{2,6},{6,2},{1... | collective-permute-start | bytes 393224 | tf_op jit(solution)/shard_map/ppermute | solution.py:252
  33.6 0.3 collective-permute-start.12
  33.9 1.2 %collective-permute-start.10 = (bf16[256,128]{1,0:T(8,128)(2,1)S(1)}, bf16[256,128]{1,0:T(8,128)(2,1)S(1)}, u32[]{:S(2)}, u32[]{:S(2)}) collective-permute-start(bf16[256,128]{1,0:T(8,128)(2,1)S(1)} %get-tuple-element.33), channel_id=1, source_target_pairs={{0,8},{4,12},{8,0},{12,4},{1,9},{5,13},{9,1},{13,5},{2,10},{6,14},... | collective-permute-start | bytes 196616 | tf_op jit(solution)/shard_map/ppermute | solution.py:252
  35.1 1.4 %collective-permute-done.9.refs_2_ = bf16[256,128]{1,0:T(8,128)(2,1)S(1)} collective-permute-done((bf16[256,128]{1,0:T(8,128)(2,1)S(1)}, bf16[256,128]{1,0:T(8,128)(2,1)S(1)}, u32[]{:S(2)}, u32[]{:S(2)}) %collective-permute-start.9) | collective-permute-done | bytes 65568 | tf_op jit(solution)/shard_map/ppermute | solution.py:252
  36.5 1.6 %collective-permute-start.11 = (bf16[256,128]{1,0:T(8,128)(2,1)S(1)}, bf16[256,128]{1,0:T(8,128)(2,1)S(1)}, u32[]{:S(2)}, u32[]{:S(2)}) collective-permute-start(bf16[256,128]{1,0:T(8,128)(2,1)S(1)} %collective-permute-done.9.refs_2_), channel_id=1, source_target_pairs={{0,4},{4,0},{8,12},{12,8},{1,5},{5,1},{9,13},{13,9},{2,6},{6,2},{1... | collective-permute-start | bytes 196616 | tf_op jit(solution)/shard_map/ppermute | solution.py:252
  38.0 2.4 %collective-permute-done.12.refs_5_ = bf16[256,128]{1,0:T(8,128)(2,1)S(1)} collective-permute-done((bf16[256,128]{1,0:T(8,128)(2,1)S(1)}, bf16[256,128]{1,0:T(8,128)(2,1)S(1)}, u32[]{:S(2)}, u32[]{:S(2)}) %collective-permute-start.12) | collective-permute-done | bytes 65568 | tf_op jit(solution)/shard_map/ppermute | solution.py:252
  40.4 1.1 %collective-permute-done.10.refs_3_ = bf16[256,128]{1,0:T(8,128)(2,1)S(1)} collective-permute-done((bf16[256,128]{1,0:T(8,128)(2,1)S(1)}, bf16[256,128]{1,0:T(8,128)(2,1)S(1)}, u32[]{:S(2)}, u32[]{:S(2)}) %collective-permute-start.10) | collective-permute-done | bytes 65568 | tf_op jit(solution)/shard_map/ppermute | solution.py:252
  41.6 0.4 collective-permute-done.11.refs_4_
  42.0 1.1 %shard_map.66 = (bf16[32,2048]{1,0:T(8,128)(2,1)}, bf16[32,8192]{1,0:T(8,128)(2,1)}) custom-call(bf16[512,128]{1,0:T(8,128)(2,1)S(1)} %get-tuple-element.31.refs_0_, bf16[512,128]{1,0:T(8,128)(2,1)S(1)} %collective-permute-done.8.refs_1_, bf16[256,128]{1,0:T(8,128)(2,1)S(1)} %collective-permute-done.9.refs_2_, ...), custom_call_target="tpu_custom_call" | custom-call | tf_op jit(solution)/shard_map/pallas_call | solution.py:233
  (14 shorter events, 0.4 us)
Async XLA Ops:
  0.6 2.2 %collective-permute-start = (bf16[32,2048]{1,0:T(8,128)(2,1)}, bf16[32,2048]{1,0:T(8,128)(2,1)S(1)}, u32[]{:S(2)}, u32[]{:S(2)}) collective-permute-start(bf16[32,2048]{1,0:T(8,128)(2,1)} %own_hbm.1), channel_id=1, source_target_pairs={{0,1},{1,0},{2,3},{3,2},{4,5},{5,4},{6,7},{7,6},{8,9},{9,8},{10,11... | collective-permute-start | bytes 393224 | tf_op jit(solution)/shard_map/ppermute | solution.py:260
  2.8 6.6 %copy-start.1 = (bf16[2048]{0:T(1024)(128)(2,1)S(1)}, bf16[2048]{0:T(1024)(128)(2,1)}, u32[]{:S(2)}) copy-start(bf16[2048]{0:T(1024)(128)(2,1)} %param.7) | copy-start | bytes 12292
  7.6 1.8 %collective-permute-start.1 = (bf16[3,32,2048]{2,1,0:T(8,128)(2,1)S(1)}, bf16[3,32,2048]{2,1,0:T(8,128)(2,1)S(1)}, u32[]{:S(2)}, u32[]{:S(2)}) collective-permute-start(bf16[3,32,2048]{2,1,0:T(8,128)(2,1)S(1)} %get-tuple-element.20), channel_id=1, source_target_pairs={{0,1},{1,0},{2,3},{3,2},{4,5},{5,4},{6,7},{7,6},{8,9},{9,8},{10,11... | collective-permute-start | bytes 1179656 | tf_op jit(solution)/shard_map/ppermute | solution.py:273
  9.5 19.9 %collective-permute-start.5 = (bf16[528,128]{1,0:T(8,128)(2,1)S(1)}, bf16[528,128]{1,0:T(8,128)(2,1)S(1)}, u32[]{:S(2)}, u32[]{:S(2)}) collective-permute-start(bf16[528,128]{1,0:T(8,128)(2,1)S(1)} %get-tuple-element.28), channel_id=1, source_target_pairs={{0,4},{4,0},{8,12},{12,8},{1,5},{5,1},{9,13},{13,9},{2,6},{6,2},{1... | collective-permute-start | bytes 405512 | tf_op jit(solution)/shard_map/ppermute | solution.py:252
  13.8 15.5 %copy-start = (bf16[32,2048]{1,0:T(8,128)(2,1)S(1)}, bf16[32,2048]{1,0:T(8,128)(2,1)}, u32[]{:S(2)}) copy-start(bf16[32,2048]{1,0:T(8,128)(2,1)} %residual_ref.1) | copy-start | bytes 393220
  13.8 6.8 %collective-permute-start.6 = (bf16[256,128]{1,0:T(8,128)(2,1)S(1)}, bf16[256,128]{1,0:T(8,128)(2,1)S(1)}, u32[]{:S(2)}, u32[]{:S(2)}) collective-permute-start(bf16[256,128]{1,0:T(8,128)(2,1)S(1)} %get-tuple-element.30), channel_id=1, source_target_pairs={{0,4},{4,0},{8,12},{12,8},{1,5},{5,1},{9,13},{13,9},{2,6},{6,2},{1... | collective-permute-start | bytes 196616 | tf_op jit(solution)/shard_map/ppermute | solution.py:252
  16.1 13.2 %collective-permute-start.2 = (bf16[1,32,2048]{2,1,0:T(8,128)(2,1)S(1)}, bf16[1,32,2048]{2,1,0:T(8,128)(2,1)S(1)}, u32[]{:S(2)}, u32[]{:S(2)}) collective-permute-start(bf16[1,32,2048]{2,1,0:T(8,128)(2,1)S(1)} %get-tuple-element.24), channel_id=1, source_target_pairs={{0,1},{1,0},{2,3},{3,2},{4,5},{5,4},{6,7},{7,6},{8,9},{9,8},{10,11... | collective-permute-start | bytes 393224 | tf_op jit(solution)/shard_map/ppermute | solution.py:273
  16.3 7.5 %collective-permute-start.3 = (bf16[272,128]{1,0:T(8,128)(2,1)S(1)}, bf16[272,128]{1,0:T(8,128)(2,1)S(1)}, u32[]{:S(2)}, u32[]{:S(2)}) collective-permute-start(bf16[272,128]{1,0:T(8,128)(2,1)S(1)} %get-tuple-element.26), channel_id=1, source_target_pairs={{0,8},{4,12},{8,0},{12,4},{1,9},{5,13},{9,1},{13,5},{2,10},{6,14},... | collective-permute-start | bytes 208904 | tf_op jit(solution)/shard_map/ppermute | solution.py:252
  19.3 6.8 %collective-permute-start.4 = (bf16[272,128]{1,0:T(8,128)(2,1)S(1)}, bf16[272,128]{1,0:T(8,128)(2,1)S(1)}, u32[]{:S(2)}, u32[]{:S(2)}) collective-permute-start(bf16[272,128]{1,0:T(8,128)(2,1)S(1)} %get-tuple-element.27), channel_id=1, source_target_pairs={{0,12},{4,8},{8,4},{12,0},{1,13},{5,9},{9,5},{13,1},{2,14},{6,10},... | collective-permute-start | bytes 208904 | tf_op jit(solution)/shard_map/ppermute | solution.py:252
  20.7 8.7 %collective-permute-start.7 = (bf16[256,128]{1,0:T(8,128)(2,1)S(1)}, bf16[256,128]{1,0:T(8,128)(2,1)S(1)}, u32[]{:S(2)}, u32[]{:S(2)}) collective-permute-start(bf16[256,128]{1,0:T(8,128)(2,1)S(1)} %shard_map.64), channel_id=1, source_target_pairs={{0,8},{4,12},{8,0},{12,4},{1,9},{5,13},{9,1},{13,5},{2,10},{6,14},... | collective-permute-start | bytes 196616 | tf_op jit(solution)/shard_map/ppermute | solution.py:252
  29.5 7.0 %collective-permute-start.9 = (bf16[256,128]{1,0:T(8,128)(2,1)S(1)}, bf16[256,128]{1,0:T(8,128)(2,1)S(1)}, u32[]{:S(2)}, u32[]{:S(2)}) collective-permute-start(bf16[256,128]{1,0:T(8,128)(2,1)S(1)} %get-tuple-element.32), channel_id=1, source_target_pairs={{0,8},{4,12},{8,0},{12,4},{1,9},{5,13},{9,1},{13,5},{2,10},{6,14},... | collective-permute-start | bytes 196616 | tf_op jit(solution)/shard_map/ppermute | solution.py:252
  30.8 11.2 %collective-permute-start.8 = (bf16[512,128]{1,0:T(8,128)(2,1)S(1)}, bf16[512,128]{1,0:T(8,128)(2,1)S(1)}, u32[]{:S(2)}, u32[]{:S(2)}) collective-permute-start(bf16[512,128]{1,0:T(8,128)(2,1)S(1)} %get-tuple-element.31.refs_0_), channel_id=1, source_target_pairs={{0,4},{4,0},{8,12},{12,8},{1,5},{5,1},{9,13},{13,9},{2,6},{6,2},{1... | collective-permute-start | bytes 393224 | tf_op jit(solution)/shard_map/ppermute | solution.py:252
  33.6 6.8 %collective-permute-start.12 = (bf16[256,128]{1,0:T(8,128)(2,1)S(1)}, bf16[256,128]{1,0:T(8,128)(2,1)S(1)}, u32[]{:S(2)}, u32[]{:S(2)}) collective-permute-start(bf16[256,128]{1,0:T(8,128)(2,1)S(1)} %get-tuple-element.33), channel_id=1, source_target_pairs={{0,12},{4,8},{8,4},{12,0},{1,13},{5,9},{9,5},{13,1},{2,14},{6,10},... | collective-permute-start | bytes 196616 | tf_op jit(solution)/shard_map/ppermute | solution.py:252
  33.9 7.7 %collective-permute-start.10 = (bf16[256,128]{1,0:T(8,128)(2,1)S(1)}, bf16[256,128]{1,0:T(8,128)(2,1)S(1)}, u32[]{:S(2)}, u32[]{:S(2)}) collective-permute-start(bf16[256,128]{1,0:T(8,128)(2,1)S(1)} %get-tuple-element.33), channel_id=1, source_target_pairs={{0,8},{4,12},{8,0},{12,4},{1,9},{5,13},{9,1},{13,5},{2,10},{6,14},... | collective-permute-start | bytes 196616 | tf_op jit(solution)/shard_map/ppermute | solution.py:252
  36.5 5.5 %collective-permute-start.11 = (bf16[256,128]{1,0:T(8,128)(2,1)S(1)}, bf16[256,128]{1,0:T(8,128)(2,1)S(1)}, u32[]{:S(2)}, u32[]{:S(2)}) collective-permute-start(bf16[256,128]{1,0:T(8,128)(2,1)S(1)} %collective-permute-done.9.refs_2_), channel_id=1, source_target_pairs={{0,4},{4,0},{8,12},{12,8},{1,5},{5,1},{9,13},{13,9},{2,6},{6,2},{1... | collective-permute-start | bytes 196616 | tf_op jit(solution)/shard_map/ppermute | solution.py:252

commit v6 on v5

v6 whole, which is shorter than its diff:
```python
import functools

import jax
import jax.numpy as jnp
from jax import lax
from jax.experimental import pallas as pl
from jax.experimental.pallas import tpu as pltpu
from jax.sharding import PartitionSpec as P


VMEM, HBM = pltpu.VMEM, pltpu.HBM
MIB = 1024 * 1024
F32, BF16 = jnp.float32, jnp.bfloat16
LANES = 128
READY = 2
LATER = 4
CHUNK = 512


def call(kernel, in_specs, out_shape, limit, scratch=(), out_space=VMEM):
    return pl.pallas_call(
        kernel,
        in_specs=[pl.BlockSpec(memory_space=space) for space in in_specs],
        out_specs=[pl.BlockSpec(memory_space=out_space)] * len(out_shape),
        out_shape=out_shape,
        scratch_shapes=list(scratch),
        compiler_params=pltpu.CompilerParams(vmem_limit_bytes=limit),
    )


def chunk_copies(tensor, chunk, steps, weight):
    block = weight.shape[1] // tensor
    rank = lax.axis_index("tensor")
    copies = []
    for step in steps:
        for piece in range(block // chunk):
            start = pl.multiple_of((rank ^ step) * block + piece * chunk, LANES)
            copies.append(functools.partial(pltpu.make_async_copy, weight.at[:, pl.ds(start, chunk)]))
    return copies


def prefetch_kernel(tensor, chunk, steps, own_hbm, weight, own_ref, ready_ref, own_sem, sems):
    depth = weight.shape[0]
    features = pl.ds(pl.multiple_of(lax.axis_index("seq") * depth, LANES), depth)
    own_copy = pltpu.make_async_copy(own_hbm.at[:, features], own_ref, own_sem)
    own_copy.start()
    copies = chunk_copies(tensor, chunk, steps, weight)[: ready_ref.shape[0]]
    copies = [copy(ready_ref.at[i], sems.at[i]) for i, copy in enumerate(copies)]
    for copy in copies:
        copy.start()
    for copy in copies:
        copy.wait()
    own_copy.wait()


def project_kernel(tensor, chunk, steps, early, after, own_ref, peer_ref, *refs):
    ready_refs, (weight, keep_ref, give_ref, *later_refs, held, sems) = refs[:early], refs[early:]
    depth, width = weight.shape
    block = width // tensor
    per_block = block // chunk
    early = ready_refs[0].shape[0] if early else 0
    copies = chunk_copies(tensor, chunk, steps, weight)[early:]
    copies = [copy(held.at[i], sems.at[i]) for i, copy in enumerate(copies)]
    later = []
    if later_refs:
        later = chunk_copies(tensor, chunk, after, weight)[: later_refs[0].shape[0]]
        later = [copy(later_refs[0].at[i], sems.at[len(copies) + i]) for i, copy in enumerate(later)]
    for copy in copies + later:
        copy.start()
    features = pl.ds(pl.multiple_of(lax.axis_index("seq") * depth, LANES), depth)
    rows = own_ref.shape[0]
    operand = jnp.concatenate([own_ref[...], peer_ref[:, features]], axis=0)
    for index in range(len(steps) * per_block):
        place, piece = divmod(index, per_block)
        if index < early:
            right = ready_refs[0][index]
        else:
            copies[index - early].wait()
            right = held[index - early]
        product = jnp.dot(operand, right, preferred_element_type=F32)
        columns = pl.ds(piece * chunk, chunk)
        keep_ref[place, :, columns] = product[:rows]
        give_ref[place, :, columns] = product[rows:].astype(BF16)
    for copy in later:
        copy.wait()


def chunk_of(weight, tensor):
    block = weight.shape[1] // tensor
    chunk = min(block, CHUNK)
    return chunk, min(READY * MIB // (2 * weight.shape[0] * chunk), block // chunk)


def prefetch(own, weight, tensor, steps):
    rows, depth = own.shape[0], weight.shape[0]
    chunk, early = chunk_of(weight, tensor)
    return call(
        functools.partial(prefetch_kernel, tensor, chunk, steps),
        [HBM, HBM],
        [
            jax.ShapeDtypeStruct((rows, depth), BF16),
            jax.ShapeDtypeStruct((early, depth, chunk), BF16),
        ],
        2 * depth * chunk * early + 2 * MIB,
        [pltpu.SemaphoreType.DMA(()), pltpu.SemaphoreType.DMA((early,))],
    )(pltpu.with_memory_space_constraint(own, HBM), pltpu.with_memory_space_constraint(weight, HBM))


def project(own, peer, ready, weight, tensor, steps, after=()):
    rows = own.shape[0]
    depth, width = weight.shape
    block = width // tensor
    chunk, _ = chunk_of(weight, tensor)
    ready = [] if ready is None else [ready]
    early = ready[0].shape[0] if ready else 0
    count = len(steps) * block // chunk - early
    later = min(LATER * MIB // (2 * depth * chunk), len(after) * block // chunk)
    shapes = [
        jax.ShapeDtypeStruct((len(steps), rows, block), F32),
        jax.ShapeDtypeStruct((len(steps), rows, block), BF16),
    ]
    if later:
        shapes.append(jax.ShapeDtypeStruct((later, depth, chunk), BF16))
    return call(
        functools.partial(project_kernel, tensor, chunk, steps, len(ready), after),
        [VMEM] * (2 + len(ready)) + [HBM],
        shapes,
        2 * depth * chunk * (len(steps) * block // chunk + later) + 4 * MIB,
        [VMEM((count, depth, chunk), BF16), pltpu.SemaphoreType.DMA((count + later,))],
    )(own, peer, *ready, pltpu.with_memory_space_constraint(weight, HBM))


def pair_kernel(plan, keep_ref, got_ref, gain_ref, *out_refs):
    rows = keep_ref.shape[1]
    for (place, first, last, gained), target in zip(plan, out_refs):
        for tile in range(first, last):
            columns = slice(tile * LANES, (tile + 1) * LANES)
            value = keep_ref[place, :, columns] + got_ref[place, :, columns].astype(F32)
            target[(tile - first) * rows : (tile - first + 1) * rows, :] = value.astype(target.dtype)
        if gained:
            target[(last - first) * rows :, :] = gain_ref[...]


def pair_sum(plan, keep, got, gain):
    rows = keep.shape[1]
    shapes = [
        jax.ShapeDtypeStruct(((last - first) * rows + gained * gain.shape[0], LANES), dtype)
        for _, first, last, gained, dtype in plan
    ]
    kernel = functools.partial(pair_kernel, [entry[:4] for entry in plan])
    return call(kernel, [VMEM] * 3, shapes, 6 * MIB)(keep, got, gain)


def relay_kernel(mine_ref, got_ref, out_ref):
    out_ref[...] = (mine_ref[...] + got_ref[...].astype(F32)).astype(BF16)


def relay_sum(mine, got):
    shapes = [jax.ShapeDtypeStruct(mine.shape, BF16)]
    return call(relay_kernel, [VMEM] * 2, shapes, 4 * MIB)(mine, got)[0]


def stream_kernel(spans, first_tile, last_tile, early, keep_ref, got_ref, residual_ref, *refs):
    rows = keep_ref.shape[1]
    parts, refs = refs[: len(spans)], refs[len(spans) :]
    early_refs, (part_ref, *whole_refs) = refs[:early], refs[early:]
    for tile in range(first_tile, last_tile):
        columns = slice(tile * LANES, (tile + 1) * LANES)
        value = keep_ref[0, :, columns] + got_ref[0, :, columns].astype(F32)
        value = value + residual_ref[:, columns].astype(F32)
        for (first, last), part in zip(spans, parts):
            if first <= tile < last:
                value = value + part[(tile - first) * rows : (tile - first + 1) * rows, :].astype(F32)
        stream = value.astype(BF16)
        part_ref[(tile - first_tile) * rows : (tile - first_tile + 1) * rows, :] = stream
        for ref in whole_refs:
            ref[tile * rows : (tile + 1) * rows, :] = stream
    for early_ref, ref in zip(early_refs, whole_refs):
        ref[last_tile * rows :, :] = early_ref[...]


def finish_stream(keep, got, residual, parts, spans, first_tile, last_tile, early=()):
    _, rows, block = keep.shape
    shapes = [jax.ShapeDtypeStruct(((last_tile - first_tile) * rows, LANES), BF16)]
    shapes += [jax.ShapeDtypeStruct((rows * block // LANES, LANES), BF16)] * len(early)
    return call(
        functools.partial(stream_kernel, spans, first_tile, last_tile, len(early)),
        [VMEM] * (3 + len(parts) + len(early)),
        shapes,
        4 * MIB,
    )(keep, got, residual, *parts, *early)


def norm_kernel(rows, block, counts, gain_rows, *refs):
    tensor = len(counts)
    tiles = block // LANES
    refs = list(refs)
    pieces = []
    for count in counts:
        group = [refs.pop(0) for _ in range(count)]
        size = tiles // count
        pieces.append([(group[tile // size], tile % size) for tile in range(tiles)])
    gains, (stream_hbm, out_hbm, stream_ref, out_ref, sems) = refs[:tensor], refs[tensor:]
    rank = lax.axis_index("tensor")
    copies = [pltpu.make_async_copy(stream_ref, stream_hbm, sems.at[tensor])]
    for step in range(tensor):
        start = pl.multiple_of((rank ^ step) * block, LANES)
        target = out_hbm.at[:, pl.ds(start, block)]
        copies.append(pltpu.make_async_copy(out_ref.at[step], target, sems.at[step]))
    for index, (ref, tile) in enumerate(pieces[0]):
        columns = slice(index * LANES, (index + 1) * LANES)
        stream_ref[:, columns] = ref[tile * rows : (tile + 1) * rows, :]
    copies[0].start()
    total = jnp.zeros((rows, LANES), F32)
    for piece in pieces:
        for ref, tile in piece:
            value = ref[tile * rows : (tile + 1) * rows, :].astype(F32)
            total = total + value * value
    mean_square = jnp.sum(total, axis=1, keepdims=True) / (tensor * block)
    scale = jnp.broadcast_to(lax.rsqrt(mean_square + 1e-05), (rows, LANES))
    for step, piece in enumerate(pieces):
        gain = gains[step][gains[step].shape[0] - gain_rows :, :].astype(F32)
        for index, (ref, tile) in enumerate(piece):
            value = ref[tile * rows : (tile + 1) * rows, :].astype(F32)
            scaled = value * scale * gain[index : index + 1, :]
            out_ref[step, :, index * LANES : (index + 1) * LANES] = scaled.astype(BF16)
        copies[step + 1].start()
    for copy in copies:
        copy.wait()


def normalize(pieces, gains, rows, block):
    tensor = len(gains)
    flat = [part for piece in pieces for part in piece]
    counts = [len(piece) for piece in pieces]
    return call(
        functools.partial(norm_kernel, rows, block, counts, gains[0].shape[0]),
        [VMEM] * (len(flat) + tensor),
        [
            jax.ShapeDtypeStruct((rows, block), BF16),
            jax.ShapeDtypeStruct((rows, tensor * block), BF16),
        ],
        6 * MIB,
        [
            VMEM((rows, block), BF16),
            VMEM((tensor, rows, block), BF16),
            pltpu.SemaphoreType.DMA((tensor + 1,)),
        ],
        HBM,
    )(*flat, *gains)


def on_device(attn_heads, out_weight, residual, norm_gain):
    tensor = lax.axis_size("tensor")
    rows, block = residual.shape
    swap = [(0, 1), (1, 0)]

    def exchange(value, step):
        return lax.ppermute(value, "tensor", [(i, i ^ step) for i in range(tensor)])

    gain = norm_gain.reshape(-1, LANES)
    gain = jnp.pad(gain, ((0, -gain.shape[0] % 16), (0, 0)))
    relay = tensor == 4
    tiles = block // LANES
    half = tiles // 2
    parts = []
    spans = []
    gains = [gain] + [None] * (tensor - 1)

    def receive(part, first, last):
        parts.append(part)
        spans.append((first, last))
        return part

    def chip_products(steps, before=None, ready=None, after=()):
        rows_in = (own, peer)
        if before is not None:
            *rows_in, _ = lax.optimization_barrier((own, peer, before))
        keep, give, *later = project(*rows_in, ready, out_weight, tensor, steps, after)
        return keep, lax.ppermute(give, "seq", swap), *later

    peer = lax.ppermute(attn_heads, "seq", swap)
    far_steps = list(range(tensor - 1, tensor // 2 - 1, -1))
    near_steps = list(range(tensor // 2 - 1, 0, -1))
    own, ready = prefetch(attn_heads, out_weight, tensor, far_steps)
    keep, got, ready = chip_products(far_steps, None, ready, near_steps)
    keep_near, got_near = chip_products(near_steps, None, ready)
    if not relay:
        for wave, steps in enumerate((far_steps, near_steps)):
            plan = [(place, 0, tiles, True, BF16) for place in range(len(steps))]
            sums = pair_sum(plan, *((keep, got), (keep_near, got_near))[wave], gain)
            for step, value in zip(steps, sums):
                gains[step] = receive(exchange(value, step), 0, tiles)
        keep, got = chip_products([0], got_near)
        stream = finish_stream(keep, got, residual, parts, spans, 0, tiles)[0]
        pieces = [[stream]] + [[exchange(stream, step)] for step in range(1, tensor)]
        return normalize(pieces, gains, rows, block)
    plan = [
        (0, 0, half, False, BF16),
        (1, half, tiles, True, BF16),
        (0, half, tiles, True, BF16),
        (1, 0, half, False, F32),
    ]
    away, near, far, mine = pair_sum(plan, keep, got, gain)
    relayed = exchange(away, 1)
    gains[2] = receive(exchange(near, 2), half, tiles)
    gains[3] = receive(exchange(far, 3), half, tiles)
    beside = pair_sum([(0, 0, tiles, True, BF16)], keep_near, got_near, gain)[0]
    gains[1] = receive(exchange(beside, 1), 0, tiles)
    keep, got = chip_products([0], got_near)
    through = relay_sum(mine, relayed)
    last = exchange(through, 2)
    second = finish_stream(keep, got, residual, parts, spans, half, tiles)[0]
    relayed = exchange(second, 2)
    receive(last, 0, half)
    first, stream = finish_stream(keep, got, residual, parts, spans, 0, half, [second])
    beside = exchange(stream, 1)
    opposite = exchange(first, 2)
    direct = exchange(first, 3)
    through = exchange(relayed, 1)
    pieces = [[stream], [beside], [opposite, relayed], [direct, through]]
    return normalize(pieces, gains, rows, block)


def solution(mesh):
    in_specs = (
        P(("groups", "dp", "seq"), "tensor"),
        P(("tensor", "seq"), None),
        P(("groups", "dp", "seq"), "tensor"),
        P("tensor"),
    )
    out_specs = (P(("groups", "dp", "seq"), "tensor"), P(("groups", "dp", "seq"), None))

    return jax.shard_map(on_device, mesh=mesh, in_specs=in_specs, out_specs=out_specs, check_vma=False)
```

time: 43.3 us -> 41.1 us (0.949)
  waiting for transfers between devices: 13.9 us -> 10.5 us
  starting transfers between devices: 17 us -> 19 us
  Pallas kernels: 11.5 us -> 10.6 us
    ppermute x10, waiting for transfers between devices: 12.2 us -> 9.49 us  [exchange(): return lax.ppermute(value, 'tensor', [(i, i ^ step) for i in range(tensor)])]
    ppermute x10, starting transfers between devices: 16.2 us -> 17.8 us  [exchange(): return lax.ppermute(value, 'tensor', [(i, i ^ step) for i in range(tensor)])]
    pallas_call x5 -> x6, Pallas kernels: 9.79 us -> 8.96 us  [the longest x3 7.88 us: project(): call(functools.partial(project_kernel, tensor, chunk, steps, len(ready),...]
    ppermute x2 -> x3, waiting for transfers between devices: 1.7 us -> 0.99 us  [chip_products(): return (keep, lax.ppermute(give, 'seq', swap), *later)]
    ppermute x2 -> x3, starting transfers between devices: 0.25 us -> 0.71 us  [chip_products(): return (keep, lax.ppermute(give, 'seq', swap), *later)]
  transfers between devices with their start and end apart: 13 -> 14, of which waited for: 8 -> 5; matrix products, arithmetic and copies ran while one was open for 0% -> 0% of each run, Pallas kernels for 12% -> 13%
where the time goes in v6:
time: 41.1 us; the launch traced here: 40.9 us
  starting transfers between devices  19 us (46%)
  Pallas kernels  10.6 us (26%)
  waiting for transfers between devices  10.5 us (26%)
  between operations  0.74 us (2%)
    ppermute x10, starting transfers between devices, exchange(): return lax.ppermute(value, 'tensor', [(i, i ^ step) for i in range(tensor)])  17.8 us
    ppermute x10, waiting for transfers between devices, exchange(): return lax.ppermute(value, 'tensor', [(i, i ^ step) for i in range(tensor)])  9.49 us
    pallas_call x3, Pallas kernels, project(): call(functools.partial(project_kernel, tensor, chunk, steps, len(ready),...  7.88 us
    pallas_call x1, Pallas kernels, prefetch(): call(functools.partial(prefetch_kernel, tensor, chunk, steps), [HBM, HBM]...  1.59 us
    ppermute x3, waiting for transfers between devices, chip_products(): return (keep, lax.ppermute(give, 'seq', swap), *later)  0.99 us
    pallas_call x1, Pallas kernels, normalize(): call(functools.partial(norm_kernel, rows, block, counts, gains[0].shape[0...  0.99 us
  transfers between devices with their start and end apart: 14, of which 5 were waited for; matrix products, arithmetic and copies ran while one was open for 0% of the time, Pallas kernels for 13%

profile of v6, /device:TPU:0, one launch (start us, length us, event | category | flops | bytes accessed | tf_op | source)
XLA Modules:
  0.0 40.9 jit_solution(1168189550867852250)
XLA Ops:
  0.6 0.6 %collective-permute-start = (bf16[32,2048]{1,0:T(8,128)(2,1)}, bf16[32,2048]{1,0:T(8,128)(2,1)S(1)}, u32[]{:S(2)}, u32[]{:S(2)}) collective-permute-start(bf16[32,2048]{1,0:T(8,128)(2,1)} %own_hbm.1), channel_id=1, source_target_pairs={{0,1},{1,0},{2,3},{3,2},{4,5},{5,4},{6,7},{7,6},{8,9},{9,8},{10,11... | collective-permute-start | bytes 393224 | tf_op jit(solution)/shard_map/ppermute | solution.py:282
  1.2 1.6 %shard_map.59 = (bf16[32,1024]{1,0:T(8,128)(2,1)S(1)}, bf16[2,1024,512]{2,1,0:T(8,128)(2,1)S(1)}) custom-call(bf16[32,2048]{1,0:T(8,128)(2,1)} %own_hbm.1, bf16[1024,8192]{1,0:T(8,128)(2,1)} %refs_0_.1), custom_call_target="tpu_custom_call" | custom-call | tf_op jit(solution)/shard_map/pallas_call | solution.py:97
  2.8 4.5 %shard_map.60 = (f32[2,32,2048]{2,1,0:T(8,128)S(1)}, bf16[2,32,2048]{2,1,0:T(8,128)(2,1)S(1)}, bf16[4,1024,512]{2,1,0:T(8,128)(2,1)S(1)}) custom-call(bf16[32,1024]{1,0:T(8,128)(2,1)S(1)} %get-tuple-element.23.own_ref, bf16[32,2048]{1,0:T(8,128)(2,1)S(1)} %collective-permute-done.peer_ref, bf16[2,1024,512]{2,1,0:T(8,128)(2,1)S(1)} %get-tuple-element.20.refs_0_, ...), custom_call_target="tpu_custom_call" | custom-call | tf_op jit(solution)/shard_map/pallas_call | solution.py:124
  7.3 0.1 collective-permute-start.3
  7.4 0.8 %shard_map.61 = (f32[1,32,2048]{2,1,0:T(8,128)S(1)}, bf16[1,32,2048]{2,1,0:T(8,128)(2,1)S(1)}) custom-call(bf16[32,1024]{1,0:T(8,128)(2,1)S(1)} %get-tuple-element.23.own_ref, bf16[32,2048]{1,0:T(8,128)(2,1)S(1)} %collective-permute-done.peer_ref, bf16[4,1024,512]{2,1,0:T(8,128)(2,1)S(1)} %get-tuple-element.21.refs_0_, bf16[1024,8192]{1,0:T(8,128)(2,1)} %refs_0_.1), custom_call_target="tpu_custom_call" | custom-call | tf_op jit(solution)/shard_map/pallas_call | solution.py:124
  8.2 0.5 %collective-permute-start.1 = (bf16[1,32,2048]{2,1,0:T(8,128)(2,1)S(1)}, bf16[1,32,2048]{2,1,0:T(8,128)(2,1)S(1)}, u32[]{:S(2)}, u32[]{:S(2)}) collective-permute-start(bf16[1,32,2048]{2,1,0:T(8,128)(2,1)S(1)} %get-tuple-element.22), channel_id=1, source_target_pairs={{0,1},{1,0},{2,3},{3,2},{4,5},{5,4},{6,7},{7,6},{8,9},{9,8},{10,11... | collective-permute-start | bytes 393224 | tf_op jit(solution)/shard_map/ppermute | solution.py:280
  8.8 1.0 %collective-permute-done.1.got_ref = bf16[1,32,2048]{2,1,0:T(8,128)(2,1)S(1)} collective-permute-done((bf16[1,32,2048]{2,1,0:T(8,128)(2,1)S(1)}, bf16[1,32,2048]{2,1,0:T(8,128)(2,1)S(1)}, u32[]{:S(2)}, u32[]{:S(2)}) %collective-permute-start.1) | collective-permute-done | bytes 131104 | tf_op jit(solution)/shard_map/ppermute | solution.py:280
  9.8 3.0 %collective-permute-start.6 = (bf16[528,128]{1,0:T(8,128)(2,1)S(1)}, bf16[528,128]{1,0:T(8,128)(2,1)S(1)}, u32[]{:S(2)}, u32[]{:S(2)}) collective-permute-start(bf16[528,128]{1,0:T(8,128)(2,1)S(1)} %shard_map.64), channel_id=1, source_target_pairs={{0,4},{4,0},{8,12},{12,8},{1,5},{5,1},{9,13},{13,9},{2,6},{6,2},{1... | collective-permute-start | bytes 405512 | tf_op jit(solution)/shard_map/ppermute | solution.py:259
  12.8 2.5 %shard_map.62 = (f32[1,32,2048]{2,1,0:T(8,128)S(1)}, bf16[1,32,2048]{2,1,0:T(8,128)(2,1)S(1)}) custom-call(bf16[32,1024]{1,0:T(8,128)(2,1)S(1)} %get-tuple-element.23.own_ref, bf16[32,2048]{1,0:T(8,128)(2,1)S(1)} %collective-permute-done.peer_ref, bf16[1024,8192]{1,0:T(8,128)(2,1)} %refs_0_.1), custom_call_target="tpu_custom_call" | custom-call | tf_op jit(solution)/shard_map/pallas_call | solution.py:124
  15.4 0.1 collective-permute-start.2
  15.5 0.2 collective-permute-start.7
  15.7 2.9 %collective-permute-start.4 = (bf16[272,128]{1,0:T(8,128)(2,1)S(1)}, bf16[272,128]{1,0:T(8,128)(2,1)S(1)}, u32[]{:S(2)}, u32[]{:S(2)}) collective-permute-start(bf16[272,128]{1,0:T(8,128)(2,1)S(1)} %get-tuple-element.29), channel_id=1, source_target_pairs={{0,8},{4,12},{8,0},{12,4},{1,9},{5,13},{9,1},{13,5},{2,10},{6,14},... | collective-permute-start | bytes 208904 | tf_op jit(solution)/shard_map/ppermute | solution.py:259
  18.6 1.4 %collective-permute-start.5 = (bf16[272,128]{1,0:T(8,128)(2,1)S(1)}, bf16[272,128]{1,0:T(8,128)(2,1)S(1)}, u32[]{:S(2)}, u32[]{:S(2)}) collective-permute-start(bf16[272,128]{1,0:T(8,128)(2,1)S(1)} %get-tuple-element.30), channel_id=1, source_target_pairs={{0,12},{4,8},{8,4},{12,0},{1,13},{5,9},{9,5},{13,1},{2,14},{6,10},... | collective-permute-start | bytes 208904 | tf_op jit(solution)/shard_map/ppermute | solution.py:259
  20.0 1.6 %collective-permute-done.7.got_ref = bf16[256,128]{1,0:T(8,128)(2,1)S(1)} collective-permute-done((bf16[256,128]{1,0:T(8,128)(2,1)S(1)}, bf16[256,128]{1,0:T(8,128)(2,1)S(1)}, u32[]{:S(2)}, u32[]{:S(2)}) %collective-permute-start.7) | collective-permute-done | bytes 65568 | tf_op jit(solution)/shard_map/ppermute | solution.py:259
  21.6 1.6 %collective-permute-start.8 = (bf16[256,128]{1,0:T(8,128)(2,1)S(1)}, bf16[256,128]{1,0:T(8,128)(2,1)S(1)}, u32[]{:S(2)}, u32[]{:S(2)}) collective-permute-start(bf16[256,128]{1,0:T(8,128)(2,1)S(1)} %shard_map.65), channel_id=1, source_target_pairs={{0,8},{4,12},{8,0},{12,4},{1,9},{5,13},{9,1},{13,5},{2,10},{6,14},... | collective-permute-start | bytes 196616 | tf_op jit(solution)/shard_map/ppermute | solution.py:259
  23.2 2.4 %collective-permute-done.5.refs_1_.refs_9_ = bf16[272,128]{1,0:T(8,128)(2,1)S(1)} collective-permute-done((bf16[272,128]{1,0:T(8,128)(2,1)S(1)}, bf16[272,128]{1,0:T(8,128)(2,1)S(1)}, u32[]{:S(2)}, u32[]{:S(2)}) %collective-permute-start.5) | collective-permute-done | bytes 69664 | tf_op jit(solution)/shard_map/ppermute | solution.py:259
  25.7 4.2 %collective-permute-start.11 = (bf16[256,128]{1,0:T(8,128)(2,1)S(1)}, bf16[256,128]{1,0:T(8,128)(2,1)S(1)}, u32[]{:S(2)}, u32[]{:S(2)}) collective-permute-start(bf16[256,128]{1,0:T(8,128)(2,1)S(1)} %shard_map.66.refs_4_), channel_id=1, source_target_pairs={{0,8},{4,12},{8,0},{12,4},{1,9},{5,13},{9,1},{13,5},{2,10},{6,14},... | collective-permute-start | bytes 196616 | tf_op jit(solution)/shard_map/ppermute | solution.py:259
  29.9 0.1 collective-permute-start.9
  30.0 2.2 %collective-permute-start.12 = (bf16[256,128]{1,0:T(8,128)(2,1)S(1)}, bf16[256,128]{1,0:T(8,128)(2,1)S(1)}, u32[]{:S(2)}, u32[]{:S(2)}) collective-permute-start(bf16[256,128]{1,0:T(8,128)(2,1)S(1)} %get-tuple-element.35), channel_id=1, source_target_pairs={{0,12},{4,8},{8,4},{12,0},{1,13},{5,9},{9,5},{13,1},{2,14},{6,10},... | collective-permute-start | bytes 196616 | tf_op jit(solution)/shard_map/ppermute | solution.py:259
  32.2 1.3 %collective-permute-start.10 = (bf16[256,128]{1,0:T(8,128)(2,1)S(1)}, bf16[256,128]{1,0:T(8,128)(2,1)S(1)}, u32[]{:S(2)}, u32[]{:S(2)}) collective-permute-start(bf16[256,128]{1,0:T(8,128)(2,1)S(1)} %get-tuple-element.35), channel_id=1, source_target_pairs={{0,8},{4,12},{8,0},{12,4},{1,9},{5,13},{9,1},{13,5},{2,10},{6,14},... | collective-permute-start | bytes 196616 | tf_op jit(solution)/shard_map/ppermute | solution.py:259
  33.5 1.0 %collective-permute-start.13 = (bf16[256,128]{1,0:T(8,128)(2,1)S(1)}, bf16[256,128]{1,0:T(8,128)(2,1)S(1)}, u32[]{:S(2)}, u32[]{:S(2)}) collective-permute-start(bf16[256,128]{1,0:T(8,128)(2,1)S(1)} %collective-permute-done.11.refs_3_), channel_id=1, source_target_pairs={{0,4},{4,0},{8,12},{12,8},{1,5},{5,1},{9,13},{13,9},{2,6},{6,2},{1... | collective-permute-start | bytes 196616 | tf_op jit(solution)/shard_map/ppermute | solution.py:259
  34.5 3.6 %collective-permute-done.12.refs_4_ = bf16[256,128]{1,0:T(8,128)(2,1)S(1)} collective-permute-done((bf16[256,128]{1,0:T(8,128)(2,1)S(1)}, bf16[256,128]{1,0:T(8,128)(2,1)S(1)}, u32[]{:S(2)}, u32[]{:S(2)}) %collective-permute-start.12) | collective-permute-done | bytes 65568 | tf_op jit(solution)/shard_map/ppermute | solution.py:259
  38.0 1.9 %collective-permute-done.10.refs_2_ = bf16[256,128]{1,0:T(8,128)(2,1)S(1)} collective-permute-done((bf16[256,128]{1,0:T(8,128)(2,1)S(1)}, bf16[256,128]{1,0:T(8,128)(2,1)S(1)}, u32[]{:S(2)}, u32[]{:S(2)}) %collective-permute-start.10) | collective-permute-done | bytes 65568 | tf_op jit(solution)/shard_map/ppermute | solution.py:259
  39.9 1.0 %shard_map.68 = (bf16[32,2048]{1,0:T(8,128)(2,1)}, bf16[32,8192]{1,0:T(8,128)(2,1)}) custom-call(bf16[512,128]{1,0:T(8,128)(2,1)S(1)} %get-tuple-element.34.refs_0_, bf16[512,128]{1,0:T(8,128)(2,1)S(1)} %collective-permute-done.9.refs_1_, bf16[256,128]{1,0:T(8,128)(2,1)S(1)} %collective-permute-done.10.refs_2_, ...), custom_call_target="tpu_custom_call" | custom-call | tf_op jit(solution)/shard_map/pallas_call | solution.py:236
  (18 shorter events, 0.2 us)
Async XLA Ops:
  0.6 2.2 %collective-permute-start = (bf16[32,2048]{1,0:T(8,128)(2,1)}, bf16[32,2048]{1,0:T(8,128)(2,1)S(1)}, u32[]{:S(2)}, u32[]{:S(2)}) collective-permute-start(bf16[32,2048]{1,0:T(8,128)(2,1)} %own_hbm.1), channel_id=1, source_target_pairs={{0,1},{1,0},{2,3},{3,2},{4,5},{5,4},{6,7},{7,6},{8,9},{9,8},{10,11... | collective-permute-start | bytes 393224 | tf_op jit(solution)/shard_map/ppermute | solution.py:282
  7.3 8.1 %collective-permute-start.3 = (bf16[2,32,2048]{2,1,0:T(8,128)(2,1)S(1)}, bf16[2,32,2048]{2,1,0:T(8,128)(2,1)S(1)}, u32[]{:S(2)}, u32[]{:S(2)}) collective-permute-start(bf16[2,32,2048]{2,1,0:T(8,128)(2,1)S(1)} %get-tuple-element.28), channel_id=1, source_target_pairs={{0,1},{1,0},{2,3},{3,2},{4,5},{5,4},{6,7},{7,6},{8,9},{9,8},{10,11... | collective-permute-start | bytes 786440 | tf_op jit(solution)/shard_map/ppermute | solution.py:280
  7.4 2.4 %copy-start.1 = (bf16[2048]{0:T(1024)(128)(2,1)S(1)}, bf16[2048]{0:T(1024)(128)(2,1)}, u32[]{:S(2)}) copy-start(bf16[2048]{0:T(1024)(128)(2,1)} %param.7) | copy-start | bytes 12292
  8.2 1.5 %collective-permute-start.1 = (bf16[1,32,2048]{2,1,0:T(8,128)(2,1)S(1)}, bf16[1,32,2048]{2,1,0:T(8,128)(2,1)S(1)}, u32[]{:S(2)}, u32[]{:S(2)}) collective-permute-start(bf16[1,32,2048]{2,1,0:T(8,128)(2,1)S(1)} %get-tuple-element.22), channel_id=1, source_target_pairs={{0,1},{1,0},{2,3},{3,2},{4,5},{5,4},{6,7},{7,6},{8,9},{9,8},{10,11... | collective-permute-start | bytes 393224 | tf_op jit(solution)/shard_map/ppermute | solution.py:280
  9.8 15.8 %copy-start = (bf16[32,2048]{1,0:T(8,128)(2,1)S(1)}, bf16[32,2048]{1,0:T(8,128)(2,1)}, u32[]{:S(2)}) copy-start(bf16[32,2048]{1,0:T(8,128)(2,1)} %residual_ref.3) | copy-start | bytes 393220
  9.8 13.4 %collective-permute-start.6 = (bf16[528,128]{1,0:T(8,128)(2,1)S(1)}, bf16[528,128]{1,0:T(8,128)(2,1)S(1)}, u32[]{:S(2)}, u32[]{:S(2)}) collective-permute-start(bf16[528,128]{1,0:T(8,128)(2,1)S(1)} %shard_map.64), channel_id=1, source_target_pairs={{0,4},{4,0},{8,12},{12,8},{1,5},{5,1},{9,13},{13,9},{2,6},{6,2},{1... | collective-permute-start | bytes 405512 | tf_op jit(solution)/shard_map/ppermute | solution.py:259
  15.4 7.8 %collective-permute-start.2 = (bf16[1,32,2048]{2,1,0:T(8,128)(2,1)S(1)}, bf16[1,32,2048]{2,1,0:T(8,128)(2,1)S(1)}, u32[]{:S(2)}, u32[]{:S(2)}) collective-permute-start(bf16[1,32,2048]{2,1,0:T(8,128)(2,1)S(1)} %get-tuple-element.26), channel_id=1, source_target_pairs={{0,1},{1,0},{2,3},{3,2},{4,5},{5,4},{6,7},{7,6},{8,9},{9,8},{10,11... | collective-permute-start | bytes 393224 | tf_op jit(solution)/shard_map/ppermute | solution.py:280
  15.5 6.0 %collective-permute-start.7 = (bf16[256,128]{1,0:T(8,128)(2,1)S(1)}, bf16[256,128]{1,0:T(8,128)(2,1)S(1)}, u32[]{:S(2)}, u32[]{:S(2)}) collective-permute-start(bf16[256,128]{1,0:T(8,128)(2,1)S(1)} %get-tuple-element.33), channel_id=1, source_target_pairs={{0,4},{4,0},{8,12},{12,8},{1,5},{5,1},{9,13},{13,9},{2,6},{6,2},{1... | collective-permute-start | bytes 196616 | tf_op jit(solution)/shard_map/ppermute | solution.py:259
  15.7 7.5 %collective-permute-start.4 = (bf16[272,128]{1,0:T(8,128)(2,1)S(1)}, bf16[272,128]{1,0:T(8,128)(2,1)S(1)}, u32[]{:S(2)}, u32[]{:S(2)}) collective-permute-start(bf16[272,128]{1,0:T(8,128)(2,1)S(1)} %get-tuple-element.29), channel_id=1, source_target_pairs={{0,8},{4,12},{8,0},{12,4},{1,9},{5,13},{9,1},{13,5},{2,10},{6,14},... | collective-permute-start | bytes 208904 | tf_op jit(solution)/shard_map/ppermute | solution.py:259
  18.6 7.0 %collective-permute-start.5 = (bf16[272,128]{1,0:T(8,128)(2,1)S(1)}, bf16[272,128]{1,0:T(8,128)(2,1)S(1)}, u32[]{:S(2)}, u32[]{:S(2)}) collective-permute-start(bf16[272,128]{1,0:T(8,128)(2,1)S(1)} %get-tuple-element.30), channel_id=1, source_target_pairs={{0,12},{4,8},{8,4},{12,0},{1,13},{5,9},{9,5},{13,1},{2,14},{6,10},... | collective-permute-start | bytes 208904 | tf_op jit(solution)/shard_map/ppermute | solution.py:259
  21.6 8.3 %collective-permute-start.8 = (bf16[256,128]{1,0:T(8,128)(2,1)S(1)}, bf16[256,128]{1,0:T(8,128)(2,1)S(1)}, u32[]{:S(2)}, u32[]{:S(2)}) collective-permute-start(bf16[256,128]{1,0:T(8,128)(2,1)S(1)} %shard_map.65), channel_id=1, source_target_pairs={{0,8},{4,12},{8,0},{12,4},{1,9},{5,13},{9,1},{13,5},{2,10},{6,14},... | collective-permute-start | bytes 196616 | tf_op jit(solution)/shard_map/ppermute | solution.py:259
  25.7 7.8 %collective-permute-start.11 = (bf16[256,128]{1,0:T(8,128)(2,1)S(1)}, bf16[256,128]{1,0:T(8,128)(2,1)S(1)}, u32[]{:S(2)}, u32[]{:S(2)}) collective-permute-start(bf16[256,128]{1,0:T(8,128)(2,1)S(1)} %shard_map.66.refs_4_), channel_id=1, source_target_pairs={{0,8},{4,12},{8,0},{12,4},{1,9},{5,13},{9,1},{13,5},{2,10},{6,14},... | collective-permute-start | bytes 196616 | tf_op jit(solution)/shard_map/ppermute | solution.py:259
  29.9 10.0 %collective-permute-start.9 = (bf16[512,128]{1,0:T(8,128)(2,1)S(1)}, bf16[512,128]{1,0:T(8,128)(2,1)S(1)}, u32[]{:S(2)}, u32[]{:S(2)}) collective-permute-start(bf16[512,128]{1,0:T(8,128)(2,1)S(1)} %get-tuple-element.34.refs_0_), channel_id=1, source_target_pairs={{0,4},{4,0},{8,12},{12,8},{1,5},{5,1},{9,13},{13,9},{2,6},{6,2},{1... | collective-permute-start | bytes 393224 | tf_op jit(solution)/shard_map/ppermute | solution.py:259
  30.0 8.0 %collective-permute-start.12 = (bf16[256,128]{1,0:T(8,128)(2,1)S(1)}, bf16[256,128]{1,0:T(8,128)(2,1)S(1)}, u32[]{:S(2)}, u32[]{:S(2)}) collective-permute-start(bf16[256,128]{1,0:T(8,128)(2,1)S(1)} %get-tuple-element.35), channel_id=1, source_target_pairs={{0,12},{4,8},{8,4},{12,0},{1,13},{5,9},{9,5},{13,1},{2,14},{6,10},... | collective-permute-start | bytes 196616 | tf_op jit(solution)/shard_map/ppermute | solution.py:259
  32.2 7.8 %collective-permute-start.10 = (bf16[256,128]{1,0:T(8,128)(2,1)S(1)}, bf16[256,128]{1,0:T(8,128)(2,1)S(1)}, u32[]{:S(2)}, u32[]{:S(2)}) collective-permute-start(bf16[256,128]{1,0:T(8,128)(2,1)S(1)} %get-tuple-element.35), channel_id=1, source_target_pairs={{0,8},{4,12},{8,0},{12,4},{1,9},{5,13},{9,1},{13,5},{2,10},{6,14},... | collective-permute-start | bytes 196616 | tf_op jit(solution)/shard_map/ppermute | solution.py:259
  33.5 6.5 %collective-permute-start.13 = (bf16[256,128]{1,0:T(8,128)(2,1)S(1)}, bf16[256,128]{1,0:T(8,128)(2,1)S(1)}, u32[]{:S(2)}, u32[]{:S(2)}) collective-permute-start(bf16[256,128]{1,0:T(8,128)(2,1)S(1)} %collective-permute-done.11.refs_3_), channel_id=1, source_target_pairs={{0,4},{4,0},{8,12},{12,8},{1,5},{5,1},{9,13},{13,9},{2,6},{6,2},{1... | collective-permute-start | bytes 196616 | tf_op jit(solution)/shard_map/ppermute | solution.py:259

commit v7 on v6

--- a/solution.py
+++ b/solution.py
@@ -14,6 +14,8 @@
 LANES = 128
 READY = 2
 LATER = 4
+LAST = 1
+HALF = 8
 CHUNK = 512
 
 
@@ -54,7 +56,7 @@
 
 
 def project_kernel(tensor, chunk, steps, early, after, own_ref, peer_ref, *refs):
-    ready_refs, (weight, keep_ref, give_ref, *later_refs, held, sems) = refs[:early], refs[early:]
+    ready_refs, (weight, keep_ref, give_ref, *later_refs, held, sems, fence) = refs[:early], refs[early:]
     depth, width = weight.shape
     block = width // tensor
     per_block = block // chunk
@@ -67,6 +69,8 @@
         later = [copy(later_refs[0].at[i], sems.at[len(copies) + i]) for i, copy in enumerate(later)]
     for copy in copies + later:
         copy.start()
+    pl.semaphore_signal(fence, 1)
+    pl.semaphore_wait(fence, 1)
     features = pl.ds(pl.multiple_of(lax.axis_index("seq") * depth, LANES), depth)
     rows = own_ref.shape[0]
     operand = jnp.concatenate([own_ref[...], peer_ref[:, features]], axis=0)
@@ -114,7 +118,8 @@
     ready = [] if ready is None else [ready]
     early = ready[0].shape[0] if ready else 0
     count = len(steps) * block // chunk - early
-    later = min(LATER * MIB // (2 * depth * chunk), len(after) * block // chunk)
+    fetched = LATER if len(steps) > 1 else LAST
+    later = min(fetched * MIB // (2 * depth * chunk), len(after) * block // chunk)
     shapes = [
         jax.ShapeDtypeStruct((len(steps), rows, block), F32),
         jax.ShapeDtypeStruct((len(steps), rows, block), BF16),
@@ -126,7 +131,7 @@
         [VMEM] * (2 + len(ready)) + [HBM],
         shapes,
         2 * depth * chunk * (len(steps) * block // chunk + later) + 4 * MIB,
-        [VMEM((count, depth, chunk), BF16), pltpu.SemaphoreType.DMA((count + later,))],
+        [VMEM((count, depth, chunk), BF16), pltpu.SemaphoreType.DMA((count + later,)), pltpu.SemaphoreType.REGULAR(())],
     )(own, peer, *ready, pltpu.with_memory_space_constraint(weight, HBM))
 
 
@@ -193,13 +198,11 @@
 
 def norm_kernel(rows, block, counts, gain_rows, *refs):
     tensor = len(counts)
-    tiles = block // LANES
     refs = list(refs)
     pieces = []
     for count in counts:
         group = [refs.pop(0) for _ in range(count)]
-        size = tiles // count
-        pieces.append([(group[tile // size], tile % size) for tile in range(tiles)])
+        pieces.append([(ref, tile) for ref in group for tile in range(ref.shape[0] // rows)])
     gains, (stream_hbm, out_hbm, stream_ref, out_ref, sems) = refs[:tensor], refs[tensor:]
     rank = lax.axis_index("tensor")
     copies = [pltpu.make_async_copy(stream_ref, stream_hbm, sems.at[tensor])]
@@ -262,7 +265,7 @@
     gain = jnp.pad(gain, ((0, -gain.shape[0] % 16), (0, 0)))
     relay = tensor == 4
     tiles = block // LANES
-    half = tiles // 2
+    half = tiles * HALF // 16
     parts = []
     spans = []
     gains = [gain] + [None] * (tensor - 1)
@@ -284,14 +287,15 @@
     near_steps = list(range(tensor // 2 - 1, 0, -1))
     own, ready = prefetch(attn_heads, out_weight, tensor, far_steps)
     keep, got, ready = chip_products(far_steps, None, ready, near_steps)
-    keep_near, got_near = chip_products(near_steps, None, ready)
+    keep_near, got_near, *ready = chip_products(near_steps, None, ready, [0])
+    ready = ready[0] if ready else None
     if not relay:
         for wave, steps in enumerate((far_steps, near_steps)):
             plan = [(place, 0, tiles, True, BF16) for place in range(len(steps))]
             sums = pair_sum(plan, *((keep, got), (keep_near, got_near))[wave], gain)
             for step, value in zip(steps, sums):
                 gains[step] = receive(exchange(value, step), 0, tiles)
-        keep, got = chip_products([0], got_near)
+        keep, got = chip_products([0], got_near, ready)
         stream = finish_stream(keep, got, residual, parts, spans, 0, tiles)[0]
         pieces = [[stream]] + [[exchange(stream, step)] for step in range(1, tensor)]
         return normalize(pieces, gains, rows, block)
@@ -307,7 +311,7 @@
     gains[3] = receive(exchange(far, 3), half, tiles)
     beside = pair_sum([(0, 0, tiles, True, BF16)], keep_near, got_near, gain)[0]
     gains[1] = receive(exchange(beside, 1), 0, tiles)
-    keep, got = chip_products([0], got_near)
+    keep, got = chip_products([0], got_near, ready)
     through = relay_sum(mine, relayed)
     last = exchange(through, 2)
     second = finish_stream(keep, got, residual, parts, spans, half, tiles)[0]

time: 41.1 us -> 40.9 us (level)
  no operation moved by 1% of the time
where the time goes in v7:
time: 40.9 us; the launch traced here: 40.7 us
  starting transfers between devices  19 us (46%)
  Pallas kernels  10.5 us (26%)
  waiting for transfers between devices  10.5 us (26%)
  between operations  0.73 us (2%)
    ppermute x10, starting transfers between devices, exchange(): return lax.ppermute(value, 'tensor', [(i, i ^ step) for i in range(tensor)])  17.8 us
    ppermute x10, waiting for transfers between devices, exchange(): return lax.ppermute(value, 'tensor', [(i, i ^ step) for i in range(tensor)])  9.49 us
    pallas_call x3, Pallas kernels, project(): call(functools.partial(project_kernel, tensor, chunk, steps, len(ready),...  7.68 us
    pallas_call x1, Pallas kernels, prefetch(): call(functools.partial(prefetch_kernel, tensor, chunk, steps), [HBM, HBM]...  1.59 us
    ppermute x3, waiting for transfers between devices, chip_products(): return (keep, lax.ppermute(give, 'seq', swap), *later)  0.99 us
    pallas_call x1, Pallas kernels, normalize(): call(functools.partial(norm_kernel, rows, block, counts, gains[0].shape[0...  0.99 us
  transfers between devices with their start and end apart: 14, of which 5 were waited for; matrix products, arithmetic and copies ran while one was open for 0% of the time, Pallas kernels for 13%

profile of v7, /device:TPU:0, one launch (start us, length us, event | category | flops | bytes accessed | tf_op | source)
XLA Modules:
  0.0 40.7 jit_solution(12587805976199855209)
XLA Ops:
  0.6 0.6 %collective-permute-start = (bf16[32,2048]{1,0:T(8,128)(2,1)}, bf16[32,2048]{1,0:T(8,128)(2,1)S(1)}, u32[]{:S(2)}, u32[]{:S(2)}) collective-permute-start(bf16[32,2048]{1,0:T(8,128)(2,1)} %own_hbm.1), channel_id=1, source_target_pairs={{0,1},{1,0},{2,3},{3,2},{4,5},{5,4},{6,7},{7,6},{8,9},{9,8},{10,11... | collective-permute-start | bytes 393224 | tf_op jit(solution)/shard_map/ppermute | solution.py:285
  1.2 1.6 %shard_map.59 = (bf16[32,1024]{1,0:T(8,128)(2,1)S(1)}, bf16[2,1024,512]{2,1,0:T(8,128)(2,1)S(1)}) custom-call(bf16[32,2048]{1,0:T(8,128)(2,1)} %own_hbm.1, bf16[1024,8192]{1,0:T(8,128)(2,1)} %refs_1_.5), custom_call_target="tpu_custom_call" | custom-call | tf_op jit(solution)/shard_map/pallas_call | solution.py:101
  2.8 4.2 %shard_map.60 = (f32[2,32,2048]{2,1,0:T(8,128)S(1)}, bf16[2,32,2048]{2,1,0:T(8,128)(2,1)S(1)}, bf16[4,1024,512]{2,1,0:T(8,128)(2,1)S(1)}) custom-call(bf16[32,1024]{1,0:T(8,128)(2,1)S(1)} %get-tuple-element.24.own_ref, bf16[32,2048]{1,0:T(8,128)(2,1)S(1)} %collective-permute-done.peer_ref, bf16[2,1024,512]{2,1,0:T(8,128)(2,1)S(1)} %get-tuple-element.21.refs_0_, ...), custom_call_target="tpu_custom_call" | custom-call | tf_op jit(solution)/shard_map/pallas_call | solution.py:129
  7.0 0.1 collective-permute-start.3
  7.1 1.3 %shard_map.61 = (f32[1,32,2048]{2,1,0:T(8,128)S(1)}, bf16[1,32,2048]{2,1,0:T(8,128)(2,1)S(1)}, bf16[1,1024,512]{2,1,0:T(8,128)(2,1)S(1)}) custom-call(bf16[32,1024]{1,0:T(8,128)(2,1)S(1)} %get-tuple-element.24.own_ref, bf16[32,2048]{1,0:T(8,128)(2,1)S(1)} %collective-permute-done.peer_ref, bf16[4,1024,512]{2,1,0:T(8,128)(2,1)S(1)} %get-tuple-element.22.refs_0_, ...), custom_call_target="tpu_custom_call" | custom-call | tf_op jit(solution)/shard_map/pallas_call | solution.py:129
  8.4 0.5 %collective-permute-start.1 = (bf16[1,32,2048]{2,1,0:T(8,128)(2,1)S(1)}, bf16[1,32,2048]{2,1,0:T(8,128)(2,1)S(1)}, u32[]{:S(2)}, u32[]{:S(2)}) collective-permute-start(bf16[1,32,2048]{2,1,0:T(8,128)(2,1)S(1)} %get-tuple-element.23), channel_id=1, source_target_pairs={{0,1},{1,0},{2,3},{3,2},{4,5},{5,4},{6,7},{7,6},{8,9},{9,8},{10,11... | collective-permute-start | bytes 393224 | tf_op jit(solution)/shard_map/ppermute | solution.py:283
  8.9 1.0 %collective-permute-done.1.got_ref = bf16[1,32,2048]{2,1,0:T(8,128)(2,1)S(1)} collective-permute-done((bf16[1,32,2048]{2,1,0:T(8,128)(2,1)S(1)}, bf16[1,32,2048]{2,1,0:T(8,128)(2,1)S(1)}, u32[]{:S(2)}, u32[]{:S(2)}) %collective-permute-start.1) | collective-permute-done | bytes 131104 | tf_op jit(solution)/shard_map/ppermute | solution.py:283
  9.9 3.0 %collective-permute-start.6 = (bf16[528,128]{1,0:T(8,128)(2,1)S(1)}, bf16[528,128]{1,0:T(8,128)(2,1)S(1)}, u32[]{:S(2)}, u32[]{:S(2)}) collective-permute-start(bf16[528,128]{1,0:T(8,128)(2,1)S(1)} %shard_map.64), channel_id=1, source_target_pairs={{0,4},{4,0},{8,12},{12,8},{1,5},{5,1},{9,13},{13,9},{2,6},{6,2},{1... | collective-permute-start | bytes 405512 | tf_op jit(solution)/shard_map/ppermute | solution.py:262
  12.9 2.2 %shard_map.62 = (f32[1,32,2048]{2,1,0:T(8,128)S(1)}, bf16[1,32,2048]{2,1,0:T(8,128)(2,1)S(1)}) custom-call(bf16[32,1024]{1,0:T(8,128)(2,1)S(1)} %get-tuple-element.24.own_ref, bf16[32,2048]{1,0:T(8,128)(2,1)S(1)} %collective-permute-done.peer_ref, bf16[1,1024,512]{2,1,0:T(8,128)(2,1)S(1)} %get-tuple-element.26.refs_0_, bf16[1024,8192]{1,0:T(8,128)(2,1)} %refs_1_.5), custom_call_target="tpu_custom_call" | custom-call | tf_op jit(solution)/shard_map/pallas_call | solution.py:129
  15.2 0.1 collective-permute-start.2
  15.3 0.2 collective-permute-start.7
  15.5 2.9 %collective-permute-start.4 = (bf16[272,128]{1,0:T(8,128)(2,1)S(1)}, bf16[272,128]{1,0:T(8,128)(2,1)S(1)}, u32[]{:S(2)}, u32[]{:S(2)}) collective-permute-start(bf16[272,128]{1,0:T(8,128)(2,1)S(1)} %get-tuple-element.31), channel_id=1, source_target_pairs={{0,8},{4,12},{8,0},{12,4},{1,9},{5,13},{9,1},{13,5},{2,10},{6,14},... | collective-permute-start | bytes 208904 | tf_op jit(solution)/shard_map/ppermute | solution.py:262
  18.4 1.3 %collective-permute-start.5 = (bf16[272,128]{1,0:T(8,128)(2,1)S(1)}, bf16[272,128]{1,0:T(8,128)(2,1)S(1)}, u32[]{:S(2)}, u32[]{:S(2)}) collective-permute-start(bf16[272,128]{1,0:T(8,128)(2,1)S(1)} %get-tuple-element.32), channel_id=1, source_target_pairs={{0,12},{4,8},{8,4},{12,0},{1,13},{5,9},{9,5},{13,1},{2,14},{6,10},... | collective-permute-start | bytes 208904 | tf_op jit(solution)/shard_map/ppermute | solution.py:262
  19.8 1.6 %collective-permute-done.7.got_ref = bf16[256,128]{1,0:T(8,128)(2,1)S(1)} collective-permute-done((bf16[256,128]{1,0:T(8,128)(2,1)S(1)}, bf16[256,128]{1,0:T(8,128)(2,1)S(1)}, u32[]{:S(2)}, u32[]{:S(2)}) %collective-permute-start.7) | collective-permute-done | bytes 65568 | tf_op jit(solution)/shard_map/ppermute | solution.py:262
  21.4 1.6 %collective-permute-start.8 = (bf16[256,128]{1,0:T(8,128)(2,1)S(1)}, bf16[256,128]{1,0:T(8,128)(2,1)S(1)}, u32[]{:S(2)}, u32[]{:S(2)}) collective-permute-start(bf16[256,128]{1,0:T(8,128)(2,1)S(1)} %shard_map.65), channel_id=1, source_target_pairs={{0,8},{4,12},{8,0},{12,4},{1,9},{5,13},{9,1},{13,5},{2,10},{6,14},... | collective-permute-start | bytes 196616 | tf_op jit(solution)/shard_map/ppermute | solution.py:262
  23.0 2.4 %collective-permute-done.5.refs_1_.refs_9_ = bf16[272,128]{1,0:T(8,128)(2,1)S(1)} collective-permute-done((bf16[272,128]{1,0:T(8,128)(2,1)S(1)}, bf16[272,128]{1,0:T(8,128)(2,1)S(1)}, u32[]{:S(2)}, u32[]{:S(2)}) %collective-permute-start.5) | collective-permute-done | bytes 69664 | tf_op jit(solution)/shard_map/ppermute | solution.py:262
  25.5 4.2 %collective-permute-start.11 = (bf16[256,128]{1,0:T(8,128)(2,1)S(1)}, bf16[256,128]{1,0:T(8,128)(2,1)S(1)}, u32[]{:S(2)}, u32[]{:S(2)}) collective-permute-start(bf16[256,128]{1,0:T(8,128)(2,1)S(1)} %shard_map.66.refs_4_), channel_id=1, source_target_pairs={{0,8},{4,12},{8,0},{12,4},{1,9},{5,13},{9,1},{13,5},{2,10},{6,14},... | collective-permute-start | bytes 196616 | tf_op jit(solution)/shard_map/ppermute | solution.py:262
  29.7 0.1 collective-permute-start.9
  29.8 2.2 %collective-permute-start.12 = (bf16[256,128]{1,0:T(8,128)(2,1)S(1)}, bf16[256,128]{1,0:T(8,128)(2,1)S(1)}, u32[]{:S(2)}, u32[]{:S(2)}) collective-permute-start(bf16[256,128]{1,0:T(8,128)(2,1)S(1)} %get-tuple-element.37), channel_id=1, source_target_pairs={{0,12},{4,8},{8,4},{12,0},{1,13},{5,9},{9,5},{13,1},{2,14},{6,10},... | collective-permute-start | bytes 196616 | tf_op jit(solution)/shard_map/ppermute | solution.py:262
  32.0 1.3 %collective-permute-start.10 = (bf16[256,128]{1,0:T(8,128)(2,1)S(1)}, bf16[256,128]{1,0:T(8,128)(2,1)S(1)}, u32[]{:S(2)}, u32[]{:S(2)}) collective-permute-start(bf16[256,128]{1,0:T(8,128)(2,1)S(1)} %get-tuple-element.37), channel_id=1, source_target_pairs={{0,8},{4,12},{8,0},{12,4},{1,9},{5,13},{9,1},{13,5},{2,10},{6,14},... | collective-permute-start | bytes 196616 | tf_op jit(solution)/shard_map/ppermute | solution.py:262
  33.3 1.0 %collective-permute-start.13 = (bf16[256,128]{1,0:T(8,128)(2,1)S(1)}, bf16[256,128]{1,0:T(8,128)(2,1)S(1)}, u32[]{:S(2)}, u32[]{:S(2)}) collective-permute-start(bf16[256,128]{1,0:T(8,128)(2,1)S(1)} %collective-permute-done.11.refs_3_), channel_id=1, source_target_pairs={{0,4},{4,0},{8,12},{12,8},{1,5},{5,1},{9,13},{13,9},{2,6},{6,2},{1... | collective-permute-start | bytes 196616 | tf_op jit(solution)/shard_map/ppermute | solution.py:262
  34.3 3.5 %collective-permute-done.12.refs_4_ = bf16[256,128]{1,0:T(8,128)(2,1)S(1)} collective-permute-done((bf16[256,128]{1,0:T(8,128)(2,1)S(1)}, bf16[256,128]{1,0:T(8,128)(2,1)S(1)}, u32[]{:S(2)}, u32[]{:S(2)}) %collective-permute-start.12) | collective-permute-done | bytes 65568 | tf_op jit(solution)/shard_map/ppermute | solution.py:262
  37.8 1.9 %collective-permute-done.10.refs_2_ = bf16[256,128]{1,0:T(8,128)(2,1)S(1)} collective-permute-done((bf16[256,128]{1,0:T(8,128)(2,1)S(1)}, bf16[256,128]{1,0:T(8,128)(2,1)S(1)}, u32[]{:S(2)}, u32[]{:S(2)}) %collective-permute-start.10) | collective-permute-done | bytes 65568 | tf_op jit(solution)/shard_map/ppermute | solution.py:262
  39.7 1.0 %shard_map.68 = (bf16[32,2048]{1,0:T(8,128)(2,1)}, bf16[32,8192]{1,0:T(8,128)(2,1)}) custom-call(bf16[512,128]{1,0:T(8,128)(2,1)S(1)} %get-tuple-element.36.refs_0_, bf16[512,128]{1,0:T(8,128)(2,1)S(1)} %collective-permute-done.9.refs_1_, bf16[256,128]{1,0:T(8,128)(2,1)S(1)} %collective-permute-done.10.refs_2_, ...), custom_call_target="tpu_custom_call" | custom-call | tf_op jit(solution)/shard_map/pallas_call | solution.py:239
  (18 shorter events, 0.2 us)
Async XLA Ops:
  0.6 2.2 %collective-permute-start = (bf16[32,2048]{1,0:T(8,128)(2,1)}, bf16[32,2048]{1,0:T(8,128)(2,1)S(1)}, u32[]{:S(2)}, u32[]{:S(2)}) collective-permute-start(bf16[32,2048]{1,0:T(8,128)(2,1)} %own_hbm.1), channel_id=1, source_target_pairs={{0,1},{1,0},{2,3},{3,2},{4,5},{5,4},{6,7},{7,6},{8,9},{9,8},{10,11... | collective-permute-start | bytes 393224 | tf_op jit(solution)/shard_map/ppermute | solution.py:285
  7.0 8.2 %collective-permute-start.3 = (bf16[2,32,2048]{2,1,0:T(8,128)(2,1)S(1)}, bf16[2,32,2048]{2,1,0:T(8,128)(2,1)S(1)}, u32[]{:S(2)}, u32[]{:S(2)}) collective-permute-start(bf16[2,32,2048]{2,1,0:T(8,128)(2,1)S(1)} %get-tuple-element.30), channel_id=1, source_target_pairs={{0,1},{1,0},{2,3},{3,2},{4,5},{5,4},{6,7},{7,6},{8,9},{9,8},{10,11... | collective-permute-start | bytes 786440 | tf_op jit(solution)/shard_map/ppermute | solution.py:283
  7.1 2.8 %copy-start.1 = (bf16[2048]{0:T(1024)(128)(2,1)S(1)}, bf16[2048]{0:T(1024)(128)(2,1)}, u32[]{:S(2)}) copy-start(bf16[2048]{0:T(1024)(128)(2,1)} %param.7) | copy-start | bytes 12292
  8.4 1.5 %collective-permute-start.1 = (bf16[1,32,2048]{2,1,0:T(8,128)(2,1)S(1)}, bf16[1,32,2048]{2,1,0:T(8,128)(2,1)S(1)}, u32[]{:S(2)}, u32[]{:S(2)}) collective-permute-start(bf16[1,32,2048]{2,1,0:T(8,128)(2,1)S(1)} %get-tuple-element.23), channel_id=1, source_target_pairs={{0,1},{1,0},{2,3},{3,2},{4,5},{5,4},{6,7},{7,6},{8,9},{9,8},{10,11... | collective-permute-start | bytes 393224 | tf_op jit(solution)/shard_map/ppermute | solution.py:283
  9.9 13.1 %collective-permute-start.6 = (bf16[528,128]{1,0:T(8,128)(2,1)S(1)}, bf16[528,128]{1,0:T(8,128)(2,1)S(1)}, u32[]{:S(2)}, u32[]{:S(2)}) collective-permute-start(bf16[528,128]{1,0:T(8,128)(2,1)S(1)} %shard_map.64), channel_id=1, source_target_pairs={{0,4},{4,0},{8,12},{12,8},{1,5},{5,1},{9,13},{13,9},{2,6},{6,2},{1... | collective-permute-start | bytes 405512 | tf_op jit(solution)/shard_map/ppermute | solution.py:262
  12.9 12.5 %copy-start = (bf16[32,2048]{1,0:T(8,128)(2,1)S(1)}, bf16[32,2048]{1,0:T(8,128)(2,1)}, u32[]{:S(2)}) copy-start(bf16[32,2048]{1,0:T(8,128)(2,1)} %residual_ref.3) | copy-start | bytes 393220
  15.2 7.9 %collective-permute-start.2 = (bf16[1,32,2048]{2,1,0:T(8,128)(2,1)S(1)}, bf16[1,32,2048]{2,1,0:T(8,128)(2,1)S(1)}, u32[]{:S(2)}, u32[]{:S(2)}) collective-permute-start(bf16[1,32,2048]{2,1,0:T(8,128)(2,1)S(1)} %get-tuple-element.28), channel_id=1, source_target_pairs={{0,1},{1,0},{2,3},{3,2},{4,5},{5,4},{6,7},{7,6},{8,9},{9,8},{10,11... | collective-permute-start | bytes 393224 | tf_op jit(solution)/shard_map/ppermute | solution.py:283
  15.3 6.0 %collective-permute-start.7 = (bf16[256,128]{1,0:T(8,128)(2,1)S(1)}, bf16[256,128]{1,0:T(8,128)(2,1)S(1)}, u32[]{:S(2)}, u32[]{:S(2)}) collective-permute-start(bf16[256,128]{1,0:T(8,128)(2,1)S(1)} %get-tuple-element.35), channel_id=1, source_target_pairs={{0,4},{4,0},{8,12},{12,8},{1,5},{5,1},{9,13},{13,9},{2,6},{6,2},{1... | collective-permute-start | bytes 196616 | tf_op jit(solution)/shard_map/ppermute | solution.py:262
  15.5 7.5 %collective-permute-start.4 = (bf16[272,128]{1,0:T(8,128)(2,1)S(1)}, bf16[272,128]{1,0:T(8,128)(2,1)S(1)}, u32[]{:S(2)}, u32[]{:S(2)}) collective-permute-start(bf16[272,128]{1,0:T(8,128)(2,1)S(1)} %get-tuple-element.31), channel_id=1, source_target_pairs={{0,8},{4,12},{8,0},{12,4},{1,9},{5,13},{9,1},{13,5},{2,10},{6,14},... | collective-permute-start | bytes 208904 | tf_op jit(solution)/shard_map/ppermute | solution.py:262
  18.4 7.0 %collective-permute-start.5 = (bf16[272,128]{1,0:T(8,128)(2,1)S(1)}, bf16[272,128]{1,0:T(8,128)(2,1)S(1)}, u32[]{:S(2)}, u32[]{:S(2)}) collective-permute-start(bf16[272,128]{1,0:T(8,128)(2,1)S(1)} %get-tuple-element.32), channel_id=1, source_target_pairs={{0,12},{4,8},{8,4},{12,0},{1,13},{5,9},{9,5},{13,1},{2,14},{6,10},... | collective-permute-start | bytes 208904 | tf_op jit(solution)/shard_map/ppermute | solution.py:262
  21.4 8.3 %collective-permute-start.8 = (bf16[256,128]{1,0:T(8,128)(2,1)S(1)}, bf16[256,128]{1,0:T(8,128)(2,1)S(1)}, u32[]{:S(2)}, u32[]{:S(2)}) collective-permute-start(bf16[256,128]{1,0:T(8,128)(2,1)S(1)} %shard_map.65), channel_id=1, source_target_pairs={{0,8},{4,12},{8,0},{12,4},{1,9},{5,13},{9,1},{13,5},{2,10},{6,14},... | collective-permute-start | bytes 196616 | tf_op jit(solution)/shard_map/ppermute | solution.py:262
  25.5 7.8 %collective-permute-start.11 = (bf16[256,128]{1,0:T(8,128)(2,1)S(1)}, bf16[256,128]{1,0:T(8,128)(2,1)S(1)}, u32[]{:S(2)}, u32[]{:S(2)}) collective-permute-start(bf16[256,128]{1,0:T(8,128)(2,1)S(1)} %shard_map.66.refs_4_), channel_id=1, source_target_pairs={{0,8},{4,12},{8,0},{12,4},{1,9},{5,13},{9,1},{13,5},{2,10},{6,14},... | collective-permute-start | bytes 196616 | tf_op jit(solution)/shard_map/ppermute | solution.py:262
  29.7 10.0 %collective-permute-start.9 = (bf16[512,128]{1,0:T(8,128)(2,1)S(1)}, bf16[512,128]{1,0:T(8,128)(2,1)S(1)}, u32[]{:S(2)}, u32[]{:S(2)}) collective-permute-start(bf16[512,128]{1,0:T(8,128)(2,1)S(1)} %get-tuple-element.36.refs_0_), channel_id=1, source_target_pairs={{0,4},{4,0},{8,12},{12,8},{1,5},{5,1},{9,13},{13,9},{2,6},{6,2},{1... | collective-permute-start | bytes 393224 | tf_op jit(solution)/shard_map/ppermute | solution.py:262
  29.8 8.0 %collective-permute-start.12 = (bf16[256,128]{1,0:T(8,128)(2,1)S(1)}, bf16[256,128]{1,0:T(8,128)(2,1)S(1)}, u32[]{:S(2)}, u32[]{:S(2)}) collective-permute-start(bf16[256,128]{1,0:T(8,128)(2,1)S(1)} %get-tuple-element.37), channel_id=1, source_target_pairs={{0,12},{4,8},{8,4},{12,0},{1,13},{5,9},{9,5},{13,1},{2,14},{6,10},... | collective-permute-start | bytes 196616 | tf_op jit(solution)/shard_map/ppermute | solution.py:262
  32.0 7.8 %collective-permute-start.10 = (bf16[256,128]{1,0:T(8,128)(2,1)S(1)}, bf16[256,128]{1,0:T(8,128)(2,1)S(1)}, u32[]{:S(2)}, u32[]{:S(2)}) collective-permute-start(bf16[256,128]{1,0:T(8,128)(2,1)S(1)} %get-tuple-element.37), channel_id=1, source_target_pairs={{0,8},{4,12},{8,0},{12,4},{1,9},{5,13},{9,1},{13,5},{2,10},{6,14},... | collective-permute-start | bytes 196616 | tf_op jit(solution)/shard_map/ppermute | solution.py:262
  33.3 6.5 %collective-permute-start.13 = (bf16[256,128]{1,0:T(8,128)(2,1)S(1)}, bf16[256,128]{1,0:T(8,128)(2,1)S(1)}, u32[]{:S(2)}, u32[]{:S(2)}) collective-permute-start(bf16[256,128]{1,0:T(8,128)(2,1)S(1)} %collective-permute-done.11.refs_3_), channel_id=1, source_target_pairs={{0,4},{4,0},{8,12},{12,8},{1,5},{5,1},{9,13},{13,9},{2,6},{6,2},{1... | collective-permute-start | bytes 196616 | tf_op jit(solution)/shard_map/ppermute | solution.py:262
